TPU v7x, 32 devices: a whole 2x2x4 slice. The times are simulated.
32 devices in a mesh: io: 16 (over z, x, core), rep: 2 (over y).
Axes of the slice: x: 2, y: 2, z: 4, core: 2. Of those that a mesh axis runs over, the one named last changes fastest.
Arguments:
- snapshots: float32 [49152, 2048], P(('rep', 'io')), parts along dimension 0, may hold values from -6 to 6
Outputs:
- coefficients: float32 [32, 256, 2048], P('rep', None, 'io'), parts along dimension 0
- resid_var: float32 [512, 2048], P('rep', 'io'), parts along dimension 0
There are 2 independent parts, one for each index of `rep`. A program takes and returns all parts, laid end to end along the dimension named above; each array names one. Nothing has to cross between parts.
All inputs are finite; a program needn't handle non-finite values.
Results may differ from a plain program's by a relative error of at most 0.000071.
Values sent between devices are 32-bit elements; how exact they have to be, the bound alone decides.
No kernel may reach another device: no remote copies, remote signals or barrier semaphores. Data moves between devices by JAX's collectives and lax.ppermute only.
A program may use at most 128 MiB of HBM per device.

v0:
```python
import jax
import jax.numpy as jnp
from jax import lax
from jax.sharding import PartitionSpec as P

TIMES = 96
HARM = 16


def basis_matrix(times):
    steps = jnp.arange(times).astype(jnp.float32)
    columns = [jnp.ones_like(steps), (steps - (times - 1) / 2.0) / (times / 2.0)]
    for harmonic in range(1, 7):
        columns.append(jnp.cos(2.0 * jnp.pi * harmonic * steps / 12.0))
    for harmonic in range(1, 6):
        columns.append(jnp.sin(2.0 * jnp.pi * harmonic * steps / 12.0))
    columns.append(jnp.cos(2.0 * jnp.pi * steps / times))
    columns.append(jnp.sin(2.0 * jnp.pi * steps / times))
    columns.append(jnp.cos(4.0 * jnp.pi * steps / times))
    return jnp.stack(columns, axis=1)


def projector_of(basis):
    gram = jnp.dot(basis.T, basis, precision=lax.Precision.HIGHEST)
    factor = jnp.linalg.cholesky(gram)
    middle = lax.linalg.triangular_solve(factor, basis.T, left_side=True, lower=True)
    return lax.linalg.triangular_solve(factor, middle, left_side=True, lower=True, transpose_a=True)


def fit_block(block, basis, projector):
    width = block.shape[-1]
    lat_rows = block.shape[0] // TIMES
    series = block.reshape(TIMES, lat_rows * width)
    coeffs = jnp.dot(projector, series, precision=lax.Precision.HIGHEST)
    moments = jnp.dot(basis.T, series, precision=lax.Precision.HIGHEST)
    total = jnp.sum(series * series, axis=0)
    variance = (total - jnp.sum(coeffs * moments, axis=0)) / TIMES
    return (coeffs.reshape(HARM, lat_rows, width), variance.reshape(1, lat_rows, width))


def local(snapshots):
    groups = lax.axis_size("io")
    local_rows = snapshots.shape[0]
    lon_dev = snapshots.shape[1] // groups
    split_view = snapshots.reshape(local_rows, groups, lon_dev)
    basis = basis_matrix(TIMES)
    projector = projector_of(basis)
    moved = lax.all_to_all(split_view, "io", split_axis=1, concat_axis=0, tiled=True)
    coeffs, variance = fit_block(moved[:, 0, :], basis, projector)
    return (coeffs, variance[0])


def solution(mesh):
    placed = (P(("rep", "io"), None),)
    return jax.shard_map(
        local,
        mesh=mesh,
        in_specs=placed,
        out_specs=(P("rep", None, "io"), P("rep", "io")),
        check_vma=False,
    )
```

profile of v0, /device:TPU:11, one launch (start us, length us, event | category | flops | bytes accessed | tf_op | source)
XLA Modules:
  0.0 326.1 jit_solution(2681641074615959106)
XLA Ops:
  0.6 10.3 %copy_bitcast_fusion = f32[1536,16,128]{2,0,1:T(8,128)} fusion(f32[1536,2048]{1,0:T(8,128)} %param.1), kind=kLoop, calls=%fused_computation.1 | loop fusion | bytes 25165824 | tf_op jit(solution)/shard_map/reshape | solution.py:45
  10.9 6.5 %all-to-all-start = ((f32[1536,16,128]{2,0,1:T(8,128)}), f32[1536,16,128]{2,0,1:T(8,128)}, u32[]{:S(2)}, u32[]{:S(2)}) async-start(f32[1536,16,128]{2,0,1:T(8,128)} %copy_bitcast_fusion), calls=%async_computation | async-start | bytes 25165824 | tf_op jit(solution)/shard_map/all_to_all | solution.py:48
  17.5 0.1 fusion.16
  17.6 0.1 fusion.14
  17.6 0.1 fusion.12
  17.7 0.1 fusion.10
  17.7 0.1 fusion.8
  17.9 0.1 stack.2
  18.0 0.1 fusion.19
  18.1 0.1 copy.6
  18.2 1.5 cholesky.16
  19.7 0.6 compare_reduce_fusion
  20.3 0.6 fusion.1
  21.0 1.2 custom-call.8
  22.2 0.2 fusion.4
  22.4 0.1 fusion.2
  22.5 267.2 %all-to-all-done = f32[1536,16,128]{2,0,1:T(8,128)} async-done(((f32[1536,16,128]{2,0,1:T(8,128)}), f32[1536,16,128]{2,0,1:T(8,128)}, u32[]{:S(2)}, u32[]{:S(2)}) %all-to-all-start) | async-done | bytes 12582944 | tf_op jit(solution)/shard_map/all_to_all | solution.py:48
  289.7 13.8 %reshape_squeeze.3 = f32[96,32768]{1,0:T(8,128)} reshape(f32[16,1536,1,128]{3,1,0,2:T(8,128)} %bitcast.4) | data formatting | bytes 25165824 | tf_op jit(solution)/shard_map/reshape;squeeze | solution.py:33
  303.5 5.8 %multiply_reduce_fusion = f32[32768]{0:T(1024)S(1)} fusion(f32[96,32768]{1,0:T(8,128)} %reshape_squeeze.3), kind=kLoop, calls=%fused_computation.2 | loop fusion | flops 6258688 | bytes 12713984 | tf_op jit(solution)/shard_map/reduce_sum | solution.py:36
  309.3 2.4 copy-done
  311.7 6.0 %fusion.20 = f32[16,32768]{1,0:T(8,128)S(1)} fusion(f32[16,96]{1,0:T(8,128)S(1)} %fusion.2, f32[96,32768]{1,0:T(8,128)S(1)} %copy-done), kind=kOutput, calls=%fused_computation.39 | convolution fusion | flops 603979776 | bytes 14686208 | tf_op jit(solution)/shard_map/dot_general | solution.py:34
  317.6 6.1 %fusion = f32[32768]{0:T(1024)S(1)} fusion(f32[16,32768]{1,0:T(8,128)S(1)} %fusion.20, f32[96,16]{0,1:T(8,128)S(1)} %stack.2, f32[96,32768]{1,0:T(8,128)S(1)} %copy-done), kind=kOutput, calls=%fused_computation.3 | convolution fusion | flops 604995584 | bytes 14817280 | tf_op jit(solution)/shard_map/dot_general | solution.py:35
  323.7 1.7 copy.9
  325.4 0.7 multiply_bitcast_fusion
  (7 shorter events, 0.2 us)
Async XLA Ops:
  10.9 278.8 %all-to-all-start = ((f32[1536,16,128]{2,0,1:T(8,128)}), f32[1536,16,128]{2,0,1:T(8,128)}, u32[]{:S(2)}, u32[]{:S(2)}) async-start(f32[1536,16,128]{2,0,1:T(8,128)} %copy_bitcast_fusion), calls=%async_computation | async-start | bytes 25165824 | tf_op jit(solution)/shard_map/all_to_all | solution.py:48
  303.5 8.2 %copy-start = (f32[96,32768]{1,0:T(8,128)S(1)}, f32[96,32768]{1,0:T(8,128)}, u32[]{:S(2)}) copy-start(f32[96,32768]{1,0:T(8,128)} %reshape_squeeze.3) | copy-start | bytes 37748740
where the time goes:
time: 327 us; the launch traced here: 326 us
  waiting for transfers between devices  267 us (82%)
  local copies, waits for them, and re-layouts  28.3 us (9%)
  matrix products  12.5 us (4%)
  other arithmetic  10.9 us (3%)
  starting transfers between devices  6.52 us (2%)
    all_to_all x1, waiting for transfers between devices, local(): lax.all_to_all(split_view, 'io', split_axis=1, concat_axis=0, tiled=True)  267 us
    another operation x1, local copies, waits for them, and re-layouts, fit_block(): series = block.reshape(TIMES, lat_rows * width)  13.8 us
    reshape x1, local copies, waits for them, and re-layouts, local(): split_view = snapshots.reshape(local_rows, groups, lon_dev)  10.3 us
  transfers between devices with their start and end apart: 1, of which 1 were waited for; matrix products, arithmetic and copies ran while one was open for 2% of the time, Pallas kernels for 0%

commit v1 on v0

v1 whole, which is shorter than its diff:
```python
import functools

import jax
import jax.numpy as jnp
import numpy as np
from jax import lax
from jax.experimental import pallas as pl
from jax.experimental.pallas import tpu as pltpu
from jax.sharding import PartitionSpec as P


TIMES = 96
HARM = 16
PERIOD = 12
SLOW = HARM - PERIOD
STATS = HARM + 1
PLANES = 4

PARTS = (3, 4, 6, 7, 7, 5)
MODES = "ssssdd"
ORDER = " ".join((
    "p0 p1 t0 p2",
    "p3 t1 m0 p4",
    "p5 t2 m1 r0",
    "t3 m2 r1 f0",
    "t4 m3 r2 f1",
    "t5 r3 f2 f3",
    "f4 f5",
)).split()
FINAL_ROWS = 8
VMEM_LIMIT = 8 << 20


def basis_matrix(times):
    steps = np.arange(times, dtype=np.float64)
    columns = [np.ones_like(steps), (steps - (times - 1) / 2.0) / (times / 2.0)]
    for harmonic in range(1, 7):
        columns.append(np.cos(2.0 * np.pi * harmonic * steps / 12.0))
    for harmonic in range(1, 6):
        columns.append(np.sin(2.0 * np.pi * harmonic * steps / 12.0))
    columns.append(np.cos(2.0 * np.pi * steps / times))
    columns.append(np.sin(2.0 * np.pi * steps / times))
    columns.append(np.cos(4.0 * np.pi * steps / times))
    return np.stack(columns, axis=1)


PERIODIC = [0] + list(range(2, 13))
SLOWS = [1, 13, 14, 15]


def fit_matrices():
    basis = basis_matrix(TIMES)
    to_moments = np.zeros((HARM, HARM))
    for column in PERIODIC:
        to_moments[column, :PERIOD] = basis[:PERIOD, column]
    for at, column in enumerate(SLOWS):
        to_moments[column, PERIOD + at] = 1.0
    to_coeffs = np.linalg.solve(basis.T @ basis, to_moments)
    return to_moments, to_coeffs


def fit_block(block, basis, projector):
    width = block.shape[-1]
    lat_rows = block.shape[0] // TIMES
    series = block.reshape(TIMES, lat_rows * width)
    coeffs = jnp.dot(projector, series, precision=lax.Precision.HIGHEST)
    moments = jnp.dot(basis.T, series, precision=lax.Precision.HIGHEST)
    total = jnp.sum(series * series, axis=0)
    variance = (total - jnp.sum(coeffs * moments, axis=0)) / TIMES
    return coeffs.reshape(HARM, lat_rows, width), variance.reshape(lat_rows, width)


def general(snapshots):
    groups = lax.axis_size("io")
    local_rows = snapshots.shape[0]
    lon_dev = snapshots.shape[1] // groups
    split_view = snapshots.reshape(local_rows, groups, lon_dev)
    basis = basis_matrix(TIMES)
    projector = np.linalg.solve(basis.T @ basis, basis.T)
    moved = lax.all_to_all(split_view, "io", split_axis=1, concat_axis=0, tiled=True)
    return fit_block(moved[:, 0, :], jnp.float32(basis), jnp.float32(projector))


def zone_of(mode, step, where_ref):
    if mode == "d":
        return where_ref[3] ^ step
    return jnp.where(where_ref[2] > 0, PLANES - 1 - step, step)


def pack_kernel(first, mode, where_ref, x_ref, *rest):
    plane = 4
    outs, sem = rest[-plane - 2 : -2], rest[-1]
    rows, width = outs[0].shape[2:]
    copies = []
    for shift in (2, 3, 1, 0):
        for step in range(PLANES):
            column = (zone_of(mode, step, where_ref) * plane + (where_ref[0] ^ shift)) * width
            source = x_ref.at[:, pl.ds(first, rows), pl.ds(pl.multiple_of(column, width), width)]
            copies.append(pltpu.make_async_copy(source, outs[shift].at[step], sem))
            copies[-1].start()
    for copy in copies:
        copy.wait()


def totals_kernel(mode, where_ref, weight_ref, own_ref, r1_ref, r2_ref, r3_ref, *rest):
    outs = rest[-(PLANES if mode == "d" else 2) - 1 : -1]
    held, rows = own_ref.shape[1:3]
    size = 16 if rows % 16 == 0 else 8
    first = (where_ref[0] % 2) * held
    second = held - first
    sources = (own_ref, r1_ref, r2_ref, r3_ref)
    for step in range(PLANES):
        out_ref = outs[step] if mode == "d" or step == 0 else outs[1].at[step - 1]

        @pl.loop(0, rows // size)
        def _(block):
            at_rows = pl.ds(pl.multiple_of(block * size, size), size)
            slow = [None] * SLOW
            square = None
            for k in range(held):
                values = [ref[step, k, at_rows] for ref in sources]
                out_ref[first + k, at_rows] = values[0] + values[2]
                out_ref[second + k, at_rows] = values[1] + values[3]
                for at, value in enumerate(values):
                    for j in range(SLOW):
                        term = value * weight_ref[j, at * held + k]
                        slow[j] = term if slow[j] is None else slow[j] + term
                    term = value * value
                    square = term if square is None else square + term
            for j in range(SLOW):
                out_ref[PERIOD + j, at_rows] = slow[j]
            out_ref[HARM, at_rows] = square


def merge_kernel(away_ref, in_ref, *rest):
    rest[-2][...] = away_ref[1:3] + in_ref[1:3]


def relay_kernel(home_ref, b_ref, *rest):
    rest[-2][...] = home_ref[...] + b_ref[1]


def final_kernel(first, mode, to_moments, to_coeffs, where_ref, *refs):
    coeff_out, var_out, _, coeff_ref, var_ref, sem = refs[-6:]
    rows = var_ref.shape[0]

    def solve(load):
        @pl.loop(0, rows // FINAL_ROWS)
        def _(block):
            at_rows = pl.ds(pl.multiple_of(block * FINAL_ROWS, FINAL_ROWS), FINAL_ROWS)
            stats = [load(row, at_rows) for row in range(STATS)]

            def mix(weights):
                total = None
                for weight, stat in zip(weights, stats):
                    if abs(weight) > 1e-12:
                        term = stat if weight == 1.0 else stat * np.float32(weight)
                        total = term if total is None else total + term
                return total

            explained = None
            for column in range(HARM):
                coeff = mix(to_coeffs[column])
                coeff_ref[column, at_rows] = coeff
                term = coeff * mix(to_moments[column])
                explained = term if explained is None else explained + term
            var_ref[at_rows] = (stats[HARM] - explained) * np.float32(1.0 / TIMES)

    if mode == "d":
        parts = refs[:PLANES]
        solve(lambda row, at: (parts[0][row, at] + parts[1][row, at]) + (parts[2][row, at] + parts[3][row, at]))
    else:
        home_ref, away_ref, a_ref, b_ref, c_ref = refs[:5]

        @pl.when(where_ref[1] > 0)
        def _():
            solve(lambda row, at: away_ref[0, row, at] + a_ref[0, row, at] + b_ref[0, row, at])

        @pl.when(where_ref[1] == 0)
        def _():
            solve(lambda row, at: home_ref[row, at] + c_ref[row, at])

    copies = [
        pltpu.make_async_copy(coeff_ref, coeff_out.at[:, pl.ds(first, rows)], sem.at[0]),
        pltpu.make_async_copy(var_ref, var_out.at[pl.ds(first, rows)], sem.at[1]),
    ]
    for copy in copies:
        copy.start()
    for copy in copies:
        copy.wait()


def plane_plan(snapshots):
    groups = lax.axis_size("io")
    plane = groups // PLANES
    held = TIMES // groups
    lat = snapshots.shape[0] // held
    lon = snapshots.shape[1]
    width = lon // groups
    view = snapshots.reshape(held, lat, lon)

    me = lax.axis_index("io")
    place, level = me % plane, me // plane
    flip = (level >= PLANES // 2).astype(jnp.int32)
    inner = ((level > 0) & (level < PLANES - 1)).astype(jnp.int32)
    where = jnp.stack([place, inner, flip, level]).astype(jnp.int32)

    slow = basis_matrix(TIMES)[:, SLOWS].T
    table = np.zeros((groups, SLOW, plane * held), np.float32)
    for device in range(groups):
        for shift in range(plane):
            start = ((device // plane) * plane + ((device % plane) ^ shift)) * held
            table[device, :, shift * held : (shift + 1) * held] = slow[:, start : start + held]
    weights = lax.dynamic_index_in_dim(jnp.asarray(table), me, 0, keepdims=False)

    smem = pl.BlockSpec(memory_space=pltpu.SMEM)
    vmem = pl.BlockSpec(memory_space=pltpu.VMEM)
    hbm = pl.BlockSpec(memory_space=pltpu.HBM)
    space = {id(vmem): pltpu.VMEM, id(hbm): pltpu.HBM}
    token = []

    def near(*dims):
        return pltpu.VMEM(dims, jnp.float32)

    def call(kernel, flops, moved, ins, args, outs, out_specs, **more):
        ins, args = ins + [hbm] * len(token), list(args) + token
        args = [
            pltpu.with_memory_space_constraint(arg, space[id(spec)]) if id(spec) in space else arg
            for spec, arg in zip(ins, args)
        ]
        *results, last = pl.pallas_call(
            kernel,
            in_specs=ins,
            out_specs=out_specs + [hbm],
            out_shape=outs + [pltpu.HBM((8, 128), jnp.float32)],
            cost_estimate=pl.CostEstimate(flops=flops, bytes_accessed=moved, transcendentals=0),
            compiler_params=pltpu.CompilerParams(vmem_limit_bytes=VMEM_LIMIT),
            **more,
        )(*args)
        token[:] = [last]
        return results

    def move(value, pairs):
        return lax.ppermute(value, "io", pairs)

    sizes = [part * lat // sum(PARTS) for part in PARTS]
    firsts = [sum(sizes[:chunk]) for chunk in range(len(sizes))]
    swaps = [[(i, i ^ shift) for i in range(groups)] for shift in range(plane)]
    hops = [[(i, i ^ (step * plane)) for i in range(groups)] for step in range(PLANES)]
    to_inner = [(i, i + plane) for i in range(plane)] + [(i, i - plane) for i in range(groups - plane, groups)]
    to_outer = [(b, a) for a, b in to_inner]
    middle = [(i, i + plane) for i in range(plane, 2 * plane)]
    middle = middle + [(b, a) for a, b in middle]
    to_moments, to_coeffs = fit_matrices()

    packed, kept, got, outs = {}, {}, {}, []
    for item in ORDER:
        kind, chunk = item[0], int(item[1:])
        first, rows, mode = firsts[chunk], sizes[chunk], MODES[chunk]
        piece = rows * width
        if kind == "p":
            parts = call(
                functools.partial(pack_kernel, first, mode), piece * held, piece * PLANES * held * plane * 8,
                [smem, hbm], [where, view], [near(PLANES, held, rows, width)] * plane, [vmem] * plane,
                scratch_shapes=[pltpu.SemaphoreType.DMA],
            )
            packed[chunk] = [None] * plane
            packed[chunk][0] = parts[0]
            for shift in (2, 3, 1):
                packed[chunk][shift] = move(parts[shift], swaps[shift])
        elif kind == "t":
            one = near(STATS, rows, width)
            kept[chunk] = call(
                functools.partial(totals_kernel, mode), piece * PLANES * held * plane * 10, piece * 164 * 4,
                [smem, smem] + [vmem] * plane, [where, weights, *packed[chunk]],
                [one] * PLANES if mode == "d" else [one, near(PLANES - 1, STATS, rows, width)],
                [vmem] * (PLANES if mode == "d" else 2),
            )
            if mode == "d":
                for step in (3, 2, 1):
                    kept[chunk][step] = move(kept[chunk][step], hops[step])
            else:
                got[chunk] = [move(kept[chunk][1], to_inner)]
        elif kind == "m":
            (both,) = call(
                merge_kernel, piece * 34, piece * 34 * 12,
                [vmem, vmem], [kept[chunk][1], got[chunk][0]], [near(2, STATS, rows, width)], [vmem],
            )
            got[chunk].append(move(both, middle))
        elif kind == "r":
            (one,) = call(
                relay_kernel, piece * 17, piece * 17 * 12,
                [vmem, vmem], [kept[chunk][0], got[chunk][1]], [near(STATS, rows, width)], [vmem],
            )
            got[chunk].append(move(one, to_outer))
        else:
            args = [*kept[chunk], *got.get(chunk, [])]
            outs = call(
                functools.partial(final_kernel, first, mode, to_moments, to_coeffs), piece * 832, piece * 272,
                [smem] + [vmem] * len(args) + [hbm] * len(outs), [where, *args, *outs],
                [pltpu.HBM((HARM, lat, width), jnp.float32), pltpu.HBM((lat, width), jnp.float32)], [hbm, hbm],
                input_output_aliases={len(args) + 1: 0, len(args) + 2: 1} if outs else {},
                scratch_shapes=[
                    pltpu.VMEM((HARM, rows, width), jnp.float32),
                    pltpu.VMEM((rows, width), jnp.float32),
                    pltpu.SemaphoreType.DMA((2,)),
                ],
            )
    return tuple(outs)


def fits(groups):
    return groups == 4 * PLANES and TIMES % groups == 0 and TIMES // PLANES == 2 * PERIOD


def local(snapshots):
    groups = lax.axis_size("io")
    lat = snapshots.shape[0] * groups // TIMES
    if fits(groups) and lat % (8 * sum(PARTS)) == 0 and snapshots.shape[1] == 128 * groups:
        return plane_plan(snapshots)
    return general(snapshots)


def solution(mesh):
    return jax.shard_map(
        local,
        mesh=mesh,
        in_specs=(P(("rep", "io"), None),),
        out_specs=(P("rep", None, "io"), P("rep", "io")),
        check_vma=False,
    )
```

time: 327 us -> 256 us (0.78)
  waiting for transfers between devices: 267 us -> 167 us
  starting transfers between devices: 6.52 us -> 50.9 us
  Pallas kernels: 0 us -> 36.4 us
  local copies, waits for them, and re-layouts: 28.3 us -> 0.68 us
  matrix products: 12.5 us -> 0 us
  other arithmetic: 10.9 us -> 0.08 us
    all_to_all x1 -> x0, waiting for transfers between devices: 267 us -> none  [local(): lax.all_to_all(split_view, 'io', split_axis=1, concat_axis=0, tiled=True)]
    ppermute x0 -> x36, waiting for transfers between devices: none -> 167 us  [move(): return lax.ppermute(value, 'io', pairs)]
    ppermute x0 -> x36, starting transfers between devices: none -> 50.9 us  [move(): return lax.ppermute(value, 'io', pairs)]
    pallas_call x0 -> x26, Pallas kernels: none -> 36.4 us  [call(): pl.pallas_call(kernel, in_specs=ins, out_specs=out_specs + [hbm], out_sha...]
    another operation x3 -> x0, local copies, waits for them, and re-layouts: 13.9 us -> none  [the longest x1 13.8 us: fit_block(): series = block.reshape(TIMES, lat_rows * width)]
    dot_general x3 -> x0, matrix products: 12.2 us -> none  [the longest x1 6.06 us: fit_block(): moments = jnp.dot(basis.T, series, precision=lax.Precision.HIGHEST)]
    reshape x1 -> x0, local copies, waits for them, and re-layouts: 10.3 us -> none  [local(): split_view = snapshots.reshape(local_rows, groups, lon_dev)]
    all_to_all x1 -> x0, starting transfers between devices: 6.52 us -> none  [local(): lax.all_to_all(split_view, 'io', split_axis=1, concat_axis=0, tiled=True)]
  transfers between devices with their start and end apart: 1 -> 36, of which waited for: 1 -> 17; matrix products, arithmetic and copies ran while one was open for 2% -> 0% of each run, Pallas kernels for 0% -> 12%
where the time goes in v1:
time: 256 us
  waiting for transfers between devices  167 us (65%)
  starting transfers between devices  50.9 us (20%)
  Pallas kernels  36.4 us (14%)
    ppermute x36, waiting for transfers between devices, move(): return lax.ppermute(value, 'io', pairs)  167 us
    ppermute x36, starting transfers between devices, move(): return lax.ppermute(value, 'io', pairs)  50.9 us
    pallas_call x26, Pallas kernels, call(): pl.pallas_call(kernel, in_specs=ins, out_specs=out_specs + [hbm], out_sha...  36.4 us
  transfers between devices with their start and end apart: 36, of which 17 were waited for; matrix products, arithmetic and copies ran while one was open for 0% of the time, Pallas kernels for 12%

profile of v1, /device:TPU:11, one launch (start us, length us, event | category | flops | bytes accessed | tf_op | source)
XLA Modules:
  0.0 255.8 jit_solution(1123370771195631234)
XLA Ops:
  0.7 2.8 %shard_map.41 = (f32[4,6,24,128]{3,2,1,0:T(8,128)S(1)}, f32[4,6,24,128]{3,2,1,0:T(8,128)S(1)}, f32[4,6,24,128]{3,2,1,0:T(8,128)}, f32[4,6,24,128]{3,2,1,0:T(8,128)}, f32[8,128]{1,0:T(8,128)}) custom-call(s32[4]{0:T(128)S(1)} %pad_add_fusion.where_ref, f32[6,256,2048]{2,1,0:T(8,128)} %bitcast.7), custom_call_target="tpu_custom_call" | custom-call | flops 18432 | bytes 2359296 | tf_op jit(solution)/shard_map/pallas_call | solution.py:231
  4.2 2.8 %shard_map.42 = (f32[4,6,32,128]{3,2,1,0:T(8,128)S(1)}, f32[4,6,32,128]{3,2,1,0:T(8,128)}, f32[4,6,32,128]{3,2,1,0:T(8,128)S(1)}, f32[4,6,32,128]{3,2,1,0:T(8,128)S(1)}, f32[8,128]{1,0:T(8,128)}) custom-call(s32[4]{0:T(128)S(1)} %pad_add_fusion.where_ref, f32[6,256,2048]{2,1,0:T(8,128)} %bitcast.8, f32[8,128]{1,0:T(8,128)} %get-tuple-element.91.rest_0_), custom_call_target="tpu_custom_call" | custom-call | flops 24576 | bytes 3145728 | tf_op jit(solution)/shard_map/pallas_call | solution.py:231
  11.4 20.8 %collective-permute-done.1.r2_ref = f32[4,6,24,128]{3,2,1,0:T(8,128)S(1)} collective-permute-done((f32[4,6,24,128]{3,2,1,0:T(8,128)}, f32[4,6,24,128]{3,2,1,0:T(8,128)S(1)}, u32[]{:S(2)}, u32[]{:S(2)}) %collective-permute-start.1) | collective-permute-done | bytes 294944 | tf_op jit(solution)/shard_map/ppermute | solution.py:244
  32.2 6.9 %collective-permute-done.2.r3_ref = f32[4,6,24,128]{3,2,1,0:T(8,128)S(1)} collective-permute-done((f32[4,6,24,128]{3,2,1,0:T(8,128)}, f32[4,6,24,128]{3,2,1,0:T(8,128)S(1)}, u32[]{:S(2)}, u32[]{:S(2)}) %collective-permute-start.2) | collective-permute-done | bytes 294944 | tf_op jit(solution)/shard_map/ppermute | solution.py:244
  44.4 2.5 shard_map.45
  51.3 7.2 %collective-permute-done.12.r2_ref = f32[4,6,48,128]{3,2,1,0:T(8,128)S(1)} collective-permute-done((f32[4,6,48,128]{3,2,1,0:T(8,128)S(1)}, f32[4,6,48,128]{3,2,1,0:T(8,128)S(1)}, u32[]{:S(2)}, u32[]{:S(2)}) %collective-permute-start.12) | collective-permute-done | bytes 589856 | tf_op jit(solution)/shard_map/ppermute | solution.py:244
  58.8 3.5 %collective-permute-start.18 = (f32[4,6,56,128]{3,2,1,0:T(8,128)S(1)}, f32[4,6,56,128]{3,2,1,0:T(8,128)S(1)}, u32[]{:S(2)}, u32[]{:S(2)}) collective-permute-start(f32[4,6,56,128]{3,2,1,0:T(8,128)S(1)} %get-tuple-element.121), channel_id=1, source_target_pairs={{0,6},{2,4},{4,2},{6,0},{8,14},{10,12},{12,10},{14,8},{16,22},{18,... | collective-permute-start | bytes 2064392 | tf_op jit(solution)/shard_map/ppermute | solution.py:244
  67.1 5.9 %collective-permute-done.13.r3_ref = f32[4,6,48,128]{3,2,1,0:T(8,128)S(1)} collective-permute-done((f32[4,6,48,128]{3,2,1,0:T(8,128)S(1)}, f32[4,6,48,128]{3,2,1,0:T(8,128)S(1)}, u32[]{:S(2)}, u32[]{:S(2)}) %collective-permute-start.13) | collective-permute-done | bytes 589856 | tf_op jit(solution)/shard_map/ppermute | solution.py:244
  76.0 3.2 %collective-permute-start.19 = (f32[2,17,24,128]{3,2,1,0:T(8,128)S(1)}, f32[2,17,24,128]{3,2,1,0:T(8,128)S(1)}, u32[]{:S(2)}, u32[]{:S(2)}) collective-permute-start(f32[2,17,24,128]{3,2,1,0:T(8,128)S(1)} %get-tuple-element.123), channel_id=1, source_target_pairs={{8,16},{10,18},{12,20},{14,22},{16,8},{18,10},{20,12},{22,14},{9,1... | collective-permute-start | bytes 1253384 | tf_op jit(solution)/shard_map/ppermute | solution.py:244
  79.3 9.2 %collective-permute-done.19.b_ref.refs_3_ = f32[2,17,24,128]{3,2,1,0:T(8,128)S(1)} collective-permute-done((f32[2,17,24,128]{3,2,1,0:T(8,128)S(1)}, f32[2,17,24,128]{3,2,1,0:T(8,128)S(1)}, u32[]{:S(2)}, u32[]{:S(2)}) %collective-permute-start.19) | collective-permute-done | bytes 417824 | tf_op jit(solution)/shard_map/ppermute | solution.py:244
  88.5 13.1 %collective-permute-done.18.r3_ref = f32[4,6,56,128]{3,2,1,0:T(8,128)S(1)} collective-permute-done((f32[4,6,56,128]{3,2,1,0:T(8,128)S(1)}, f32[4,6,56,128]{3,2,1,0:T(8,128)S(1)}, u32[]{:S(2)}, u32[]{:S(2)}) %collective-permute-start.18) | collective-permute-done | bytes 688160 | tf_op jit(solution)/shard_map/ppermute | solution.py:244
  105.0 4.1 %collective-permute-start.21 = (f32[17,24,128]{2,1,0:T(8,128)S(1)}, f32[17,24,128]{2,1,0:T(8,128)S(1)}, u32[]{:S(2)}, u32[]{:S(2)}) collective-permute-start(f32[17,24,128]{2,1,0:T(8,128)S(1)} %get-tuple-element.129), channel_id=1, source_target_pairs={{8,0},{10,2},{12,4},{14,6},{16,24},{18,26},{20,28},{22,30},{9,1},{... | collective-permute-start | bytes 626696 | tf_op jit(solution)/shard_map/ppermute | solution.py:244
  109.1 3.2 %collective-permute-start.14 = (f32[2,17,32,128]{3,2,1,0:T(8,128)S(1)}, f32[2,17,32,128]{3,2,1,0:T(8,128)S(1)}, u32[]{:S(2)}, u32[]{:S(2)}) collective-permute-start(f32[2,17,32,128]{3,2,1,0:T(8,128)S(1)} %get-tuple-element.116), channel_id=1, source_target_pairs={{8,16},{10,18},{12,20},{14,22},{16,8},{18,10},{20,12},{22,14},{9,1... | collective-permute-start | bytes 1671176 | tf_op jit(solution)/shard_map/ppermute | solution.py:244
  116.1 8.9 %collective-permute-done.14.b_ref.refs_3_ = f32[2,17,32,128]{3,2,1,0:T(8,128)S(1)} collective-permute-done((f32[2,17,32,128]{3,2,1,0:T(8,128)S(1)}, f32[2,17,32,128]{3,2,1,0:T(8,128)S(1)}, u32[]{:S(2)}, u32[]{:S(2)}) %collective-permute-start.14) | collective-permute-done | bytes 557088 | tf_op jit(solution)/shard_map/ppermute | solution.py:244
  125.1 3.2 %collective-permute-start.22 = (f32[2,17,48,128]{3,2,1,0:T(8,128)S(1)}, f32[2,17,48,128]{3,2,1,0:T(8,128)S(1)}, u32[]{:S(2)}, u32[]{:S(2)}) collective-permute-start(f32[2,17,48,128]{3,2,1,0:T(8,128)S(1)} %get-tuple-element.134), channel_id=1, source_target_pairs={{8,16},{10,18},{12,20},{14,22},{16,8},{18,10},{20,12},{22,14},{9,1... | collective-permute-start | bytes 2506760 | tf_op jit(solution)/shard_map/ppermute | solution.py:244
  130.1 15.8 %collective-permute-done.26.r3_ref = f32[4,6,56,128]{3,2,1,0:T(8,128)S(1)} collective-permute-done((f32[4,6,56,128]{3,2,1,0:T(8,128)S(1)}, f32[4,6,56,128]{3,2,1,0:T(8,128)S(1)}, u32[]{:S(2)}, u32[]{:S(2)}) %collective-permute-start.26) | collective-permute-done | bytes 688160 | tf_op jit(solution)/shard_map/ppermute | solution.py:244
  148.2 3.2 %collective-permute-start.33 = (f32[2,17,56,128]{3,2,1,0:T(8,128)S(1)}, f32[2,17,56,128]{3,2,1,0:T(8,128)S(1)}, u32[]{:S(2)}, u32[]{:S(2)}) collective-permute-start(f32[2,17,56,128]{3,2,1,0:T(8,128)S(1)} %get-tuple-element.154), channel_id=1, source_target_pairs={{8,16},{10,18},{12,20},{14,22},{16,8},{18,10},{20,12},{22,14},{9,1... | collective-permute-start | bytes 2924552 | tf_op jit(solution)/shard_map/ppermute | solution.py:244
  155.0 6.1 %collective-permute-done.20.refs_4_ = f32[17,32,128]{2,1,0:T(8,128)S(1)} collective-permute-done((f32[17,32,128]{2,1,0:T(8,128)S(1)}, f32[17,32,128]{2,1,0:T(8,128)S(1)}, u32[]{:S(2)}, u32[]{:S(2)}) %collective-permute-start.20) | collective-permute-done | bytes 278560 | tf_op jit(solution)/shard_map/ppermute | solution.py:244
  165.0 10.0 %collective-permute-done.9.r3_ref = f32[4,6,40,128]{3,2,1,0:T(8,128)S(1)} collective-permute-done((f32[4,6,40,128]{3,2,1,0:T(8,128)S(1)}, f32[4,6,40,128]{3,2,1,0:T(8,128)S(1)}, u32[]{:S(2)}, u32[]{:S(2)}) %collective-permute-start.9) | collective-permute-done | bytes 491552 | tf_op jit(solution)/shard_map/ppermute | solution.py:244
  183.3 35.8 %collective-permute-done.35.refs_4_ = f32[17,48,128]{2,1,0:T(8,128)S(1)} collective-permute-done((f32[17,48,128]{2,1,0:T(8,128)S(1)}, f32[17,48,128]{2,1,0:T(8,128)S(1)}, u32[]{:S(2)}, u32[]{:S(2)}) %collective-permute-start.35) | collective-permute-done | bytes 417824 | tf_op jit(solution)/shard_map/ppermute | solution.py:244
  219.2 3.2 %collective-permute-start.28 = (f32[17,40,128]{2,1,0:T(8,128)S(1)}, f32[17,40,128]{2,1,0:T(8,128)S(1)}, u32[]{:S(2)}, u32[]{:S(2)}) collective-permute-start(f32[17,40,128]{2,1,0:T(8,128)S(1)} %get-tuple-element.147), channel_id=1, source_target_pairs={{0,16},{2,18},{4,20},{6,22},{8,24},{10,26},{12,28},{14,30},{16,0},... | collective-permute-start | bytes 1044488 | tf_op jit(solution)/shard_map/ppermute | solution.py:244
  226.5 12.6 %collective-permute-done.32.refs_3_ = f32[17,56,128]{2,1,0:T(8,128)S(1)} collective-permute-done((f32[17,56,128]{2,1,0:T(8,128)S(1)}, f32[17,56,128]{2,1,0:T(8,128)S(1)}, u32[]{:S(2)}, u32[]{:S(2)}) %collective-permute-start.32) | collective-permute-done | bytes 487456 | tf_op jit(solution)/shard_map/ppermute | solution.py:244
  241.1 3.8 %collective-permute-done.28.refs_2_ = f32[17,40,128]{2,1,0:T(8,128)S(1)} collective-permute-done((f32[17,40,128]{2,1,0:T(8,128)S(1)}, f32[17,40,128]{2,1,0:T(8,128)S(1)}, u32[]{:S(2)}, u32[]{:S(2)}) %collective-permute-start.28) | collective-permute-done | bytes 348192 | tf_op jit(solution)/shard_map/ppermute | solution.py:244
  244.9 9.1 %collective-permute-done.29.refs_3_ = f32[17,40,128]{2,1,0:T(8,128)S(1)} collective-permute-done((f32[17,40,128]{2,1,0:T(8,128)S(1)}, f32[17,40,128]{2,1,0:T(8,128)S(1)}, u32[]{:S(2)}, u32[]{:S(2)}) %collective-permute-start.29) | collective-permute-done | bytes 348192 | tf_op jit(solution)/shard_map/ppermute | solution.py:244
  (76 shorter events, 57.8 us)
Async XLA Ops:
  7.1 37.0 %collective-permute-start.4 = (f32[4,6,32,128]{3,2,1,0:T(8,128)}, f32[4,6,32,128]{3,2,1,0:T(8,128)S(1)}, u32[]{:S(2)}, u32[]{:S(2)}) collective-permute-start(f32[4,6,32,128]{3,2,1,0:T(8,128)} %get-tuple-element.95), channel_id=1, source_target_pairs={{0,2},{2,0},{4,6},{6,4},{8,10},{10,8},{12,14},{14,12},{16,18},{18,... | collective-permute-start | bytes 1179656 | tf_op jit(solution)/shard_map/ppermute | solution.py:244
  7.1 39.7 %collective-permute-start.5 = (f32[4,6,32,128]{3,2,1,0:T(8,128)S(1)}, f32[4,6,32,128]{3,2,1,0:T(8,128)S(1)}, u32[]{:S(2)}, u32[]{:S(2)}) collective-permute-start(f32[4,6,32,128]{3,2,1,0:T(8,128)S(1)} %get-tuple-element.96), channel_id=1, source_target_pairs={{0,4},{2,6},{4,0},{6,2},{8,12},{10,14},{12,8},{14,10},{16,20},{18,... | collective-permute-start | bytes 1179656 | tf_op jit(solution)/shard_map/ppermute | solution.py:244
  7.5 39.4 %collective-permute-start.6 = (f32[4,6,32,128]{3,2,1,0:T(8,128)S(1)}, f32[4,6,32,128]{3,2,1,0:T(8,128)S(1)}, u32[]{:S(2)}, u32[]{:S(2)}) collective-permute-start(f32[4,6,32,128]{3,2,1,0:T(8,128)S(1)} %get-tuple-element.97), channel_id=1, source_target_pairs={{0,6},{2,4},{4,2},{6,0},{8,14},{10,12},{12,10},{14,8},{16,22},{18,... | collective-permute-start | bytes 1179656 | tf_op jit(solution)/shard_map/ppermute | solution.py:244
  9.3 22.9 %collective-permute-start.1 = (f32[4,6,24,128]{3,2,1,0:T(8,128)}, f32[4,6,24,128]{3,2,1,0:T(8,128)S(1)}, u32[]{:S(2)}, u32[]{:S(2)}) collective-permute-start(f32[4,6,24,128]{3,2,1,0:T(8,128)} %get-tuple-element.89), channel_id=1, source_target_pairs={{0,4},{2,6},{4,0},{6,2},{8,12},{10,14},{12,8},{14,10},{16,20},{18,... | collective-permute-start | bytes 884744 | tf_op jit(solution)/shard_map/ppermute | solution.py:244
  9.5 29.6 %collective-permute-start.2 = (f32[4,6,24,128]{3,2,1,0:T(8,128)}, f32[4,6,24,128]{3,2,1,0:T(8,128)S(1)}, u32[]{:S(2)}, u32[]{:S(2)}) collective-permute-start(f32[4,6,24,128]{3,2,1,0:T(8,128)} %get-tuple-element.90), channel_id=1, source_target_pairs={{0,6},{2,4},{4,2},{6,0},{8,14},{10,12},{12,10},{14,8},{16,22},{18,... | collective-permute-start | bytes 884744 | tf_op jit(solution)/shard_map/ppermute | solution.py:244
  48.2 27.8 %collective-permute-start.10 = (f32[3,17,32,128]{3,2,1,0:T(8,128)S(1)}, f32[3,17,32,128]{3,2,1,0:T(8,128)S(1)}, u32[]{:S(2)}, u32[]{:S(2)}) collective-permute-start(f32[3,17,32,128]{3,2,1,0:T(8,128)S(1)} %get-tuple-element.109.away_ref.refs_1_), channel_id=1, source_target_pairs={{0,8},{2,10},{4,12},{6,14},{24,16},{26,18},{28,20},{30,22},{1,9},{... | collective-permute-start | bytes 2506760 | tf_op jit(solution)/shard_map/ppermute | solution.py:244
  49.5 23.5 %collective-permute-start.13 = (f32[4,6,48,128]{3,2,1,0:T(8,128)S(1)}, f32[4,6,48,128]{3,2,1,0:T(8,128)S(1)}, u32[]{:S(2)}, u32[]{:S(2)}) collective-permute-start(f32[4,6,48,128]{3,2,1,0:T(8,128)S(1)} %get-tuple-element.113), channel_id=1, source_target_pairs={{0,6},{2,4},{4,2},{6,0},{8,14},{10,12},{12,10},{14,8},{16,22},{18,... | collective-permute-start | bytes 1769480 | tf_op jit(solution)/shard_map/ppermute | solution.py:244
  51.3 37.1 %collective-permute-start.16 = (f32[4,6,56,128]{3,2,1,0:T(8,128)S(1)}, f32[4,6,56,128]{3,2,1,0:T(8,128)S(1)}, u32[]{:S(2)}, u32[]{:S(2)}) collective-permute-start(f32[4,6,56,128]{3,2,1,0:T(8,128)S(1)} %get-tuple-element.119), channel_id=1, source_target_pairs={{0,2},{2,0},{4,6},{6,4},{8,10},{10,8},{12,14},{14,12},{16,18},{18,... | collective-permute-start | bytes 2064392 | tf_op jit(solution)/shard_map/ppermute | solution.py:244
  58.6 29.9 %collective-permute-start.17 = (f32[4,6,56,128]{3,2,1,0:T(8,128)S(1)}, f32[4,6,56,128]{3,2,1,0:T(8,128)S(1)}, u32[]{:S(2)}, u32[]{:S(2)}) collective-permute-start(f32[4,6,56,128]{3,2,1,0:T(8,128)S(1)} %get-tuple-element.120), channel_id=1, source_target_pairs={{0,4},{2,6},{4,0},{6,2},{8,12},{10,14},{12,8},{14,10},{16,20},{18,... | collective-permute-start | bytes 2064392 | tf_op jit(solution)/shard_map/ppermute | solution.py:244
  58.8 42.8 %collective-permute-start.18 = (f32[4,6,56,128]{3,2,1,0:T(8,128)S(1)}, f32[4,6,56,128]{3,2,1,0:T(8,128)S(1)}, u32[]{:S(2)}, u32[]{:S(2)}) collective-permute-start(f32[4,6,56,128]{3,2,1,0:T(8,128)S(1)} %get-tuple-element.121), channel_id=1, source_target_pairs={{0,6},{2,4},{4,2},{6,0},{8,14},{10,12},{12,10},{14,8},{16,22},{18,... | collective-permute-start | bytes 2064392 | tf_op jit(solution)/shard_map/ppermute | solution.py:244
  74.7 39.4 %collective-permute-start.15 = (f32[3,17,48,128]{3,2,1,0:T(8,128)S(1)}, f32[3,17,48,128]{3,2,1,0:T(8,128)S(1)}, u32[]{:S(2)}, u32[]{:S(2)}) collective-permute-start(f32[3,17,48,128]{3,2,1,0:T(8,128)S(1)} %get-tuple-element.117.away_ref.refs_1_), channel_id=1, source_target_pairs={{0,8},{2,10},{4,12},{6,14},{24,16},{26,18},{28,20},{30,22},{1,9},{... | collective-permute-start | bytes 3760136 | tf_op jit(solution)/shard_map/ppermute | solution.py:244
  103.7 44.4 %collective-permute-start.23 = (f32[3,17,56,128]{3,2,1,0:T(8,128)S(1)}, f32[3,17,56,128]{3,2,1,0:T(8,128)S(1)}, u32[]{:S(2)}, u32[]{:S(2)}) collective-permute-start(f32[3,17,56,128]{3,2,1,0:T(8,128)S(1)} %get-tuple-element.135.away_ref.refs_1_), channel_id=1, source_target_pairs={{0,8},{2,10},{4,12},{6,14},{24,16},{26,18},{28,20},{30,22},{1,9},{... | collective-permute-start | bytes 4386824 | tf_op jit(solution)/shard_map/ppermute | solution.py:244
  114.0 31.9 %collective-permute-start.26 = (f32[4,6,56,128]{3,2,1,0:T(8,128)S(1)}, f32[4,6,56,128]{3,2,1,0:T(8,128)S(1)}, u32[]{:S(2)}, u32[]{:S(2)}) collective-permute-start(f32[4,6,56,128]{3,2,1,0:T(8,128)S(1)} %get-tuple-element.139), channel_id=1, source_target_pairs={{0,6},{2,4},{4,2},{6,0},{8,14},{10,12},{12,10},{14,8},{16,22},{18,... | collective-permute-start | bytes 2064392 | tf_op jit(solution)/shard_map/ppermute | solution.py:244
  125.1 28.5 %collective-permute-start.22 = (f32[2,17,48,128]{3,2,1,0:T(8,128)S(1)}, f32[2,17,48,128]{3,2,1,0:T(8,128)S(1)}, u32[]{:S(2)}, u32[]{:S(2)}) collective-permute-start(f32[2,17,48,128]{3,2,1,0:T(8,128)S(1)} %get-tuple-element.134), channel_id=1, source_target_pairs={{8,16},{10,18},{12,20},{14,22},{16,8},{18,10},{20,12},{22,14},{9,1... | collective-permute-start | bytes 2506760 | tf_op jit(solution)/shard_map/ppermute | solution.py:244
  148.2 28.5 %collective-permute-start.33 = (f32[2,17,56,128]{3,2,1,0:T(8,128)S(1)}, f32[2,17,56,128]{3,2,1,0:T(8,128)S(1)}, u32[]{:S(2)}, u32[]{:S(2)}) collective-permute-start(f32[2,17,56,128]{3,2,1,0:T(8,128)S(1)} %get-tuple-element.154), channel_id=1, source_target_pairs={{8,16},{10,18},{12,20},{14,22},{16,8},{18,10},{20,12},{22,14},{9,1... | collective-permute-start | bytes 2924552 | tf_op jit(solution)/shard_map/ppermute | solution.py:244
  151.8 23.2 %collective-permute-start.9 = (f32[4,6,40,128]{3,2,1,0:T(8,128)S(1)}, f32[4,6,40,128]{3,2,1,0:T(8,128)S(1)}, u32[]{:S(2)}, u32[]{:S(2)}) collective-permute-start(f32[4,6,40,128]{3,2,1,0:T(8,128)S(1)} %get-tuple-element.107), channel_id=1, source_target_pairs={{0,6},{2,4},{4,2},{6,0},{8,14},{10,12},{12,10},{14,8},{16,22},{18,... | collective-permute-start | bytes 1474568 | tf_op jit(solution)/shard_map/ppermute | solution.py:244
  161.1 20.1 %collective-permute-start.30 = (f32[17,56,128]{2,1,0:T(8,128)S(1)}, f32[17,56,128]{2,1,0:T(8,128)S(1)}, u32[]{:S(2)}, u32[]{:S(2)}) collective-permute-start(f32[17,56,128]{2,1,0:T(8,128)S(1)} %get-tuple-element.150), channel_id=1, source_target_pairs={{0,8},{2,10},{4,12},{6,14},{8,0},{10,2},{12,4},{14,6},{16,24},{18,... | collective-permute-start | bytes 1462280 | tf_op jit(solution)/shard_map/ppermute | solution.py:244
  176.8 45.6 %collective-permute-start.34 = (f32[17,56,128]{2,1,0:T(8,128)S(1)}, f32[17,56,128]{2,1,0:T(8,128)S(1)}, u32[]{:S(2)}, u32[]{:S(2)}) collective-permute-start(f32[17,56,128]{2,1,0:T(8,128)S(1)} %get-tuple-element.156), channel_id=1, source_target_pairs={{8,0},{10,2},{12,4},{14,6},{16,24},{18,26},{20,28},{22,30},{9,1},{... | collective-permute-start | bytes 1462280 | tf_op jit(solution)/shard_map/ppermute | solution.py:244
  178.4 40.7 %collective-permute-start.35 = (f32[17,48,128]{2,1,0:T(8,128)S(1)}, f32[17,48,128]{2,1,0:T(8,128)S(1)}, u32[]{:S(2)}, u32[]{:S(2)}) collective-permute-start(f32[17,48,128]{2,1,0:T(8,128)S(1)} %get-tuple-element.157), channel_id=1, source_target_pairs={{8,0},{10,2},{12,4},{14,6},{16,24},{18,26},{20,28},{22,30},{9,1},{... | collective-permute-start | bytes 1253384 | tf_op jit(solution)/shard_map/ppermute | solution.py:244
  179.7 46.7 %collective-permute-start.31 = (f32[17,56,128]{2,1,0:T(8,128)S(1)}, f32[17,56,128]{2,1,0:T(8,128)S(1)}, u32[]{:S(2)}, u32[]{:S(2)}) collective-permute-start(f32[17,56,128]{2,1,0:T(8,128)S(1)} %get-tuple-element.151), channel_id=1, source_target_pairs={{0,16},{2,18},{4,20},{6,22},{8,24},{10,26},{12,28},{14,30},{16,0},... | collective-permute-start | bytes 1462280 | tf_op jit(solution)/shard_map/ppermute | solution.py:244
  180.1 58.9 %collective-permute-start.32 = (f32[17,56,128]{2,1,0:T(8,128)S(1)}, f32[17,56,128]{2,1,0:T(8,128)S(1)}, u32[]{:S(2)}, u32[]{:S(2)}) collective-permute-start(f32[17,56,128]{2,1,0:T(8,128)S(1)} %get-tuple-element.152), channel_id=1, source_target_pairs={{0,24},{2,26},{4,28},{6,30},{8,16},{10,18},{12,20},{14,22},{16,8},... | collective-permute-start | bytes 1462280 | tf_op jit(solution)/shard_map/ppermute | solution.py:244
  181.2 59.9 %collective-permute-start.27 = (f32[17,40,128]{2,1,0:T(8,128)S(1)}, f32[17,40,128]{2,1,0:T(8,128)S(1)}, u32[]{:S(2)}, u32[]{:S(2)}) collective-permute-start(f32[17,40,128]{2,1,0:T(8,128)S(1)} %get-tuple-element.146), channel_id=1, source_target_pairs={{0,8},{2,10},{4,12},{6,14},{8,0},{10,2},{12,4},{14,6},{16,24},{18,... | collective-permute-start | bytes 1044488 | tf_op jit(solution)/shard_map/ppermute | solution.py:244
  219.2 25.7 %collective-permute-start.28 = (f32[17,40,128]{2,1,0:T(8,128)S(1)}, f32[17,40,128]{2,1,0:T(8,128)S(1)}, u32[]{:S(2)}, u32[]{:S(2)}) collective-permute-start(f32[17,40,128]{2,1,0:T(8,128)S(1)} %get-tuple-element.147), channel_id=1, source_target_pairs={{0,16},{2,18},{4,20},{6,22},{8,24},{10,26},{12,28},{14,30},{16,0},... | collective-permute-start | bytes 1044488 | tf_op jit(solution)/shard_map/ppermute | solution.py:244
  222.4 31.6 %collective-permute-start.29 = (f32[17,40,128]{2,1,0:T(8,128)S(1)}, f32[17,40,128]{2,1,0:T(8,128)S(1)}, u32[]{:S(2)}, u32[]{:S(2)}) collective-permute-start(f32[17,40,128]{2,1,0:T(8,128)S(1)} %get-tuple-element.148), channel_id=1, source_target_pairs={{0,24},{2,26},{4,28},{6,30},{8,16},{10,18},{12,20},{14,22},{16,8},... | collective-permute-start | bytes 1044488 | tf_op jit(solution)/shard_map/ppermute | solution.py:244
  (12 other events, 152.3 us)

commit v2 on v1

v2 whole, which is shorter than its diff:
```python
import functools

import jax
import jax.numpy as jnp
import numpy as np
from jax import lax
from jax.experimental import pallas as pl
from jax.experimental.pallas import tpu as pltpu
from jax.sharding import PartitionSpec as P


TIMES = 96
HARM = 16
PERIOD = 12
SLOW = HARM - PERIOD
STATS = HARM + 1
PLANES = 4

ROUND = 3
PARTS = (7, 5, 7, 6, 4)
GROUPS = (("s", (0,)), ("s", (1,)), ("s", (2,)), ("s", (3,)), ("e", (4,)))
NEARS = ((0, 1), (2, 3, 4))
PAIRS = ((0,), (1, 2, 3, 4))
ORDER = " ".join((
    "p0 P0 q0 p1",
    "q1 p2 p3 p4",
    "t0 T0 t1 n0",
    "m0 m1 t2 r0",
    "r1 f0 t3 m2",
    "f1 t4 n1 m3",
    "F0 r2 m4 r3",
    "f2 f3 f4",
)).split()
FINAL_ROWS = 8
VMEM_LIMIT = 8 << 20


def basis_matrix(times):
    steps = np.arange(times, dtype=np.float64)
    columns = [np.ones_like(steps), (steps - (times - 1) / 2.0) / (times / 2.0)]
    for harmonic in range(1, 7):
        columns.append(np.cos(2.0 * np.pi * harmonic * steps / 12.0))
    for harmonic in range(1, 6):
        columns.append(np.sin(2.0 * np.pi * harmonic * steps / 12.0))
    columns.append(np.cos(2.0 * np.pi * steps / times))
    columns.append(np.sin(2.0 * np.pi * steps / times))
    columns.append(np.cos(4.0 * np.pi * steps / times))
    return np.stack(columns, axis=1)


PERIODIC = [0] + list(range(2, 13))
SLOWS = [1, 13, 14, 15]


def fit_matrices():
    basis = basis_matrix(TIMES)
    to_moments = np.zeros((HARM, HARM))
    for column in PERIODIC:
        to_moments[column, :PERIOD] = basis[:PERIOD, column]
    for at, column in enumerate(SLOWS):
        to_moments[column, PERIOD + at] = 1.0
    to_coeffs = np.linalg.solve(basis.T @ basis, to_moments)
    return to_moments, to_coeffs


def fit_block(block, basis, projector):
    width = block.shape[-1]
    lat_rows = block.shape[0] // TIMES
    series = block.reshape(TIMES, lat_rows * width)
    coeffs = jnp.dot(projector, series, precision=lax.Precision.HIGHEST)
    moments = jnp.dot(basis.T, series, precision=lax.Precision.HIGHEST)
    total = jnp.sum(series * series, axis=0)
    variance = (total - jnp.sum(coeffs * moments, axis=0)) / TIMES
    return coeffs.reshape(HARM, lat_rows, width), variance.reshape(lat_rows, width)


def general(snapshots):
    groups = lax.axis_size("io")
    local_rows = snapshots.shape[0]
    lon_dev = snapshots.shape[1] // groups
    split_view = snapshots.reshape(local_rows, groups, lon_dev)
    basis = basis_matrix(TIMES)
    projector = np.linalg.solve(basis.T @ basis, basis.T)
    moved = lax.all_to_all(split_view, "io", split_axis=1, concat_axis=0, tiled=True)
    return fit_block(moved[:, 0, :], jnp.float32(basis), jnp.float32(projector))


def fetch_kernel(pieces, where_ref, x_ref, *rest):
    outs, sem = rest[-1 - pieces(None) - 1 : -2], rest[-1]
    copies = []
    for out, to_rows, first, rows, at, column in pieces(where_ref):
        ref = outs[out] if at is None else outs[out].at[at]
        width = ref.shape[-1]
        source = x_ref.at[:, pl.ds(first, rows), pl.ds(pl.multiple_of(column, width), width)]
        copies.append(pltpu.make_async_copy(source, ref.at[:, pl.ds(to_rows, rows)], sem))
        copies[-1].start()
    for copy in copies:
        copy.wait()


def sums(values, weights, way, emit):
    slow, square = [None] * SLOW, None
    held = len(values[0])
    for k in range(held):
        for at, source in enumerate(values):
            for j in range(SLOW):
                term = source[k] * weights[way * SLOW + j, at * held + k]
                slow[j] = term if slow[j] is None else slow[j] + term
            term = source[k] * source[k]
            square = term if square is None else square + term
    for j in range(SLOW):
        emit(j, slow[j])
    emit(SLOW, square)


def row_blocks(rows, body):
    size = 16 if rows % 16 == 0 else 8

    @pl.loop(0, rows // size)
    def _(block):
        body(block * size, size)


def totals_kernel(offset, where_ref, weight_ref, own_ref, r1_ref, r2_ref, r3_ref, *rest):
    home_ref, near_ref, far_ref = rest[-4:-1]
    held, rows = own_ref.shape[1:3]
    first = (where_ref[0] % 2) * held
    second = held - first
    for step in range(PLANES):
        out_ref = (home_ref, near_ref, far_ref.at[0], far_ref.at[1])[step]

        def body(start, size):
            at, at1 = pl.ds(pl.multiple_of(start, 8), size), pl.ds(pl.multiple_of(start + offset, 8), size)
            values = [
                [ref[step, k, rows_] for k in range(held)]
                for ref, rows_ in ((own_ref, at), (r1_ref, at1), (r2_ref, at), (r3_ref, at))
            ]
            for k in range(held):
                out_ref[first + k, at] = values[0][k] + values[2][k]
                out_ref[second + k, at] = values[1][k] + values[3][k]

            def emit(row, value):
                out_ref[PERIOD + row, at] = value

            sums(values, weight_ref, 0, emit)

        row_blocks(rows, body)


def round_kernel(where_ref, weight_ref, *rest):
    sources, outs = rest[:PLANES], rest[-5:-1]
    held, rows = sources[0].shape[:2]
    width = outs[0].shape[-1]
    for shift, out_ref in enumerate(outs):
        column = pl.ds(pl.multiple_of((where_ref[0] ^ shift) * width, width), width)

        def body(start, size):
            at = pl.ds(pl.multiple_of(start, 8), size)
            values = [[ref[k, at, column] for k in range(held)] for ref in sources]
            for k in range(held):
                out_ref[k, at] = (values[0][k] + values[1][k]) + (values[2][k] + values[3][k])

            def emit(row, value):
                out_ref[held + row, at] = value

            sums(values, weight_ref, 1, emit)

        row_blocks(rows, body)


def join_kernel(count, *refs):
    out_ref, start = refs[-2], 0
    for ref in refs[:count]:
        rows = ref.shape[1]
        out_ref[:, start : start + rows] = ref[...]
        start += rows


def merge_kernel(count, straight, *refs):
    outs, start = refs[-3:-1] if straight else refs[-2:-1], 0
    for own_ref, in_ref in zip(refs[:count], refs[count : 2 * count]):
        rows = own_ref.shape[2]
        for hop in range(2):
            out_ref = outs[hop] if straight else outs[0].at[hop]
            out_ref[:, start : start + rows] = own_ref[hop] + in_ref[hop]
        start += rows


def relay_kernel(count, b_ref, *refs):
    out_ref, start = refs[-2], 0
    for ref in refs[:count]:
        rows = ref.shape[1]
        out_ref[:, start : start + rows] = ref[...] + b_ref[1, :, start : start + rows]
        start += rows


def solve(matrices, coeff_ref, var_ref, start, rows, load):
    to_moments, to_coeffs = matrices

    @pl.loop(0, rows // FINAL_ROWS)
    def _(block):
        at = pl.multiple_of(block * FINAL_ROWS, FINAL_ROWS)
        stats = [load(row, at) for row in range(STATS)]

        def mix(weights):
            total = None
            for weight, stat in zip(weights, stats):
                if abs(weight) > 1e-12:
                    term = stat if weight == 1.0 else stat * np.float32(weight)
                    total = term if total is None else total + term
            return total

        to = pl.ds(pl.multiple_of(start + at, FINAL_ROWS), FINAL_ROWS)
        explained = None
        for column in range(HARM):
            coeff = mix(to_coeffs[column])
            coeff_ref[column, to] = coeff
            term = coeff * mix(to_moments[column])
            explained = term if explained is None else explained + term
        var_ref[to] = (stats[HARM] - explained) * np.float32(1.0 / TIMES)


def store(first, coeff_out, var_out, coeff_ref, var_ref, sem):
    rows = var_ref.shape[0]
    copies = [
        pltpu.make_async_copy(coeff_ref, coeff_out.at[:, pl.ds(first, rows)], sem.at[0]),
        pltpu.make_async_copy(var_ref, var_out.at[pl.ds(first, rows)], sem.at[1]),
    ]
    for copy in copies:
        copy.start()
    for copy in copies:
        copy.wait()


def final_kernel(first, chunks, mode, matrices, where_ref, *refs):
    coeff_out, var_out, _, coeff_ref, var_ref, sem = refs[-6:]
    count = len(chunks)
    homes, owns, nears = refs[:count], refs[count : 2 * count], refs[2 * count : 3 * count]
    one_ref, two_ref = refs[3 * count : 3 * count + 2]

    @pl.when(where_ref[1] > 0)
    def _():
        start = 0
        for (rows, place), own_ref, in_ref in zip(chunks, owns, nears):

            def load(row, at, start=start, place=place, own_ref=own_ref, in_ref=in_ref):
                middle = one_ref if mode == "e" else one_ref.at[0]
                value = own_ref[row, pl.ds(at, FINAL_ROWS)] + in_ref[row, pl.ds(pl.multiple_of(at + place, 8), FINAL_ROWS)]
                return value + middle[row, pl.ds(pl.multiple_of(at + start, 8), FINAL_ROWS)]

            solve(matrices, coeff_ref, var_ref, start, rows, load)
            start += rows

    @pl.when(where_ref[1] == 0)
    def _():
        start = 0
        for (rows, place), home_ref in zip(chunks, homes):

            def load(row, at, start=start, home_ref=home_ref):
                value = home_ref[row, pl.ds(at, FINAL_ROWS)] + two_ref[row, pl.ds(pl.multiple_of(at + start, 8), FINAL_ROWS)]
                if mode == "e":
                    value = value + refs[3 * count + 2][row, pl.ds(at, FINAL_ROWS)]
                return value

            solve(matrices, coeff_ref, var_ref, start, rows, load)
            start += rows

    store(first, coeff_out, var_out, coeff_ref, var_ref, sem)


def round_final_kernel(held, matrices, where_ref, *refs):
    coeff_out, var_out, _, coeff_ref, var_ref, sem = refs[-6:]
    rows = var_ref.shape[0]

    def run(early, late):
        def load(row, at):
            rows_ = pl.ds(at, FINAL_ROWS)
            if row < PERIOD:
                one, two = early if row < held else late
                return one[row % held, rows_] + two[row % held, rows_]
            row = row - PERIOD + held
            return (refs[0][row, rows_] + refs[1][row, rows_]) + (refs[2][row, rows_] + refs[3][row, rows_])

        solve(matrices, coeff_ref, var_ref, 0, rows, load)

    @pl.when(where_ref[0] % 2 == 0)
    def _():
        run((refs[0], refs[2]), (refs[1], refs[3]))

    @pl.when(where_ref[0] % 2 == 1)
    def _():
        run((refs[1], refs[3]), (refs[0], refs[2]))

    store(0, coeff_out, var_out, coeff_ref, var_ref, sem)


def plane_plan(snapshots):
    groups = lax.axis_size("io")
    plane = groups // PLANES
    held = TIMES // groups
    lat = snapshots.shape[0] // held
    lon = snapshots.shape[1]
    width = lon // groups
    view = snapshots.reshape(held, lat, lon)

    me = lax.axis_index("io")
    place, level = me % plane, me // plane
    flip = (level >= PLANES // 2).astype(jnp.int32)
    inner = ((level > 0) & (level < PLANES - 1)).astype(jnp.int32)
    where = jnp.stack([place, inner, flip, level]).astype(jnp.int32)

    slow = basis_matrix(TIMES)[:, SLOWS].T
    table = np.zeros((groups, 2 * SLOW, plane * held), np.float32)
    for device in range(groups):
        for shift in range(plane):
            for way, other in enumerate((device ^ shift, device ^ (shift * plane))):
                rows, columns = way * SLOW, shift * held
                table[device, rows : rows + SLOW, columns : columns + held] = slow[:, other * held : (other + 1) * held]
    weights = lax.dynamic_index_in_dim(jnp.asarray(table), me, 0, keepdims=False)
    matrices = fit_matrices()

    smem = pl.BlockSpec(memory_space=pltpu.SMEM)
    vmem = pl.BlockSpec(memory_space=pltpu.VMEM)
    hbm = pl.BlockSpec(memory_space=pltpu.HBM)
    space = {id(vmem): pltpu.VMEM, id(hbm): pltpu.HBM}
    token = [weights]

    def near(*dims):
        return pltpu.VMEM(dims, jnp.float32)

    def call(kernel, flops, moved, ins, args, outs, out_specs=None, **more):
        ins, args = ins + [hbm] * len(token), list(args) + token
        args = [
            pltpu.with_memory_space_constraint(arg, space[id(spec)]) if id(spec) in space else arg
            for spec, arg in zip(ins, args)
        ]
        *results, last = pl.pallas_call(
            kernel,
            in_specs=ins,
            out_specs=(out_specs or [vmem] * len(outs)) + [hbm],
            out_shape=outs + [pltpu.HBM((8, 128), jnp.float32)],
            cost_estimate=pl.CostEstimate(flops=flops, bytes_accessed=moved, transcendentals=0),
            compiler_params=pltpu.CompilerParams(vmem_limit_bytes=VMEM_LIMIT),
            **more,
        )(*args)
        token[:] = [last]
        return results

    def move(value, pairs):
        return lax.ppermute(value, "io", pairs)

    unit = lat // (ROUND + sum(PARTS))
    sizes = [part * unit for part in PARTS]
    firsts = [(ROUND + sum(PARTS[:chunk])) * unit for chunk in range(len(PARTS))]
    turn = ROUND * unit
    swaps = [[(i, i ^ shift) for i in range(groups)] for shift in range(plane)]
    hops = [[(i, i ^ (step * plane)) for i in range(groups)] for step in range(PLANES)]
    to_inner = [(i, i + plane) for i in range(plane)] + [(i, i - plane) for i in range(groups - plane, groups)]
    to_outer = [(b, a) for a, b in to_inner]
    middle = [(i, i + plane) for i in range(plane, 2 * plane)]
    middle = middle + [(b, a) for a, b in middle]
    across = [(i, i + 2 * plane) for i in range(plane, 2 * plane)]
    across = across + [(i, i - 2 * plane) for i in range(2 * plane, 3 * plane)]

    def fetch(outs, pieces, rows):
        def count_or_pieces(where_ref):
            return len(outs) if where_ref is None else pieces(where_ref)

        return call(
            functools.partial(fetch_kernel, count_or_pieces), rows * lon, rows * lon * held * 8,
            [smem, hbm], [where, view], outs, scratch_shapes=[pltpu.SemaphoreType.DMA],
        )

    def column(where_ref, step, shift):
        zone = jnp.where(where_ref[2] > 0, PLANES - 1 - step, step)
        return (zone * plane + (where_ref[0] ^ shift)) * width

    def finish(kernel, rows, args, outs):
        count = len(args)
        return call(
            kernel, rows * width * 832, rows * width * 272,
            [smem] + [vmem] * count + [hbm] * len(outs), [where, *args, *outs],
            [pltpu.HBM((HARM, lat, width), jnp.float32), pltpu.HBM((lat, width), jnp.float32)], [hbm, hbm],
            input_output_aliases={count + 1: 0, count + 2: 1} if outs else {},
            scratch_shapes=[
                pltpu.VMEM((HARM, rows, width), jnp.float32),
                pltpu.VMEM((rows, width), jnp.float32),
                pltpu.SemaphoreType.DMA((2,)),
            ],
        )

    packed, paired, home, own, far, moved, outs = {}, {}, {}, {}, {}, {}, []
    for item in ORDER:
        kind, at = item[0], int(item[1:])
        if kind == "P":
            parts = fetch(
                [near(held, turn, plane * width)] * PLANES,
                lambda w: [(step, 0, 0, turn, None, (w[3] ^ step) * plane * width) for step in (3, 2, 1, 0)], turn,
            )
            around = [move(parts[step], hops[step]) for step in (3, 2, 1)]
            around = parts[:1] + around[::-1]
        elif kind == "T":
            parts = call(
                round_kernel, turn * lon * 60, turn * lon * held * 4,
                [smem, smem] + [vmem] * PLANES, [where, weights, *around],
                [near(held + SLOW + 1, turn, width)] * plane,
            )
            around = parts[:1] + [move(parts[shift], swaps[shift]) for shift in range(1, plane)]
        elif kind == "F":
            outs = finish(functools.partial(round_final_kernel, held, matrices), turn, around, outs)
        elif kind == "p":
            first, rows = firsts[at], sizes[at]
            parts = fetch(
                [near(PLANES, held, rows, width)] * 3,
                lambda w, first=first, rows=rows: [
                    (out, 0, first, rows, step, column(w, step, shift))
                    for out, shift in ((1, 2), (2, 3), (0, 0))
                    for step in range(PLANES)
                ],
                rows,
            )
            packed[at] = [parts[0], move(parts[1], swaps[2]), move(parts[2], swaps[3])]
        elif kind == "q":
            first, rows = firsts[PAIRS[at][0]], sum(sizes[chunk] for chunk in PAIRS[at])
            (part,) = fetch(
                [near(PLANES, held, rows, width)],
                lambda w, first=first, rows=rows: [(0, 0, first, rows, step, column(w, step, 1)) for step in range(PLANES)],
                rows,
            )
            part = move(part, swaps[1])
            for chunk in PAIRS[at]:
                paired[chunk] = (part, firsts[chunk] - first)
        elif kind == "t":
            rows = sizes[at]
            mode = next(mode for mode, chunks in GROUPS if at in chunks)
            part, offset = paired[at]
            home[at], own[at], far[at] = call(
                functools.partial(totals_kernel, offset), rows * width * PLANES * 240, rows * width * 656,
                [smem, smem] + [vmem] * plane, [where, weights, packed[at][0], part, *packed[at][1:]],
                [near(STATS, rows, width)] * 2 + [near(2, STATS, rows, width)],
            )
            moved["a", at] = move(far[at], to_inner)
            if mode == "e":
                moved["h", at] = move(home[at], to_outer)
        elif kind == "n":
            chunks = NEARS[at]
            rows = sum(sizes[chunk] for chunk in chunks)
            (part,) = call(
                functools.partial(join_kernel, len(chunks)), rows * width * 17, rows * width * 136,
                [vmem] * len(chunks), [own[chunk] for chunk in chunks], [near(STATS, rows, width)],
            )
            part = move(part, to_inner)
            for chunk in chunks:
                moved["n", chunk] = (part, sum(sizes[other] for other in chunks if other < chunk))
        elif kind == "m":
            mode, chunks = GROUPS[at]
            rows = sum(sizes[chunk] for chunk in chunks)
            shapes = [near(STATS, rows, width)] * 2 if mode == "e" else [near(2, STATS, rows, width)]
            args = [far[chunk] for chunk in chunks] + [moved["a", chunk] for chunk in chunks]
            parts = call(
                functools.partial(merge_kernel, len(chunks), mode == "e"), rows * width * 34, rows * width * 408,
                [vmem] * len(args), args, shapes,
            )
            moved["b", at] = move(parts[0], middle)
            if mode == "e":
                moved["g", at] = move(parts[1], across)
        elif kind == "r":
            chunks = GROUPS[at][1]
            rows = sum(sizes[chunk] for chunk in chunks)
            (part,) = call(
                functools.partial(relay_kernel, len(chunks)), rows * width * 17, rows * width * 204,
                [vmem] * (1 + len(chunks)), [moved["b", at]] + [home[chunk] for chunk in chunks],
                [near(STATS, rows, width)],
            )
            moved["c", at] = move(part, to_outer)
        else:
            mode, chunks = GROUPS[at]
            rows = sum(sizes[chunk] for chunk in chunks)
            args = [home[chunk] for chunk in chunks] + [own[chunk] for chunk in chunks]
            args += [moved["n", chunk][0] for chunk in chunks] + [moved["b", at]]
            args += [moved["g", at], moved["h", chunks[0]]] if mode == "e" else [moved["c", at]]
            places = [(sizes[chunk], moved["n", chunk][1]) for chunk in chunks]
            kernel = functools.partial(final_kernel, firsts[chunks[0]], places, mode, matrices)
            outs = finish(kernel, rows, args, outs)
    return tuple(outs)


def fits(groups):
    return groups == 4 * PLANES and TIMES % groups == 0 and TIMES // PLANES == 2 * PERIOD


def local(snapshots):
    groups = lax.axis_size("io")
    lat = snapshots.shape[0] * groups // TIMES
    if fits(groups) and lat % (8 * (ROUND + sum(PARTS))) == 0 and snapshots.shape[1] == 128 * groups:
        return plane_plan(snapshots)
    return general(snapshots)


def solution(mesh):
    return jax.shard_map(
        local,
        mesh=mesh,
        in_specs=(P(("rep", "io"), None),),
        out_specs=(P("rep", None, "io"), P("rep", "io")),
        check_vma=False,
    )
```

time: 256 us -> 252 us (0.984)
  the two profiles are of different devices: /device:TPU:11 before, /device:TPU:0 now
where the time goes in v2:
time: 252 us; the launch traced here: 251 us
  waiting for transfers between devices  147 us (58%)
  starting transfers between devices  63 us (25%)
  Pallas kernels  38.1 us (15%)
    ppermute x36, waiting for transfers between devices, move(): return lax.ppermute(value, 'io', pairs)  147 us
    ppermute x36, starting transfers between devices, move(): return lax.ppermute(value, 'io', pairs)  63 us
    pallas_call x31, Pallas kernels, call(): pl.pallas_call(kernel, in_specs=ins, out_specs=(out_specs or [vmem] * len...  38.1 us
  transfers between devices with their start and end apart: 36, of which 16 were waited for; matrix products, arithmetic and copies ran while one was open for 0% of the time, Pallas kernels for 11%

profile of v2, /device:TPU:0, one launch (start us, length us, event | category | flops | bytes accessed | tf_op | source)
XLA Modules:
  0.0 251.1 jit_solution(5060256743177602485)
XLA Ops:
  2.0 2.2 shard_map.41
  12.6 2.6 %collective-permute-start.10 = (f32[4,6,56,128]{3,2,1,0:T(8,128)S(1)}, f32[4,6,56,128]{3,2,1,0:T(8,128)S(1)}, u32[]{:S(2)}, u32[]{:S(2)}) collective-permute-start(f32[4,6,56,128]{3,2,1,0:T(8,128)S(1)} %get-tuple-element.117), channel_id=1, source_target_pairs={{0,6},{2,4},{4,2},{6,0},{8,14},{10,12},{12,10},{14,8},{16,22},{18,... | collective-permute-start | bytes 2064392 | tf_op jit(solution)/shard_map/ppermute | solution.py:350
  23.6 7.4 %collective-permute-done.10.r3_ref = f32[4,6,56,128]{3,2,1,0:T(8,128)S(1)} collective-permute-done((f32[4,6,56,128]{3,2,1,0:T(8,128)S(1)}, f32[4,6,56,128]{3,2,1,0:T(8,128)S(1)}, u32[]{:S(2)}, u32[]{:S(2)}) %collective-permute-start.10) | collective-permute-done | bytes 688160 | tf_op jit(solution)/shard_map/ppermute | solution.py:350
  31.0 14.9 %collective-permute-done.9.r2_ref = f32[4,6,56,128]{3,2,1,0:T(8,128)S(1)} collective-permute-done((f32[4,6,56,128]{3,2,1,0:T(8,128)S(1)}, f32[4,6,56,128]{3,2,1,0:T(8,128)S(1)}, u32[]{:S(2)}, u32[]{:S(2)}) %collective-permute-start.9) | collective-permute-done | bytes 688160 | tf_op jit(solution)/shard_map/ppermute | solution.py:350
  48.1 4.1 %collective-permute-start.13 = (f32[2,17,56,128]{3,2,1,0:T(8,128)S(1)}, f32[2,17,56,128]{3,2,1,0:T(8,128)S(1)}, u32[]{:S(2)}, u32[]{:S(2)}) collective-permute-start(f32[2,17,56,128]{3,2,1,0:T(8,128)S(1)} %get-tuple-element.127.refs_0_), channel_id=1, source_target_pairs={{0,8},{2,10},{4,12},{6,14},{24,16},{26,18},{28,20},{30,22},{1,9},{... | collective-permute-start | bytes 2924552 | tf_op jit(solution)/shard_map/ppermute | solution.py:350
  54.1 25.2 %collective-permute-done.6.rest_2_ = f32[6,24,512]{2,1,0:T(8,128)S(1)} collective-permute-done((f32[6,24,512]{2,1,0:T(8,128)S(1)}, f32[6,24,512]{2,1,0:T(8,128)S(1)}, u32[]{:S(2)}, u32[]{:S(2)}) %collective-permute-start.6) | collective-permute-done | bytes 294944 | tf_op jit(solution)/shard_map/ppermute | solution.py:350
  79.3 2.5 collective-permute-start.7
  81.7 7.3 %collective-permute-done.7.rest_3_ = f32[6,24,512]{2,1,0:T(8,128)S(1)} collective-permute-done((f32[6,24,512]{2,1,0:T(8,128)S(1)}, f32[6,24,512]{2,1,0:T(8,128)S(1)}, u32[]{:S(2)}, u32[]{:S(2)}) %collective-permute-start.7) | collective-permute-done | bytes 294944 | tf_op jit(solution)/shard_map/ppermute | solution.py:350
  92.1 8.7 %collective-permute-start.12 = (f32[2,17,40,128]{3,2,1,0:T(8,128)S(1)}, f32[2,17,40,128]{3,2,1,0:T(8,128)S(1)}, u32[]{:S(2)}, u32[]{:S(2)}) collective-permute-start(f32[2,17,40,128]{3,2,1,0:T(8,128)S(1)} %get-tuple-element.126.refs_0_), channel_id=1, source_target_pairs={{0,8},{2,10},{4,12},{6,14},{24,16},{26,18},{28,20},{30,22},{1,9},{... | collective-permute-start | bytes 2088968 | tf_op jit(solution)/shard_map/ppermute | solution.py:350
  103.3 12.5 %collective-permute-done.12.refs_1_ = f32[2,17,40,128]{3,2,1,0:T(8,128)S(1)} collective-permute-done((f32[2,17,40,128]{3,2,1,0:T(8,128)S(1)}, f32[2,17,40,128]{3,2,1,0:T(8,128)S(1)}, u32[]{:S(2)}, u32[]{:S(2)}) %collective-permute-start.12) | collective-permute-done | bytes 696352 | tf_op jit(solution)/shard_map/ppermute | solution.py:350
  116.6 7.2 %collective-permute-start.11 = (f32[17,96,128]{2,1,0:T(8,128)S(1)}, f32[17,96,128]{2,1,0:T(8,128)S(1)}, u32[]{:S(2)}, u32[]{:S(2)}) collective-permute-start(f32[17,96,128]{2,1,0:T(8,128)S(1)} %get-tuple-element.125), channel_id=1, source_target_pairs={{0,8},{2,10},{4,12},{6,14},{24,16},{26,18},{28,20},{30,22},{1,9},{... | collective-permute-start | bytes 2506760 | tf_op jit(solution)/shard_map/ppermute | solution.py:350
  125.4 8.5 %collective-permute-done.17.r3_ref = f32[4,6,56,128]{3,2,1,0:T(8,128)S(1)} collective-permute-done((f32[4,6,56,128]{3,2,1,0:T(8,128)S(1)}, f32[4,6,56,128]{3,2,1,0:T(8,128)S(1)}, u32[]{:S(2)}, u32[]{:S(2)}) %collective-permute-start.17) | collective-permute-done | bytes 688160 | tf_op jit(solution)/shard_map/ppermute | solution.py:350
  139.2 4.6 %collective-permute-start.20 = (f32[2,17,56,128]{3,2,1,0:T(8,128)S(1)}, f32[2,17,56,128]{3,2,1,0:T(8,128)S(1)}, u32[]{:S(2)}, u32[]{:S(2)}) collective-permute-start(f32[2,17,56,128]{3,2,1,0:T(8,128)S(1)} %get-tuple-element.144.refs_0_), channel_id=1, source_target_pairs={{0,8},{2,10},{4,12},{6,14},{24,16},{26,18},{28,20},{30,22},{1,9},{... | collective-permute-start | bytes 2924552 | tf_op jit(solution)/shard_map/ppermute | solution.py:350
  143.9 7.9 %collective-permute-done.19.refs_4_ = f32[17,56,128]{2,1,0:T(8,128)S(1)} collective-permute-done((f32[17,56,128]{2,1,0:T(8,128)S(1)}, f32[17,56,128]{2,1,0:T(8,128)S(1)}, u32[]{:S(2)}, u32[]{:S(2)}) %collective-permute-start.19) | collective-permute-done | bytes 487456 | tf_op jit(solution)/shard_map/ppermute | solution.py:350
  153.8 4.1 %collective-permute-done.22.r3_ref = f32[4,6,48,128]{3,2,1,0:T(8,128)S(1)} collective-permute-done((f32[4,6,48,128]{3,2,1,0:T(8,128)S(1)}, f32[4,6,48,128]{3,2,1,0:T(8,128)S(1)}, u32[]{:S(2)}, u32[]{:S(2)}) %collective-permute-start.22) | collective-permute-done | bytes 589856 | tf_op jit(solution)/shard_map/ppermute | solution.py:350
  159.6 4.1 %collective-permute-start.29 = (f32[2,17,48,128]{3,2,1,0:T(8,128)S(1)}, f32[2,17,48,128]{3,2,1,0:T(8,128)S(1)}, u32[]{:S(2)}, u32[]{:S(2)}) collective-permute-start(f32[2,17,48,128]{3,2,1,0:T(8,128)S(1)} %get-tuple-element.167.refs_0_), channel_id=1, source_target_pairs={{0,8},{2,10},{4,12},{6,14},{24,16},{26,18},{28,20},{30,22},{1,9},{... | collective-permute-start | bytes 2506760 | tf_op jit(solution)/shard_map/ppermute | solution.py:350
  168.1 9.7 %collective-permute-done.18.refs_4_ = f32[17,40,128]{2,1,0:T(8,128)S(1)} collective-permute-done((f32[17,40,128]{2,1,0:T(8,128)S(1)}, f32[17,40,128]{2,1,0:T(8,128)S(1)}, u32[]{:S(2)}, u32[]{:S(2)}) %collective-permute-start.18) | collective-permute-done | bytes 348192 | tf_op jit(solution)/shard_map/ppermute | solution.py:350
  179.6 4.3 %collective-permute-done.2.r3_ref = f32[4,6,32,128]{3,2,1,0:T(8,128)S(1)} collective-permute-done((f32[4,6,32,128]{3,2,1,0:T(8,128)S(1)}, f32[4,6,32,128]{3,2,1,0:T(8,128)S(1)}, u32[]{:S(2)}, u32[]{:S(2)}) %collective-permute-start.2) | collective-permute-done | bytes 393248 | tf_op jit(solution)/shard_map/ppermute | solution.py:350
  187.8 2.9 %collective-permute-start.24 = (f32[2,17,32,128]{3,2,1,0:T(8,128)S(1)}, f32[2,17,32,128]{3,2,1,0:T(8,128)S(1)}, u32[]{:S(2)}, u32[]{:S(2)}) collective-permute-start(f32[2,17,32,128]{3,2,1,0:T(8,128)S(1)} %get-tuple-element.158.refs_0_), channel_id=1, source_target_pairs={{0,8},{2,10},{4,12},{6,14},{24,16},{26,18},{28,20},{30,22},{1,9},{... | collective-permute-start | bytes 1671176 | tf_op jit(solution)/shard_map/ppermute | solution.py:350
  193.3 4.4 %collective-permute-done.27.refs_2_ = f32[11,24,128]{2,1,0:T(8,128)S(1)} collective-permute-done((f32[11,24,128]{2,1,0:T(8,128)S(1)}, f32[11,24,128]{2,1,0:T(8,128)S(1)}, u32[]{:S(2)}, u32[]{:S(2)}) %collective-permute-start.27) | collective-permute-done | bytes 135200 | tf_op jit(solution)/shard_map/ppermute | solution.py:350
  197.9 5.5 %collective-permute-done.28.refs_3_ = f32[11,24,128]{2,1,0:T(8,128)S(1)} collective-permute-done((f32[11,24,128]{2,1,0:T(8,128)S(1)}, f32[11,24,128]{2,1,0:T(8,128)S(1)}, u32[]{:S(2)}, u32[]{:S(2)}) %collective-permute-start.28) | collective-permute-done | bytes 135200 | tf_op jit(solution)/shard_map/ppermute | solution.py:350
  206.4 18.1 %collective-permute-done.24.refs_1_ = f32[2,17,32,128]{3,2,1,0:T(8,128)S(1)} collective-permute-done((f32[2,17,32,128]{3,2,1,0:T(8,128)S(1)}, f32[2,17,32,128]{3,2,1,0:T(8,128)S(1)}, u32[]{:S(2)}, u32[]{:S(2)}) %collective-permute-start.24) | collective-permute-done | bytes 557088 | tf_op jit(solution)/shard_map/ppermute | solution.py:350
  231.2 9.6 %collective-permute-done.34.refs_4_ = f32[17,48,128]{2,1,0:T(8,128)S(1)} collective-permute-done((f32[17,48,128]{2,1,0:T(8,128)S(1)}, f32[17,48,128]{2,1,0:T(8,128)S(1)}, u32[]{:S(2)}, u32[]{:S(2)}) %collective-permute-start.34) | collective-permute-done | bytes 417824 | tf_op jit(solution)/shard_map/ppermute | solution.py:350
  242.7 6.7 %collective-permute-done.32.refs_5_ = f32[17,32,128]{2,1,0:T(8,128)S(1)} collective-permute-done((f32[17,32,128]{2,1,0:T(8,128)S(1)}, f32[17,32,128]{2,1,0:T(8,128)S(1)}, u32[]{:S(2)}, u32[]{:S(2)}) %collective-permute-start.32) | collective-permute-done | bytes 278560 | tf_op jit(solution)/shard_map/ppermute | solution.py:350
  (83 shorter events, 64.8 us)
Async XLA Ops:
  12.0 78.4 %collective-permute-start = (f32[4,6,176,128]{3,2,1,0:T(8,128)S(1)}, f32[4,6,176,128]{3,2,1,0:T(8,128)S(1)}, u32[]{:S(2)}, u32[]{:S(2)}) collective-permute-start(f32[4,6,176,128]{3,2,1,0:T(8,128)S(1)} %get-tuple-element.104), channel_id=1, source_target_pairs={{0,2},{2,0},{4,6},{6,4},{8,10},{10,8},{12,14},{14,12},{16,18},{18,... | collective-permute-start | bytes 6488072 | tf_op jit(solution)/shard_map/ppermute | solution.py:350
  15.2 30.7 %collective-permute-start.9 = (f32[4,6,56,128]{3,2,1,0:T(8,128)S(1)}, f32[4,6,56,128]{3,2,1,0:T(8,128)S(1)}, u32[]{:S(2)}, u32[]{:S(2)}) collective-permute-start(f32[4,6,56,128]{3,2,1,0:T(8,128)S(1)} %get-tuple-element.116), channel_id=1, source_target_pairs={{0,4},{2,6},{4,0},{6,2},{8,12},{10,14},{12,8},{14,10},{16,20},{18,... | collective-permute-start | bytes 2064392 | tf_op jit(solution)/shard_map/ppermute | solution.py:350
  15.5 38.5 %collective-permute-start.5 = (f32[6,24,512]{2,1,0:T(8,128)S(1)}, f32[6,24,512]{2,1,0:T(8,128)S(1)}, u32[]{:S(2)}, u32[]{:S(2)}) collective-permute-start(f32[6,24,512]{2,1,0:T(8,128)S(1)} %get-tuple-element.111), channel_id=1, source_target_pairs={{0,8},{2,10},{4,12},{6,14},{8,0},{10,2},{12,4},{14,6},{16,24},{18,... | collective-permute-start | bytes 884744 | tf_op jit(solution)/shard_map/ppermute | solution.py:350
  48.1 52.8 %collective-permute-start.13 = (f32[2,17,56,128]{3,2,1,0:T(8,128)S(1)}, f32[2,17,56,128]{3,2,1,0:T(8,128)S(1)}, u32[]{:S(2)}, u32[]{:S(2)}) collective-permute-start(f32[2,17,56,128]{3,2,1,0:T(8,128)S(1)} %get-tuple-element.127.refs_0_), channel_id=1, source_target_pairs={{0,8},{2,10},{4,12},{6,14},{24,16},{26,18},{28,20},{30,22},{1,9},{... | collective-permute-start | bytes 2924552 | tf_op jit(solution)/shard_map/ppermute | solution.py:350
  52.2 27.1 %collective-permute-start.6 = (f32[6,24,512]{2,1,0:T(8,128)S(1)}, f32[6,24,512]{2,1,0:T(8,128)S(1)}, u32[]{:S(2)}, u32[]{:S(2)}) collective-permute-start(f32[6,24,512]{2,1,0:T(8,128)S(1)} %get-tuple-element.112), channel_id=1, source_target_pairs={{0,16},{2,18},{4,20},{6,22},{8,24},{10,26},{12,28},{14,30},{16,0},... | collective-permute-start | bytes 884744 | tf_op jit(solution)/shard_map/ppermute | solution.py:350
  52.6 37.8 %collective-permute-start.3 = (f32[4,6,40,128]{3,2,1,0:T(8,128)S(1)}, f32[4,6,40,128]{3,2,1,0:T(8,128)S(1)}, u32[]{:S(2)}, u32[]{:S(2)}) collective-permute-start(f32[4,6,40,128]{3,2,1,0:T(8,128)S(1)} %get-tuple-element.108), channel_id=1, source_target_pairs={{0,4},{2,6},{4,0},{6,2},{8,12},{10,14},{12,8},{14,10},{16,20},{18,... | collective-permute-start | bytes 1474568 | tf_op jit(solution)/shard_map/ppermute | solution.py:350
  54.1 36.3 %collective-permute-start.4 = (f32[4,6,40,128]{3,2,1,0:T(8,128)S(1)}, f32[4,6,40,128]{3,2,1,0:T(8,128)S(1)}, u32[]{:S(2)}, u32[]{:S(2)}) collective-permute-start(f32[4,6,40,128]{3,2,1,0:T(8,128)S(1)} %get-tuple-element.109), channel_id=1, source_target_pairs={{0,6},{2,4},{4,2},{6,0},{8,14},{10,12},{12,10},{14,8},{16,22},{18,... | collective-permute-start | bytes 1474568 | tf_op jit(solution)/shard_map/ppermute | solution.py:350
  92.1 23.7 %collective-permute-start.12 = (f32[2,17,40,128]{3,2,1,0:T(8,128)S(1)}, f32[2,17,40,128]{3,2,1,0:T(8,128)S(1)}, u32[]{:S(2)}, u32[]{:S(2)}) collective-permute-start(f32[2,17,40,128]{3,2,1,0:T(8,128)S(1)} %get-tuple-element.126.refs_0_), channel_id=1, source_target_pairs={{0,8},{2,10},{4,12},{6,14},{24,16},{26,18},{28,20},{30,22},{1,9},{... | collective-permute-start | bytes 2088968 | tf_op jit(solution)/shard_map/ppermute | solution.py:350
  101.0 36.9 %collective-permute-start.15 = (f32[2,17,56,128]{3,2,1,0:T(8,128)S(1)}, f32[2,17,56,128]{3,2,1,0:T(8,128)S(1)}, u32[]{:S(2)}, u32[]{:S(2)}) collective-permute-start(f32[2,17,56,128]{3,2,1,0:T(8,128)S(1)} %get-tuple-element.131), channel_id=1, source_target_pairs={{8,16},{10,18},{12,20},{14,22},{16,8},{18,10},{20,12},{22,14},{9,1... | collective-permute-start | bytes 2924552 | tf_op jit(solution)/shard_map/ppermute | solution.py:350
  101.7 22.1 %collective-permute-start.16 = (f32[4,6,56,128]{3,2,1,0:T(8,128)S(1)}, f32[4,6,56,128]{3,2,1,0:T(8,128)S(1)}, u32[]{:S(2)}, u32[]{:S(2)}) collective-permute-start(f32[4,6,56,128]{3,2,1,0:T(8,128)S(1)} %get-tuple-element.134), channel_id=1, source_target_pairs={{0,4},{2,6},{4,0},{6,2},{8,12},{10,14},{12,8},{14,10},{16,20},{18,... | collective-permute-start | bytes 2064392 | tf_op jit(solution)/shard_map/ppermute | solution.py:350
  103.3 30.6 %collective-permute-start.17 = (f32[4,6,56,128]{3,2,1,0:T(8,128)S(1)}, f32[4,6,56,128]{3,2,1,0:T(8,128)S(1)}, u32[]{:S(2)}, u32[]{:S(2)}) collective-permute-start(f32[4,6,56,128]{3,2,1,0:T(8,128)S(1)} %get-tuple-element.135), channel_id=1, source_target_pairs={{0,6},{2,4},{4,2},{6,0},{8,14},{10,12},{12,10},{14,8},{16,22},{18,... | collective-permute-start | bytes 2064392 | tf_op jit(solution)/shard_map/ppermute | solution.py:350
  115.9 23.3 %collective-permute-start.14 = (f32[2,17,40,128]{3,2,1,0:T(8,128)S(1)}, f32[2,17,40,128]{3,2,1,0:T(8,128)S(1)}, u32[]{:S(2)}, u32[]{:S(2)}) collective-permute-start(f32[2,17,40,128]{3,2,1,0:T(8,128)S(1)} %get-tuple-element.130), channel_id=1, source_target_pairs={{8,16},{10,18},{12,20},{14,22},{16,8},{18,10},{20,12},{22,14},{9,1... | collective-permute-start | bytes 2088968 | tf_op jit(solution)/shard_map/ppermute | solution.py:350
  116.6 27.3 %collective-permute-start.11 = (f32[17,96,128]{2,1,0:T(8,128)S(1)}, f32[17,96,128]{2,1,0:T(8,128)S(1)}, u32[]{:S(2)}, u32[]{:S(2)}) collective-permute-start(f32[17,96,128]{2,1,0:T(8,128)S(1)} %get-tuple-element.125), channel_id=1, source_target_pairs={{0,8},{2,10},{4,12},{6,14},{24,16},{26,18},{28,20},{30,22},{1,9},{... | collective-permute-start | bytes 2506760 | tf_op jit(solution)/shard_map/ppermute | solution.py:350
  123.8 30.0 %collective-permute-start.21 = (f32[4,6,48,128]{3,2,1,0:T(8,128)S(1)}, f32[4,6,48,128]{3,2,1,0:T(8,128)S(1)}, u32[]{:S(2)}, u32[]{:S(2)}) collective-permute-start(f32[4,6,48,128]{3,2,1,0:T(8,128)S(1)} %get-tuple-element.146), channel_id=1, source_target_pairs={{0,4},{2,6},{4,0},{6,2},{8,12},{10,14},{12,8},{14,10},{16,20},{18,... | collective-permute-start | bytes 1769480 | tf_op jit(solution)/shard_map/ppermute | solution.py:350
  133.9 24.1 %collective-permute-start.22 = (f32[4,6,48,128]{3,2,1,0:T(8,128)S(1)}, f32[4,6,48,128]{3,2,1,0:T(8,128)S(1)}, u32[]{:S(2)}, u32[]{:S(2)}) collective-permute-start(f32[4,6,48,128]{3,2,1,0:T(8,128)S(1)} %get-tuple-element.147), channel_id=1, source_target_pairs={{0,6},{2,4},{4,2},{6,0},{8,14},{10,12},{12,10},{14,8},{16,22},{18,... | collective-permute-start | bytes 1769480 | tf_op jit(solution)/shard_map/ppermute | solution.py:350
  139.2 28.0 %collective-permute-start.20 = (f32[2,17,56,128]{3,2,1,0:T(8,128)S(1)}, f32[2,17,56,128]{3,2,1,0:T(8,128)S(1)}, u32[]{:S(2)}, u32[]{:S(2)}) collective-permute-start(f32[2,17,56,128]{3,2,1,0:T(8,128)S(1)} %get-tuple-element.144.refs_0_), channel_id=1, source_target_pairs={{0,8},{2,10},{4,12},{6,14},{24,16},{26,18},{28,20},{30,22},{1,9},{... | collective-permute-start | bytes 2924552 | tf_op jit(solution)/shard_map/ppermute | solution.py:350
  159.6 27.3 %collective-permute-start.29 = (f32[2,17,48,128]{3,2,1,0:T(8,128)S(1)}, f32[2,17,48,128]{3,2,1,0:T(8,128)S(1)}, u32[]{:S(2)}, u32[]{:S(2)}) collective-permute-start(f32[2,17,48,128]{3,2,1,0:T(8,128)S(1)} %get-tuple-element.167.refs_0_), channel_id=1, source_target_pairs={{0,8},{2,10},{4,12},{6,14},{24,16},{26,18},{28,20},{30,22},{1,9},{... | collective-permute-start | bytes 2506760 | tf_op jit(solution)/shard_map/ppermute | solution.py:350
  167.4 37.6 %collective-permute-start.25 = (f32[2,17,56,128]{3,2,1,0:T(8,128)S(1)}, f32[2,17,56,128]{3,2,1,0:T(8,128)S(1)}, u32[]{:S(2)}, u32[]{:S(2)}) collective-permute-start(f32[2,17,56,128]{3,2,1,0:T(8,128)S(1)} %get-tuple-element.159), channel_id=1, source_target_pairs={{8,16},{10,18},{12,20},{14,22},{16,8},{18,10},{20,12},{22,14},{9,1... | collective-permute-start | bytes 2924552 | tf_op jit(solution)/shard_map/ppermute | solution.py:350
  185.3 42.5 %collective-permute-start.23 = (f32[17,136,128]{2,1,0:T(8,128)S(1)}, f32[17,136,128]{2,1,0:T(8,128)S(1)}, u32[]{:S(2)}, u32[]{:S(2)}) collective-permute-start(f32[17,136,128]{2,1,0:T(8,128)S(1)} %get-tuple-element.157), channel_id=1, source_target_pairs={{0,8},{2,10},{4,12},{6,14},{24,16},{26,18},{28,20},{30,22},{1,9},{... | collective-permute-start | bytes 3551240 | tf_op jit(solution)/shard_map/ppermute | solution.py:350
  187.0 37.4 %collective-permute-start.33 = (f32[2,17,48,128]{3,2,1,0:T(8,128)S(1)}, f32[2,17,48,128]{3,2,1,0:T(8,128)S(1)}, u32[]{:S(2)}, u32[]{:S(2)}) collective-permute-start(f32[2,17,48,128]{3,2,1,0:T(8,128)S(1)} %get-tuple-element.175), channel_id=1, source_target_pairs={{8,16},{10,18},{12,20},{14,22},{16,8},{18,10},{20,12},{22,14},{9,1... | collective-permute-start | bytes 2506760 | tf_op jit(solution)/shard_map/ppermute | solution.py:350
  187.8 36.6 %collective-permute-start.24 = (f32[2,17,32,128]{3,2,1,0:T(8,128)S(1)}, f32[2,17,32,128]{3,2,1,0:T(8,128)S(1)}, u32[]{:S(2)}, u32[]{:S(2)}) collective-permute-start(f32[2,17,32,128]{3,2,1,0:T(8,128)S(1)} %get-tuple-element.158.refs_0_), channel_id=1, source_target_pairs={{0,8},{2,10},{4,12},{6,14},{24,16},{26,18},{28,20},{30,22},{1,9},{... | collective-permute-start | bytes 1671176 | tf_op jit(solution)/shard_map/ppermute | solution.py:350
  205.1 24.1 %collective-permute-start.35 = (f32[17,56,128]{2,1,0:T(8,128)S(1)}, f32[17,56,128]{2,1,0:T(8,128)S(1)}, u32[]{:S(2)}, u32[]{:S(2)}) collective-permute-start(f32[17,56,128]{2,1,0:T(8,128)S(1)} %get-tuple-element.178), channel_id=1, source_target_pairs={{8,0},{10,2},{12,4},{14,6},{16,24},{18,26},{20,28},{22,30},{9,1},{... | collective-permute-start | bytes 1462280 | tf_op jit(solution)/shard_map/ppermute | solution.py:350
  225.9 23.5 %collective-permute-start.32 = (f32[17,32,128]{2,1,0:T(8,128)S(1)}, f32[17,32,128]{2,1,0:T(8,128)S(1)}, u32[]{:S(2)}, u32[]{:S(2)}) collective-permute-start(f32[17,32,128]{2,1,0:T(8,128)S(1)} %get-tuple-element.152.refs_0_), channel_id=1, source_target_pairs={{8,0},{10,2},{12,4},{14,6},{16,24},{18,26},{20,28},{22,30},{9,1},{... | collective-permute-start | bytes 835592 | tf_op jit(solution)/shard_map/ppermute | solution.py:350
  227.2 22.2 %collective-permute-start.30 = (f32[17,32,128]{2,1,0:T(8,128)S(1)}, f32[17,32,128]{2,1,0:T(8,128)S(1)}, u32[]{:S(2)}, u32[]{:S(2)}) collective-permute-start(f32[17,32,128]{2,1,0:T(8,128)S(1)} %get-tuple-element.172), channel_id=1, source_target_pairs={{8,16},{10,18},{12,20},{14,22},{16,8},{18,10},{20,12},{22,14},{9,1... | collective-permute-start | bytes 835592 | tf_op jit(solution)/shard_map/ppermute | solution.py:350
  (13 other events, 174.6 us)

commit v3 on v2

--- a/solution.py
+++ b/solution.py
@@ -16,20 +16,20 @@
 STATS = HARM + 1
 PLANES = 4
 
-ROUND = 3
-PARTS = (7, 5, 7, 6, 4)
-GROUPS = (("s", (0,)), ("s", (1,)), ("s", (2,)), ("s", (3,)), ("e", (4,)))
-NEARS = ((0, 1), (2, 3, 4))
-PAIRS = ((0,), (1, 2, 3, 4))
+ROUND = 4
+PARTS = (6, 5, 4, 5, 4, 4)
+GROUPS = (("s", (0, 1, 2)), ("s", (3, 4)), ("s", (5,)))
+NEARS = ((2, 3, 4), (5,))
+PAIRS = ((0, 1, 2, 3, 4, 5),)
 ORDER = " ".join((
     "p0 P0 q0 p1",
-    "q1 p2 p3 p4",
-    "t0 T0 t1 n0",
-    "m0 m1 t2 r0",
-    "r1 f0 t3 m2",
-    "f1 t4 n1 m3",
-    "F0 r2 m4 r3",
-    "f2 f3 f4",
+    "p2 p3 t0 S0",
+    "p4 p5 t1 m0",
+    "t2 R0 m1 t3",
+    "T0 m2 t4 m3",
+    "r0 t5 m4 n0",
+    "n1 F0 m5 r1",
+    "r2 f0 f1 f2",
 )).split()
 FINAL_ROWS = 8
 VMEM_LIMIT = 8 << 20
@@ -121,13 +121,13 @@
         body(block * size, size)
 
 
-def totals_kernel(offset, where_ref, weight_ref, own_ref, r1_ref, r2_ref, r3_ref, *rest):
-    home_ref, near_ref, far_ref = rest[-4:-1]
+def totals_kernel(offset, split, where_ref, weight_ref, own_ref, r1_ref, r2_ref, r3_ref, *rest):
+    home_ref, near_ref, far_ref = rest[-4:-1] if split else (rest[-3], None, rest[-2])
     held, rows = own_ref.shape[1:3]
     first = (where_ref[0] % 2) * held
     second = held - first
     for step in range(PLANES):
-        out_ref = (home_ref, near_ref, far_ref.at[0], far_ref.at[1])[step]
+        out_ref = (home_ref, near_ref if near_ref is not None else far_ref.at[2], far_ref.at[0], far_ref.at[1])[step]
 
         def body(start, size):
             at, at1 = pl.ds(pl.multiple_of(start, 8), size), pl.ds(pl.multiple_of(start + offset, 8), size)
@@ -147,25 +147,48 @@
         row_blocks(rows, body)
 
 
-def round_kernel(where_ref, weight_ref, *rest):
-    sources, outs = rest[:PLANES], rest[-5:-1]
-    held, rows = sources[0].shape[:2]
+def round_sums_kernel(where_ref, weight_ref, own_ref, in_ref, *rest):
+    home_ref, near_ref, far_ref = rest[-4:-1]
+    held, rows = own_ref.shape[1:3]
+    width = 128
+    for step in range(PLANES):
+        out_ref = (home_ref, near_ref, far_ref.at[0], far_ref.at[1])[step]
+        for part in range(own_ref.shape[3] // width):
+            columns = slice(part * width, (part + 1) * width)
+
+            def body(start, size):
+                at = pl.ds(pl.multiple_of(start, 8), size)
+                values = [[own_ref[step, k, at, columns] for k in range(held)]]
+                if step > 0:
+                    values.append([in_ref[step - 1, k, at, columns] for k in range(held)])
+                for k in range(held):
+                    out_ref[k, at, columns] = values[0][k] + values[1][k] if step > 0 else values[0][k]
+
+                def emit(row, value):
+                    out_ref[held + row, at, columns] = value
+
+                sums(values, weight_ref, 1, emit)
+
+            row_blocks(rows, body)
+
+
+def round_relay_kernel(home_ref, b_ref, *rest):
+    rest[-2][...] = home_ref[...] + b_ref[1]
+
+
+def round_split_kernel(where_ref, home_ref, near_ref, b_ref, c_ref, *rest):
+    outs = rest[-5:-1]
     width = outs[0].shape[-1]
     for shift, out_ref in enumerate(outs):
         column = pl.ds(pl.multiple_of((where_ref[0] ^ shift) * width, width), width)
 
-        def body(start, size):
-            at = pl.ds(pl.multiple_of(start, 8), size)
-            values = [[ref[k, at, column] for k in range(held)] for ref in sources]
-            for k in range(held):
-                out_ref[k, at] = (values[0][k] + values[1][k]) + (values[2][k] + values[3][k])
-
-            def emit(row, value):
-                out_ref[held + row, at] = value
-
-            sums(values, weight_ref, 1, emit)
-
-        row_blocks(rows, body)
+        @pl.when(where_ref[1] > 0)
+        def _():
+            out_ref[...] = near_ref[:, :, column] + b_ref[0, :, :, column]
+
+        @pl.when(where_ref[1] == 0)
+        def _():
+            out_ref[...] = home_ref[:, :, column] + c_ref[:, :, column]
 
 
 def join_kernel(count, *refs):
@@ -176,21 +199,18 @@
         start += rows
 
 
-def merge_kernel(count, straight, *refs):
-    outs, start = refs[-3:-1] if straight else refs[-2:-1], 0
-    for own_ref, in_ref in zip(refs[:count], refs[count : 2 * count]):
-        rows = own_ref.shape[2]
-        for hop in range(2):
-            out_ref = outs[hop] if straight else outs[0].at[hop]
-            out_ref[:, start : start + rows] = own_ref[hop] + in_ref[hop]
-        start += rows
-
-
-def relay_kernel(count, b_ref, *refs):
+def merge_kernel(straight, own_ref, in_ref, *rest):
+    outs = rest[-3:-1] if straight else rest[-2:-1]
+    for hop in range(2):
+        out_ref = outs[hop] if straight else outs[0].at[hop]
+        out_ref[...] = own_ref[hop] + in_ref[hop]
+
+
+def relay_kernel(count, *refs):
     out_ref, start = refs[-2], 0
-    for ref in refs[:count]:
-        rows = ref.shape[1]
-        out_ref[:, start : start + rows] = ref[...] + b_ref[1, :, start : start + rows]
+    for home_ref, b_ref in zip(refs[:count], refs[count : 2 * count]):
+        rows = home_ref.shape[1]
+        out_ref[:, start : start + rows] = home_ref[...] + b_ref[1]
         start += rows
 
 
@@ -236,17 +256,18 @@
     coeff_out, var_out, _, coeff_ref, var_ref, sem = refs[-6:]
     count = len(chunks)
     homes, owns, nears = refs[:count], refs[count : 2 * count], refs[2 * count : 3 * count]
-    one_ref, two_ref = refs[3 * count : 3 * count + 2]
+    middles, two_ref = refs[3 * count : 4 * count], refs[4 * count]
 
     @pl.when(where_ref[1] > 0)
     def _():
         start = 0
-        for (rows, place), own_ref, in_ref in zip(chunks, owns, nears):
-
-            def load(row, at, start=start, place=place, own_ref=own_ref, in_ref=in_ref):
-                middle = one_ref if mode == "e" else one_ref.at[0]
-                value = own_ref[row, pl.ds(at, FINAL_ROWS)] + in_ref[row, pl.ds(pl.multiple_of(at + place, 8), FINAL_ROWS)]
-                return value + middle[row, pl.ds(pl.multiple_of(at + start, 8), FINAL_ROWS)]
+        for (rows, place), own_ref, in_ref, b_ref in zip(chunks, owns, nears, middles):
+
+            def load(row, at, place=place, own_ref=own_ref, in_ref=in_ref, b_ref=b_ref):
+                middle = b_ref if mode == "e" else b_ref.at[0]
+                own_part, in_part = (ref if len(ref.shape) == 3 else ref.at[2] for ref in (own_ref, in_ref))
+                value = own_part[row, pl.ds(at, FINAL_ROWS)] + in_part[row, pl.ds(pl.multiple_of(at + place, 8), FINAL_ROWS)]
+                return value + middle[row, pl.ds(at, FINAL_ROWS)]
 
             solve(matrices, coeff_ref, var_ref, start, rows, load)
             start += rows
@@ -259,7 +280,7 @@
             def load(row, at, start=start, home_ref=home_ref):
                 value = home_ref[row, pl.ds(at, FINAL_ROWS)] + two_ref[row, pl.ds(pl.multiple_of(at + start, 8), FINAL_ROWS)]
                 if mode == "e":
-                    value = value + refs[3 * count + 2][row, pl.ds(at, FINAL_ROWS)]
+                    value = value + refs[4 * count + 1][row, pl.ds(at, FINAL_ROWS)]
                 return value
 
             solve(matrices, coeff_ref, var_ref, start, rows, load)
@@ -354,7 +375,6 @@
     firsts = [(ROUND + sum(PARTS[:chunk])) * unit for chunk in range(len(PARTS))]
     turn = ROUND * unit
     swaps = [[(i, i ^ shift) for i in range(groups)] for shift in range(plane)]
-    hops = [[(i, i ^ (step * plane)) for i in range(groups)] for step in range(PLANES)]
     to_inner = [(i, i + plane) for i in range(plane)] + [(i, i - plane) for i in range(groups - plane, groups)]
     to_outer = [(b, a) for a, b in to_inner]
     middle = [(i, i + plane) for i in range(plane, 2 * plane)]
@@ -394,15 +414,32 @@
         kind, at = item[0], int(item[1:])
         if kind == "P":
             parts = fetch(
-                [near(held, turn, plane * width)] * PLANES,
-                lambda w: [(step, 0, 0, turn, None, (w[3] ^ step) * plane * width) for step in (3, 2, 1, 0)], turn,
-            )
-            around = [move(parts[step], hops[step]) for step in (3, 2, 1)]
-            around = parts[:1] + around[::-1]
+                [near(PLANES, held, turn, plane * width), near(PLANES - 1, held, turn, plane * width)],
+                lambda w: [
+                    (out, 0, 0, turn, step - out, column(w, step, w[0]))
+                    for out, steps in ((1, (1, 2, 3)), (0, range(PLANES)))
+                    for step in steps
+                ],
+                turn,
+            )
+            around = [parts[0], move(parts[1], to_inner)]
+        elif kind == "S":
+            parts = call(
+                round_sums_kernel, turn * lon * 40, turn * lon * held * 8,
+                [smem, smem, vmem, vmem], [where, weights, *around],
+                [near(held + SLOW + 1, turn, plane * width)] * 2 + [near(2, held + SLOW + 1, turn, plane * width)],
+            )
+            around = [parts[0], parts[1], move(parts[2], middle)]
+        elif kind == "R":
+            (part,) = call(
+                round_relay_kernel, turn * lon, turn * lon * 12,
+                [vmem, vmem], [around[0], around[2]], [near(held + SLOW + 1, turn, plane * width)],
+            )
+            around.append(move(part, to_outer))
         elif kind == "T":
             parts = call(
-                round_kernel, turn * lon * 60, turn * lon * held * 4,
-                [smem, smem] + [vmem] * PLANES, [where, weights, *around],
+                round_split_kernel, turn * lon, turn * lon * 12,
+                [smem] + [vmem] * 4, [where, *around],
                 [near(held + SLOW + 1, turn, width)] * plane,
             )
             around = parts[:1] + [move(parts[shift], swaps[shift]) for shift in range(1, plane)]
@@ -434,12 +471,16 @@
             rows = sizes[at]
             mode = next(mode for mode, chunks in GROUPS if at in chunks)
             part, offset = paired[at]
-            home[at], own[at], far[at] = call(
-                functools.partial(totals_kernel, offset), rows * width * PLANES * 240, rows * width * 656,
+            split = any(at in chunks for chunks in NEARS)
+            results = call(
+                functools.partial(totals_kernel, offset, split), rows * width * PLANES * 240, rows * width * 656,
                 [smem, smem] + [vmem] * plane, [where, weights, packed[at][0], part, *packed[at][1:]],
-                [near(STATS, rows, width)] * 2 + [near(2, STATS, rows, width)],
-            )
+                [near(STATS, rows, width)] * (2 if split else 1) + [near(2 if split else 3, STATS, rows, width)],
+            )
+            home[at], own[at], far[at] = results[0], results[-2] if split else results[-1], results[-1]
             moved["a", at] = move(far[at], to_inner)
+            if not split:
+                moved["n", at] = (moved["a", at], 0)
             if mode == "e":
                 moved["h", at] = move(home[at], to_outer)
         elif kind == "n":
@@ -453,13 +494,12 @@
             for chunk in chunks:
                 moved["n", chunk] = (part, sum(sizes[other] for other in chunks if other < chunk))
         elif kind == "m":
-            mode, chunks = GROUPS[at]
-            rows = sum(sizes[chunk] for chunk in chunks)
-            shapes = [near(STATS, rows, width)] * 2 if mode == "e" else [near(2, STATS, rows, width)]
-            args = [far[chunk] for chunk in chunks] + [moved["a", chunk] for chunk in chunks]
+            rows = sizes[at]
+            mode = next(mode for mode, chunks in GROUPS if at in chunks)
             parts = call(
-                functools.partial(merge_kernel, len(chunks), mode == "e"), rows * width * 34, rows * width * 408,
-                [vmem] * len(args), args, shapes,
+                functools.partial(merge_kernel, mode == "e"), rows * width * 34, rows * width * 408,
+                [vmem] * 2, [far[at], moved["a", at]],
+                [near(STATS, rows, width)] * 2 if mode == "e" else [near(2, STATS, rows, width)],
             )
             moved["b", at] = move(parts[0], middle)
             if mode == "e":
@@ -467,18 +507,18 @@
         elif kind == "r":
             chunks = GROUPS[at][1]
             rows = sum(sizes[chunk] for chunk in chunks)
+            args = [home[chunk] for chunk in chunks] + [moved["b", chunk] for chunk in chunks]
             (part,) = call(
                 functools.partial(relay_kernel, len(chunks)), rows * width * 17, rows * width * 204,
-                [vmem] * (1 + len(chunks)), [moved["b", at]] + [home[chunk] for chunk in chunks],
-                [near(STATS, rows, width)],
+                [vmem] * len(args), args, [near(STATS, rows, width)],
             )
             moved["c", at] = move(part, to_outer)
         else:
             mode, chunks = GROUPS[at]
             rows = sum(sizes[chunk] for chunk in chunks)
             args = [home[chunk] for chunk in chunks] + [own[chunk] for chunk in chunks]
-            args += [moved["n", chunk][0] for chunk in chunks] + [moved["b", at]]
-            args += [moved["g", at], moved["h", chunks[0]]] if mode == "e" else [moved["c", at]]
+            args += [moved["n", chunk][0] for chunk in chunks] + [moved["b", chunk] for chunk in chunks]
+            args += [moved["g", chunks[0]], moved["h", chunks[0]]] if mode == "e" else [moved["c", at]]
             places = [(sizes[chunk], moved["n", chunk][1]) for chunk in chunks]
             kernel = functools.partial(final_kernel, firsts[chunks[0]], places, mode, matrices)
             outs = finish(kernel, rows, args, outs)

time: 252 us -> 219 us (0.87)
  waiting for transfers between devices: 147 us -> 114 us
    ppermute x36, waiting for transfers between devices: 147 us -> 114 us  [move(): return lax.ppermute(value, 'io', pairs)]
    pallas_call x31 -> x32, Pallas kernels: 38.1 us -> 37.8 us  [call(): pl.pallas_call(kernel, in_specs=ins, out_specs=(out_specs or [vmem] * len...]
  transfers between devices with their start and end apart: 36 -> 36, of which waited for: 16 -> 16; matrix products, arithmetic and copies ran while one was open for 0% -> 0% of each run, Pallas kernels for 11% -> 13%
where the time goes in v3:
time: 219 us; the launch traced here: 218 us
  waiting for transfers between devices  114 us (52%)
  starting transfers between devices  63.9 us (29%)
  Pallas kernels  37.8 us (17%)
    ppermute x36, waiting for transfers between devices, move(): return lax.ppermute(value, 'io', pairs)  114 us
    ppermute x36, starting transfers between devices, move(): return lax.ppermute(value, 'io', pairs)  63.9 us
    pallas_call x32, Pallas kernels, call(): pl.pallas_call(kernel, in_specs=ins, out_specs=(out_specs or [vmem] * len...  37.8 us
  transfers between devices with their start and end apart: 36, of which 16 were waited for; matrix products, arithmetic and copies ran while one was open for 0% of the time, Pallas kernels for 13%

profile of v3, /device:TPU:0, one launch (start us, length us, event | category | flops | bytes accessed | tf_op | source)
XLA Modules:
  0.0 217.9 jit_solution(16182302938677427900)
XLA Ops:
  2.0 2.1 shard_map.41
  4.1 2.3 %shard_map.42 = (f32[4,6,32,512]{3,2,1,0:T(8,128)S(1)}, f32[3,6,32,512]{3,2,1,0:T(8,128)S(1)}, f32[8,128]{1,0:T(8,128)}) custom-call(s32[4]{0:T(128)S(1)} %pad_add_fusion.where_ref, f32[6,256,2048]{2,1,0:T(8,128)} %bitcast.8, f32[8,128]{1,0:T(8,128)} %get-tuple-element.97.rest_0_), custom_call_target="tpu_custom_call" | custom-call | flops 65536 | bytes 3145728 | tf_op jit(solution)/shard_map/pallas_call | solution.py:358
  6.4 2.3 %shard_map.43 = (f32[4,6,224,128]{3,2,1,0:T(8,128)S(1)}, f32[8,128]{1,0:T(8,128)}) custom-call(s32[4]{0:T(128)S(1)} %pad_add_fusion.where_ref, f32[6,256,2048]{2,1,0:T(8,128)} %bitcast.9, f32[8,128]{1,0:T(8,128)} %get-tuple-element.101.rest_0_), custom_call_target="tpu_custom_call" | custom-call | flops 458752 | bytes 22020096 | tf_op jit(solution)/shard_map/pallas_call | solution.py:358
  9.3 4.6 %collective-permute-start = (f32[3,6,32,512]{3,2,1,0:T(8,128)S(1)}, f32[3,6,32,512]{3,2,1,0:T(8,128)S(1)}, u32[]{:S(2)}, u32[]{:S(2)}) collective-permute-start(f32[3,6,32,512]{3,2,1,0:T(8,128)S(1)} %get-tuple-element.99), channel_id=1, source_target_pairs={{0,8},{2,10},{4,12},{6,14},{24,16},{26,18},{28,20},{30,22},{1,9},{... | collective-permute-start | bytes 3538952 | tf_op jit(solution)/shard_map/ppermute | solution.py:371
  21.5 8.7 %collective-permute-done.2.r2_ref = f32[4,6,48,128]{3,2,1,0:T(8,128)S(1)} collective-permute-done((f32[4,6,48,128]{3,2,1,0:T(8,128)S(1)}, f32[4,6,48,128]{3,2,1,0:T(8,128)S(1)}, u32[]{:S(2)}, u32[]{:S(2)}) %collective-permute-start.2) | collective-permute-done | bytes 589856 | tf_op jit(solution)/shard_map/ppermute | solution.py:371
  30.2 11.1 %collective-permute-done.3.r3_ref = f32[4,6,48,128]{3,2,1,0:T(8,128)S(1)} collective-permute-done((f32[4,6,48,128]{3,2,1,0:T(8,128)S(1)}, f32[4,6,48,128]{3,2,1,0:T(8,128)S(1)}, u32[]{:S(2)}, u32[]{:S(2)}) %collective-permute-start.3) | collective-permute-done | bytes 589856 | tf_op jit(solution)/shard_map/ppermute | solution.py:371
  45.8 4.6 %collective-permute-start.10 = (f32[3,17,48,128]{3,2,1,0:T(8,128)S(1)}, f32[3,17,48,128]{3,2,1,0:T(8,128)S(1)}, u32[]{:S(2)}, u32[]{:S(2)}) collective-permute-start(f32[3,17,48,128]{3,2,1,0:T(8,128)S(1)} %get-tuple-element.124.own_ref.refs_3_), channel_id=1, source_target_pairs={{0,8},{2,10},{4,12},{6,14},{24,16},{26,18},{28,20},{30,22},{1,9},{... | collective-permute-start | bytes 3760136 | tf_op jit(solution)/shard_map/ppermute | solution.py:371
  55.8 8.8 %collective-permute-done.6.r2_ref = f32[4,6,40,128]{3,2,1,0:T(8,128)S(1)} collective-permute-done((f32[4,6,40,128]{3,2,1,0:T(8,128)S(1)}, f32[4,6,40,128]{3,2,1,0:T(8,128)S(1)}, u32[]{:S(2)}, u32[]{:S(2)}) %collective-permute-start.6) | collective-permute-done | bytes 491552 | tf_op jit(solution)/shard_map/ppermute | solution.py:371
  64.5 8.7 %collective-permute-done.7.r3_ref = f32[4,6,40,128]{3,2,1,0:T(8,128)S(1)} collective-permute-done((f32[4,6,40,128]{3,2,1,0:T(8,128)S(1)}, f32[4,6,40,128]{3,2,1,0:T(8,128)S(1)}, u32[]{:S(2)}, u32[]{:S(2)}) %collective-permute-start.7) | collective-permute-done | bytes 491552 | tf_op jit(solution)/shard_map/ppermute | solution.py:371
  78.6 10.2 %collective-permute-done.8.r2_ref = f32[4,6,32,128]{3,2,1,0:T(8,128)S(1)} collective-permute-done((f32[4,6,32,128]{3,2,1,0:T(8,128)S(1)}, f32[4,6,32,128]{3,2,1,0:T(8,128)S(1)}, u32[]{:S(2)}, u32[]{:S(2)}) %collective-permute-start.8) | collective-permute-done | bytes 393248 | tf_op jit(solution)/shard_map/ppermute | solution.py:371
  90.4 5.8 %collective-permute-done.9.r3_ref = f32[4,6,32,128]{3,2,1,0:T(8,128)S(1)} collective-permute-done((f32[4,6,32,128]{3,2,1,0:T(8,128)S(1)}, f32[4,6,32,128]{3,2,1,0:T(8,128)S(1)}, u32[]{:S(2)}, u32[]{:S(2)}) %collective-permute-start.9) | collective-permute-done | bytes 393248 | tf_op jit(solution)/shard_map/ppermute | solution.py:371
  99.0 4.6 %collective-permute-start.15 = (f32[2,17,32,128]{3,2,1,0:T(8,128)S(1)}, f32[2,17,32,128]{3,2,1,0:T(8,128)S(1)}, u32[]{:S(2)}, u32[]{:S(2)}) collective-permute-start(f32[2,17,32,128]{3,2,1,0:T(8,128)S(1)} %get-tuple-element.135.own_ref), channel_id=1, source_target_pairs={{0,8},{2,10},{4,12},{6,14},{24,16},{26,18},{28,20},{30,22},{1,9},{... | collective-permute-start | bytes 1671176 | tf_op jit(solution)/shard_map/ppermute | solution.py:371
  104.4 3.3 %collective-permute-done.17.r2_ref = f32[4,6,40,128]{3,2,1,0:T(8,128)S(1)} collective-permute-done((f32[4,6,40,128]{3,2,1,0:T(8,128)S(1)}, f32[4,6,40,128]{3,2,1,0:T(8,128)S(1)}, u32[]{:S(2)}, u32[]{:S(2)}) %collective-permute-start.17) | collective-permute-done | bytes 491552 | tf_op jit(solution)/shard_map/ppermute | solution.py:371
  107.8 9.6 %collective-permute-done.18.r3_ref = f32[4,6,40,128]{3,2,1,0:T(8,128)S(1)} collective-permute-done((f32[4,6,40,128]{3,2,1,0:T(8,128)S(1)}, f32[4,6,40,128]{3,2,1,0:T(8,128)S(1)}, u32[]{:S(2)}, u32[]{:S(2)}) %collective-permute-start.18) | collective-permute-done | bytes 491552 | tf_op jit(solution)/shard_map/ppermute | solution.py:371
  124.0 8.9 %collective-permute-done.21.r2_ref = f32[4,6,32,128]{3,2,1,0:T(8,128)S(1)} collective-permute-done((f32[4,6,32,128]{3,2,1,0:T(8,128)S(1)}, f32[4,6,32,128]{3,2,1,0:T(8,128)S(1)}, u32[]{:S(2)}, u32[]{:S(2)}) %collective-permute-start.21) | collective-permute-done | bytes 393248 | tf_op jit(solution)/shard_map/ppermute | solution.py:371
  133.6 6.0 %collective-permute-done.22.r3_ref = f32[4,6,32,128]{3,2,1,0:T(8,128)S(1)} collective-permute-done((f32[4,6,32,128]{3,2,1,0:T(8,128)S(1)}, f32[4,6,32,128]{3,2,1,0:T(8,128)S(1)}, u32[]{:S(2)}, u32[]{:S(2)}) %collective-permute-start.22) | collective-permute-done | bytes 393248 | tf_op jit(solution)/shard_map/ppermute | solution.py:371
  145.0 6.5 %collective-permute-done.4.r2_ref = f32[4,6,32,128]{3,2,1,0:T(8,128)S(1)} collective-permute-done((f32[4,6,32,128]{3,2,1,0:T(8,128)S(1)}, f32[4,6,32,128]{3,2,1,0:T(8,128)S(1)}, u32[]{:S(2)}, u32[]{:S(2)}) %collective-permute-start.4) | collective-permute-done | bytes 393248 | tf_op jit(solution)/shard_map/ppermute | solution.py:371
  151.6 7.9 %collective-permute-done.5.r3_ref = f32[4,6,32,128]{3,2,1,0:T(8,128)S(1)} collective-permute-done((f32[4,6,32,128]{3,2,1,0:T(8,128)S(1)}, f32[4,6,32,128]{3,2,1,0:T(8,128)S(1)}, u32[]{:S(2)}, u32[]{:S(2)}) %collective-permute-start.5) | collective-permute-done | bytes 393248 | tf_op jit(solution)/shard_map/ppermute | solution.py:371
  166.2 4.8 %collective-permute-done.27.refs_2_ = f32[11,32,128]{2,1,0:T(8,128)S(1)} collective-permute-done((f32[11,32,128]{2,1,0:T(8,128)S(1)}, f32[11,32,128]{2,1,0:T(8,128)S(1)}, u32[]{:S(2)}, u32[]{:S(2)}) %collective-permute-start.27) | collective-permute-done | bytes 180256 | tf_op jit(solution)/shard_map/ppermute | solution.py:371
  173.7 4.7 %collective-permute-start.33 = (f32[17,104,128]{2,1,0:T(8,128)S(1)}, f32[17,104,128]{2,1,0:T(8,128)S(1)}, u32[]{:S(2)}, u32[]{:S(2)}) collective-permute-start(f32[17,104,128]{2,1,0:T(8,128)S(1)} %get-tuple-element.178), channel_id=1, source_target_pairs={{0,8},{2,10},{4,12},{6,14},{24,16},{26,18},{28,20},{30,22},{1,9},{... | collective-permute-start | bytes 2715656 | tf_op jit(solution)/shard_map/ppermute | solution.py:371
  182.3 15.3 %collective-permute-start.24 = (f32[17,32,128]{2,1,0:T(8,128)S(1)}, f32[17,32,128]{2,1,0:T(8,128)S(1)}, u32[]{:S(2)}, u32[]{:S(2)}) collective-permute-start(f32[17,32,128]{2,1,0:T(8,128)S(1)} %get-tuple-element.162), channel_id=1, source_target_pairs={{0,8},{2,10},{4,12},{6,14},{24,16},{26,18},{28,20},{30,22},{1,9},{... | collective-permute-start | bytes 835592 | tf_op jit(solution)/shard_map/ppermute | solution.py:371
  199.0 2.9 %shard_map.70 = (f32[16,256,128]{2,1,0:T(8,128)}, f32[256,128]{1,0:T(8,128)}, f32[8,128]{1,0:T(8,128)}) custom-call(s32[4]{0:T(128)S(1)} %pad_add_fusion.where_ref, f32[17,48,128]{2,1,0:T(8,128)S(1)} %get-tuple-element.115.refs_0_, f32[17,40,128]{2,1,0:T(8,128)S(1)} %get-tuple-element.120.refs_1_, ...), custom_call_target="tpu_custom_call", output_to_operand_aliasing={{0}: (14, {}), {1}: (15, {})} | custom-call | flops 12779520 | bytes 4177920 | tf_op jit(solution)/shard_map/pallas_call | solution.py:358
  202.0 10.2 %collective-permute-done.34.refs_8_ = f32[17,72,128]{2,1,0:T(8,128)S(1)} collective-permute-done((f32[17,72,128]{2,1,0:T(8,128)S(1)}, f32[17,72,128]{2,1,0:T(8,128)S(1)}, u32[]{:S(2)}, u32[]{:S(2)}) %collective-permute-start.34) | collective-permute-done | bytes 626720 | tf_op jit(solution)/shard_map/ppermute | solution.py:371
  212.2 2.2 %shard_map.71 = (f32[16,256,128]{2,1,0:T(8,128)}, f32[256,128]{1,0:T(8,128)}, f32[8,128]{1,0:T(8,128)}) custom-call(s32[4]{0:T(128)S(1)} %pad_add_fusion.where_ref, f32[17,40,128]{2,1,0:T(8,128)S(1)} %get-tuple-element.171.refs_0_, f32[17,32,128]{2,1,0:T(8,128)S(1)} %get-tuple-element.172.refs_1_, ...), custom_call_target="tpu_custom_call", output_to_operand_aliasing={{0}: (10, {}), {1}: (11, {})} | custom-call | flops 7667712 | bytes 2506752 | tf_op jit(solution)/shard_map/pallas_call | solution.py:358
  (84 shorter events, 60.7 us)
Async XLA Ops:
  8.8 32.5 %collective-permute-start.1 = (f32[4,6,224,128]{3,2,1,0:T(8,128)S(1)}, f32[4,6,224,128]{3,2,1,0:T(8,128)S(1)}, u32[]{:S(2)}, u32[]{:S(2)}) collective-permute-start(f32[4,6,224,128]{3,2,1,0:T(8,128)S(1)} %get-tuple-element.102), channel_id=1, source_target_pairs={{0,2},{2,0},{4,6},{6,4},{8,10},{10,8},{12,14},{14,12},{16,18},{18,... | collective-permute-start | bytes 8257544 | tf_op jit(solution)/shard_map/ppermute | solution.py:371
  9.3 33.7 %collective-permute-start = (f32[3,6,32,512]{3,2,1,0:T(8,128)S(1)}, f32[3,6,32,512]{3,2,1,0:T(8,128)S(1)}, u32[]{:S(2)}, u32[]{:S(2)}) collective-permute-start(f32[3,6,32,512]{3,2,1,0:T(8,128)S(1)} %get-tuple-element.99), channel_id=1, source_target_pairs={{0,8},{2,10},{4,12},{6,14},{24,16},{26,18},{28,20},{30,22},{1,9},{... | collective-permute-start | bytes 3538952 | tf_op jit(solution)/shard_map/ppermute | solution.py:371
  15.4 25.8 %collective-permute-start.3 = (f32[4,6,48,128]{3,2,1,0:T(8,128)S(1)}, f32[4,6,48,128]{3,2,1,0:T(8,128)S(1)}, u32[]{:S(2)}, u32[]{:S(2)}) collective-permute-start(f32[4,6,48,128]{3,2,1,0:T(8,128)S(1)} %get-tuple-element.104), channel_id=1, source_target_pairs={{0,6},{2,4},{4,2},{6,0},{8,14},{10,12},{12,10},{14,8},{16,22},{18,... | collective-permute-start | bytes 1769480 | tf_op jit(solution)/shard_map/ppermute | solution.py:371
  45.0 52.6 %collective-permute-start.13 = (f32[2,11,32,512]{3,2,1,0:T(8,128)S(1)}, f32[2,11,32,512]{3,2,1,0:T(8,128)S(1)}, u32[]{:S(2)}, u32[]{:S(2)}) collective-permute-start(f32[2,11,32,512]{3,2,1,0:T(8,128)S(1)} %get-tuple-element.131), channel_id=1, source_target_pairs={{8,16},{10,18},{12,20},{14,22},{16,8},{18,10},{20,12},{22,14},{9,1... | collective-permute-start | bytes 4325384 | tf_op jit(solution)/shard_map/ppermute | solution.py:371
  45.8 44.5 %collective-permute-start.10 = (f32[3,17,48,128]{3,2,1,0:T(8,128)S(1)}, f32[3,17,48,128]{3,2,1,0:T(8,128)S(1)}, u32[]{:S(2)}, u32[]{:S(2)}) collective-permute-start(f32[3,17,48,128]{3,2,1,0:T(8,128)S(1)} %get-tuple-element.124.own_ref.refs_3_), channel_id=1, source_target_pairs={{0,8},{2,10},{4,12},{6,14},{24,16},{26,18},{28,20},{30,22},{1,9},{... | collective-permute-start | bytes 3760136 | tf_op jit(solution)/shard_map/ppermute | solution.py:371
  51.9 21.3 %collective-permute-start.7 = (f32[4,6,40,128]{3,2,1,0:T(8,128)S(1)}, f32[4,6,40,128]{3,2,1,0:T(8,128)S(1)}, u32[]{:S(2)}, u32[]{:S(2)}) collective-permute-start(f32[4,6,40,128]{3,2,1,0:T(8,128)S(1)} %get-tuple-element.118), channel_id=1, source_target_pairs={{0,6},{2,4},{4,2},{6,0},{8,14},{10,12},{12,10},{14,8},{16,22},{18,... | collective-permute-start | bytes 1474568 | tf_op jit(solution)/shard_map/ppermute | solution.py:371
  74.9 28.7 %collective-permute-start.12 = (f32[3,17,40,128]{3,2,1,0:T(8,128)S(1)}, f32[3,17,40,128]{3,2,1,0:T(8,128)S(1)}, u32[]{:S(2)}, u32[]{:S(2)}) collective-permute-start(f32[3,17,40,128]{3,2,1,0:T(8,128)S(1)} %get-tuple-element.129.own_ref.refs_4_), channel_id=1, source_target_pairs={{0,8},{2,10},{4,12},{6,14},{24,16},{26,18},{28,20},{30,22},{1,9},{... | collective-permute-start | bytes 3133448 | tf_op jit(solution)/shard_map/ppermute | solution.py:371
  78.3 17.9 %collective-permute-start.9 = (f32[4,6,32,128]{3,2,1,0:T(8,128)S(1)}, f32[4,6,32,128]{3,2,1,0:T(8,128)S(1)}, u32[]{:S(2)}, u32[]{:S(2)}) collective-permute-start(f32[4,6,32,128]{3,2,1,0:T(8,128)S(1)} %get-tuple-element.123), channel_id=1, source_target_pairs={{0,6},{2,4},{4,2},{6,0},{8,14},{10,12},{12,10},{14,8},{16,22},{18,... | collective-permute-start | bytes 1179656 | tf_op jit(solution)/shard_map/ppermute | solution.py:371
  88.8 19.0 %collective-permute-start.17 = (f32[4,6,40,128]{3,2,1,0:T(8,128)S(1)}, f32[4,6,40,128]{3,2,1,0:T(8,128)S(1)}, u32[]{:S(2)}, u32[]{:S(2)}) collective-permute-start(f32[4,6,40,128]{3,2,1,0:T(8,128)S(1)} %get-tuple-element.139), channel_id=1, source_target_pairs={{0,4},{2,6},{4,0},{6,2},{8,12},{10,14},{12,8},{14,10},{16,20},{18,... | collective-permute-start | bytes 1474568 | tf_op jit(solution)/shard_map/ppermute | solution.py:371
  90.3 27.0 %collective-permute-start.18 = (f32[4,6,40,128]{3,2,1,0:T(8,128)S(1)}, f32[4,6,40,128]{3,2,1,0:T(8,128)S(1)}, u32[]{:S(2)}, u32[]{:S(2)}) collective-permute-start(f32[4,6,40,128]{3,2,1,0:T(8,128)S(1)} %get-tuple-element.140), channel_id=1, source_target_pairs={{0,6},{2,4},{4,2},{6,0},{8,14},{10,12},{12,10},{14,8},{16,22},{18,... | collective-permute-start | bytes 1474568 | tf_op jit(solution)/shard_map/ppermute | solution.py:371
  97.7 24.7 %collective-permute-start.16 = (f32[11,32,512]{2,1,0:T(8,128)S(1)}, f32[11,32,512]{2,1,0:T(8,128)S(1)}, u32[]{:S(2)}, u32[]{:S(2)}) collective-permute-start(f32[11,32,512]{2,1,0:T(8,128)S(1)} %get-tuple-element.137), channel_id=1, source_target_pairs={{8,0},{10,2},{12,4},{14,6},{16,24},{18,26},{20,28},{22,30},{9,1},{... | collective-permute-start | bytes 2162696 | tf_op jit(solution)/shard_map/ppermute | solution.py:371
  99.0 23.4 %collective-permute-start.15 = (f32[2,17,32,128]{3,2,1,0:T(8,128)S(1)}, f32[2,17,32,128]{3,2,1,0:T(8,128)S(1)}, u32[]{:S(2)}, u32[]{:S(2)}) collective-permute-start(f32[2,17,32,128]{3,2,1,0:T(8,128)S(1)} %get-tuple-element.135.own_ref), channel_id=1, source_target_pairs={{0,8},{2,10},{4,12},{6,14},{24,16},{26,18},{28,20},{30,22},{1,9},{... | collective-permute-start | bytes 1671176 | tf_op jit(solution)/shard_map/ppermute | solution.py:371
  103.6 37.4 %collective-permute-start.11 = (f32[2,17,48,128]{3,2,1,0:T(8,128)S(1)}, f32[2,17,48,128]{3,2,1,0:T(8,128)S(1)}, u32[]{:S(2)}, u32[]{:S(2)}) collective-permute-start(f32[2,17,48,128]{3,2,1,0:T(8,128)S(1)} %get-tuple-element.128), channel_id=1, source_target_pairs={{8,16},{10,18},{12,20},{14,22},{16,8},{18,10},{20,12},{22,14},{9,1... | collective-permute-start | bytes 2506760 | tf_op jit(solution)/shard_map/ppermute | solution.py:371
  119.0 24.0 %collective-permute-start.20 = (f32[2,17,40,128]{3,2,1,0:T(8,128)S(1)}, f32[2,17,40,128]{3,2,1,0:T(8,128)S(1)}, u32[]{:S(2)}, u32[]{:S(2)}) collective-permute-start(f32[2,17,40,128]{3,2,1,0:T(8,128)S(1)} %get-tuple-element.145.own_ref), channel_id=1, source_target_pairs={{0,8},{2,10},{4,12},{6,14},{24,16},{26,18},{28,20},{30,22},{1,9},{... | collective-permute-start | bytes 2088968 | tf_op jit(solution)/shard_map/ppermute | solution.py:371
  122.4 22.5 %collective-permute-start.14 = (f32[2,17,40,128]{3,2,1,0:T(8,128)S(1)}, f32[2,17,40,128]{3,2,1,0:T(8,128)S(1)}, u32[]{:S(2)}, u32[]{:S(2)}) collective-permute-start(f32[2,17,40,128]{3,2,1,0:T(8,128)S(1)} %get-tuple-element.134), channel_id=1, source_target_pairs={{8,16},{10,18},{12,20},{14,22},{16,8},{18,10},{20,12},{22,14},{9,1... | collective-permute-start | bytes 2088968 | tf_op jit(solution)/shard_map/ppermute | solution.py:371
  141.1 18.4 %collective-permute-start.5 = (f32[4,6,32,128]{3,2,1,0:T(8,128)S(1)}, f32[4,6,32,128]{3,2,1,0:T(8,128)S(1)}, u32[]{:S(2)}, u32[]{:S(2)}) collective-permute-start(f32[4,6,32,128]{3,2,1,0:T(8,128)S(1)} %get-tuple-element.114), channel_id=1, source_target_pairs={{0,6},{2,4},{4,2},{6,0},{8,14},{10,12},{12,10},{14,8},{16,22},{18,... | collective-permute-start | bytes 1179656 | tf_op jit(solution)/shard_map/ppermute | solution.py:371
  143.0 22.0 %collective-permute-start.23 = (f32[2,17,32,128]{3,2,1,0:T(8,128)S(1)}, f32[2,17,32,128]{3,2,1,0:T(8,128)S(1)}, u32[]{:S(2)}, u32[]{:S(2)}) collective-permute-start(f32[2,17,32,128]{3,2,1,0:T(8,128)S(1)} %get-tuple-element.158.own_ref), channel_id=1, source_target_pairs={{0,8},{2,10},{4,12},{6,14},{24,16},{26,18},{28,20},{30,22},{1,9},{... | collective-permute-start | bytes 1671176 | tf_op jit(solution)/shard_map/ppermute | solution.py:371
  160.8 19.3 %collective-permute-start.25 = (f32[2,17,32,128]{3,2,1,0:T(8,128)S(1)}, f32[2,17,32,128]{3,2,1,0:T(8,128)S(1)}, u32[]{:S(2)}, u32[]{:S(2)}) collective-permute-start(f32[2,17,32,128]{3,2,1,0:T(8,128)S(1)} %get-tuple-element.163.own_ref), channel_id=1, source_target_pairs={{0,8},{2,10},{4,12},{6,14},{24,16},{26,18},{28,20},{30,22},{1,9},{... | collective-permute-start | bytes 1671176 | tf_op jit(solution)/shard_map/ppermute | solution.py:371
  162.7 18.2 %collective-permute-start.30 = (f32[2,17,40,128]{3,2,1,0:T(8,128)S(1)}, f32[2,17,40,128]{3,2,1,0:T(8,128)S(1)}, u32[]{:S(2)}, u32[]{:S(2)}) collective-permute-start(f32[2,17,40,128]{3,2,1,0:T(8,128)S(1)} %get-tuple-element.173), channel_id=1, source_target_pairs={{8,16},{10,18},{12,20},{14,22},{16,8},{18,10},{20,12},{22,14},{9,1... | collective-permute-start | bytes 2088968 | tf_op jit(solution)/shard_map/ppermute | solution.py:371
  170.9 28.1 %collective-permute-start.35 = (f32[17,120,128]{2,1,0:T(8,128)S(1)}, f32[17,120,128]{2,1,0:T(8,128)S(1)}, u32[]{:S(2)}, u32[]{:S(2)}) collective-permute-start(f32[17,120,128]{2,1,0:T(8,128)S(1)} %get-tuple-element.180), channel_id=1, source_target_pairs={{8,0},{10,2},{12,4},{14,6},{16,24},{18,26},{20,28},{22,30},{9,1},{... | collective-permute-start | bytes 3133448 | tf_op jit(solution)/shard_map/ppermute | solution.py:371
  173.7 25.3 %collective-permute-start.33 = (f32[17,104,128]{2,1,0:T(8,128)S(1)}, f32[17,104,128]{2,1,0:T(8,128)S(1)}, u32[]{:S(2)}, u32[]{:S(2)}) collective-permute-start(f32[17,104,128]{2,1,0:T(8,128)S(1)} %get-tuple-element.178), channel_id=1, source_target_pairs={{0,8},{2,10},{4,12},{6,14},{24,16},{26,18},{28,20},{30,22},{1,9},{... | collective-permute-start | bytes 2715656 | tf_op jit(solution)/shard_map/ppermute | solution.py:371
  181.0 31.2 %collective-permute-start.34 = (f32[17,72,128]{2,1,0:T(8,128)S(1)}, f32[17,72,128]{2,1,0:T(8,128)S(1)}, u32[]{:S(2)}, u32[]{:S(2)}) collective-permute-start(f32[17,72,128]{2,1,0:T(8,128)S(1)} %get-tuple-element.179), channel_id=1, source_target_pairs={{8,0},{10,2},{12,4},{14,6},{16,24},{18,26},{20,28},{22,30},{9,1},{... | collective-permute-start | bytes 1880072 | tf_op jit(solution)/shard_map/ppermute | solution.py:371
  182.3 32.1 %collective-permute-start.24 = (f32[17,32,128]{2,1,0:T(8,128)S(1)}, f32[17,32,128]{2,1,0:T(8,128)S(1)}, u32[]{:S(2)}, u32[]{:S(2)}) collective-permute-start(f32[17,32,128]{2,1,0:T(8,128)S(1)} %get-tuple-element.162), channel_id=1, source_target_pairs={{0,8},{2,10},{4,12},{6,14},{24,16},{26,18},{28,20},{30,22},{1,9},{... | collective-permute-start | bytes 835592 | tf_op jit(solution)/shard_map/ppermute | solution.py:371
  197.7 18.5 %collective-permute-start.32 = (f32[17,32,128]{2,1,0:T(8,128)S(1)}, f32[17,32,128]{2,1,0:T(8,128)S(1)}, u32[]{:S(2)}, u32[]{:S(2)}) collective-permute-start(f32[17,32,128]{2,1,0:T(8,128)S(1)} %get-tuple-element.177), channel_id=1, source_target_pairs={{8,0},{10,2},{12,4},{14,6},{16,24},{18,26},{20,28},{22,30},{9,1},{... | collective-permute-start | bytes 835592 | tf_op jit(solution)/shard_map/ppermute | solution.py:371
  (13 other events, 168.7 us)

commit v4 on v3

--- a/solution.py
+++ b/solution.py
@@ -17,19 +17,21 @@
 PLANES = 4
 
 ROUND = 4
-PARTS = (6, 5, 4, 5, 4, 4)
-GROUPS = (("s", (0, 1, 2)), ("s", (3, 4)), ("s", (5,)))
-NEARS = ((2, 3, 4), (5,))
-PAIRS = ((0, 1, 2, 3, 4, 5),)
+PARTS = (4, 4, 5, 2, 4, 4, 3, 2)
+GROUPS = (("s", (0, 1, 2)), ("s", (3, 4)), ("s", (5,)), ("s", (6,)), ("s", (7,)))
+NEARS = ((4, 5, 6), (7,))
 ORDER = " ".join((
-    "p0 P0 q0 p1",
-    "p2 p3 t0 S0",
-    "p4 p5 t1 m0",
-    "t2 R0 m1 t3",
-    "T0 m2 t4 m3",
-    "r0 t5 m4 n0",
-    "n1 F0 m5 r1",
-    "r2 f0 f1 f2",
+    "P0 q0 p1 p2",
+    "p3 t0 S0 p4",
+    "t1 p5 m0 p6",
+    "p7 t2 m1 R0",
+    "t3 T0 m2 t4",
+    "m3 t5 r0 m4",
+    "t6 m5 t7 r1",
+    "n0 m6 F0 m7",
+    "r2 f0 n1 r3",
+    "f1 r4 f2 f3",
+    "f4",
 )).split()
 FINAL_ROWS = 8
 VMEM_LIMIT = 8 << 20
@@ -85,9 +87,13 @@
     return fit_block(moved[:, 0, :], jnp.float32(basis), jnp.float32(projector))
 
 
-def fetch_kernel(pieces, where_ref, x_ref, *rest):
-    outs, sem = rest[-1 - pieces(None) - 1 : -2], rest[-1]
+def fetch_kernel(pieces, where_ref, x_ref, table_ref, *rest):
+    count, with_table = pieces(None)
+    outs, sem = rest[-2 - count : -2], rest[-1]
     copies = []
+    if with_table:
+        copies.append(pltpu.make_async_copy(table_ref.at[where_ref[3] * 4 + where_ref[0]], outs[-1], sem))
+        copies[0].start()
     for out, to_rows, first, rows, at, column in pieces(where_ref):
         ref = outs[out] if at is None else outs[out].at[at]
         width = ref.shape[-1]
@@ -337,14 +343,14 @@
             for way, other in enumerate((device ^ shift, device ^ (shift * plane))):
                 rows, columns = way * SLOW, shift * held
                 table[device, rows : rows + SLOW, columns : columns + held] = slow[:, other * held : (other + 1) * held]
-    weights = lax.dynamic_index_in_dim(jnp.asarray(table), me, 0, keepdims=False)
+    table = jnp.asarray(table)
     matrices = fit_matrices()
 
     smem = pl.BlockSpec(memory_space=pltpu.SMEM)
     vmem = pl.BlockSpec(memory_space=pltpu.VMEM)
     hbm = pl.BlockSpec(memory_space=pltpu.HBM)
     space = {id(vmem): pltpu.VMEM, id(hbm): pltpu.HBM}
-    token = [weights]
+    token = []
 
     def near(*dims):
         return pltpu.VMEM(dims, jnp.float32)
@@ -382,14 +388,19 @@
     across = [(i, i + 2 * plane) for i in range(plane, 2 * plane)]
     across = across + [(i, i - 2 * plane) for i in range(2 * plane, 3 * plane)]
 
-    def fetch(outs, pieces, rows):
+    def fetch(outs, pieces, rows, with_table=False):
+        outs = outs + [near(2 * SLOW, plane * held)] * with_table
+
         def count_or_pieces(where_ref):
-            return len(outs) if where_ref is None else pieces(where_ref)
+            return (len(outs), with_table) if where_ref is None else pieces(where_ref)
 
         return call(
             functools.partial(fetch_kernel, count_or_pieces), rows * lon, rows * lon * held * 8,
-            [smem, hbm], [where, view], outs, scratch_shapes=[pltpu.SemaphoreType.DMA],
+            [smem, hbm, hbm], [where, view, table], outs, scratch_shapes=[pltpu.SemaphoreType.DMA],
         )
+
+    def pieces_of(w, out, first, rows, shift):
+        return [(out, 0, first, rows, step, column(w, step, shift)) for step in range(PLANES)]
 
     def column(where_ref, step, shift):
         zone = jnp.where(where_ref[2] > 0, PLANES - 1 - step, step)
@@ -409,20 +420,31 @@
             ],
         )
 
-    packed, paired, home, own, far, moved, outs = {}, {}, {}, {}, {}, {}, []
+    packed, home, own, far, moved, outs = {}, {}, {}, {}, {}, []
     for item in ORDER:
         kind, at = item[0], int(item[1:])
         if kind == "P":
+            first, rows = firsts[0], sizes[0]
             parts = fetch(
-                [near(PLANES, held, turn, plane * width), near(PLANES - 1, held, turn, plane * width)],
-                lambda w: [
-                    (out, 0, 0, turn, step - out, column(w, step, w[0]))
-                    for out, steps in ((1, (1, 2, 3)), (0, range(PLANES)))
-                    for step in steps
-                ],
-                turn,
-            )
-            around = [parts[0], move(parts[1], to_inner)]
+                [near(PLANES - 1, held, turn, plane * width)] + [near(PLANES, held, rows, width)] * 2,
+                lambda w: [(0, 0, 0, turn, step - 1, column(w, step, w[0])) for step in (1, 2, 3)]
+                + pieces_of(w, 1, first, rows, 2) + pieces_of(w, 2, first, rows, 3),
+                turn + rows,
+            )
+            around = [None, move(parts[0], to_inner)]
+            packed[0] = [None, move(parts[1], swaps[2]), move(parts[2], swaps[3])]
+        elif kind == "q":
+            first, rows, own_rows = firsts[0], sum(sizes), sizes[0]
+            parts = fetch(
+                [near(PLANES, held, rows, width), near(PLANES, held, turn, plane * width), near(PLANES, held, own_rows, width)],
+                lambda w: pieces_of(w, 0, first, rows, 1)
+                + [(1, 0, 0, turn, step, column(w, step, w[0])) for step in range(PLANES)]
+                + pieces_of(w, 2, first, own_rows, 0),
+                rows, True,
+            )
+            part = move(parts[0], swaps[1])
+            around[0], packed[0][0], weights = parts[1], parts[2], parts[3]
+            paired = [(part, other - first) for other in firsts]
         elif kind == "S":
             parts = call(
                 round_sums_kernel, turn * lon * 40, turn * lon * held * 8,
@@ -457,16 +479,6 @@
                 rows,
             )
             packed[at] = [parts[0], move(parts[1], swaps[2]), move(parts[2], swaps[3])]
-        elif kind == "q":
-            first, rows = firsts[PAIRS[at][0]], sum(sizes[chunk] for chunk in PAIRS[at])
-            (part,) = fetch(
-                [near(PLANES, held, rows, width)],
-                lambda w, first=first, rows=rows: [(0, 0, first, rows, step, column(w, step, 1)) for step in range(PLANES)],
-                rows,
-            )
-            part = move(part, swaps[1])
-            for chunk in PAIRS[at]:
-                paired[chunk] = (part, firsts[chunk] - first)
         elif kind == "t":
             rows = sizes[at]
             mode = next(mode for mode, chunks in GROUPS if at in chunks)

time: 219 us -> 233 us (1.064)
  starting transfers between devices: 63.9 us -> 77.7 us
  Pallas kernels: 37.8 us -> 42.6 us
  waiting for transfers between devices: 114 us -> 111 us
    ppermute x36 -> x46, starting transfers between devices: 63.9 us -> 77.7 us  [move(): return lax.ppermute(value, 'io', pairs)]
    pallas_call x32 -> x41, Pallas kernels: 37.8 us -> 42.6 us  [call(): pl.pallas_call(kernel, in_specs=ins, out_specs=(out_specs or [vmem] * len...]
    ppermute x36 -> x46, waiting for transfers between devices: 114 us -> 111 us  [move(): return lax.ppermute(value, 'io', pairs)]
  transfers between devices with their start and end apart: 36 -> 46, of which waited for: 16 -> 19; matrix products, arithmetic and copies ran while one was open for 0% -> 0% of each run, Pallas kernels for 13% -> 16%
where the time goes in v4:
time: 233 us; the launch traced here: 232 us
  waiting for transfers between devices  111 us (48%)
  starting transfers between devices  77.7 us (33%)
  Pallas kernels  42.6 us (18%)
    ppermute x46, waiting for transfers between devices, move(): return lax.ppermute(value, 'io', pairs)  111 us
    ppermute x46, starting transfers between devices, move(): return lax.ppermute(value, 'io', pairs)  77.7 us
    pallas_call x41, Pallas kernels, call(): pl.pallas_call(kernel, in_specs=ins, out_specs=(out_specs or [vmem] * len...  42.6 us
  transfers between devices with their start and end apart: 46, of which 19 were waited for; matrix products, arithmetic and copies ran while one was open for 0% of the time, Pallas kernels for 16%

profile of v4, /device:TPU:0, one launch (start us, length us, event | category | flops | bytes accessed | tf_op | source)
XLA Modules:
  0.0 232.2 jit_solution(9676407777995613441)
XLA Ops:
  2.8 2.9 %shard_map.42 = (f32[4,6,224,128]{3,2,1,0:T(8,128)S(1)}, f32[4,6,32,512]{3,2,1,0:T(8,128)S(1)}, f32[4,6,32,128]{3,2,1,0:T(8,128)S(1)}, f32[8,24]{1,0:T(8,128)S(1)}, f32[8,128]{1,0:T(8,128)}) custom-call(s32[4]{0:T(128)S(1)} %pad_add_fusion.where_ref, f32[6,256,2048]{2,1,0:T(8,128)} %bitcast.6, f32[16,8,24]{2,1,0:T(8,128)} %constant.37.clone.table_ref, ...), custom_call_target="tpu_custom_call" | custom-call | flops 458752 | bytes 22020096 | tf_op jit(solution)/shard_map/pallas_call | solution.py:364
  6.3 4.6 %collective-permute-start.6 = (f32[3,6,32,512]{3,2,1,0:T(8,128)S(1)}, f32[3,6,32,512]{3,2,1,0:T(8,128)S(1)}, u32[]{:S(2)}, u32[]{:S(2)}) collective-permute-start(f32[3,6,32,512]{3,2,1,0:T(8,128)S(1)} %get-tuple-element.140), channel_id=1, source_target_pairs={{0,8},{2,10},{4,12},{6,14},{24,16},{26,18},{28,20},{30,22},{1,9},{... | collective-permute-start | bytes 3538952 | tf_op jit(solution)/shard_map/ppermute | solution.py:377
  19.6 3.3 %collective-permute-done.1.r2_ref = f32[4,6,32,128]{3,2,1,0:T(8,128)S(1)} collective-permute-done((f32[4,6,32,128]{3,2,1,0:T(8,128)S(1)}, f32[4,6,32,128]{3,2,1,0:T(8,128)S(1)}, u32[]{:S(2)}, u32[]{:S(2)}) %collective-permute-start.1) | collective-permute-done | bytes 393248 | tf_op jit(solution)/shard_map/ppermute | solution.py:377
  22.9 7.4 %collective-permute-done.2.r3_ref = f32[4,6,32,128]{3,2,1,0:T(8,128)S(1)} collective-permute-done((f32[4,6,32,128]{3,2,1,0:T(8,128)S(1)}, f32[4,6,32,128]{3,2,1,0:T(8,128)S(1)}, u32[]{:S(2)}, u32[]{:S(2)}) %collective-permute-start.2) | collective-permute-done | bytes 393248 | tf_op jit(solution)/shard_map/ppermute | solution.py:377
  31.7 4.9 %collective-permute-done.6.in_ref = f32[3,6,32,512]{3,2,1,0:T(8,128)S(1)} collective-permute-done((f32[3,6,32,512]{3,2,1,0:T(8,128)S(1)}, f32[3,6,32,512]{3,2,1,0:T(8,128)S(1)}, u32[]{:S(2)}, u32[]{:S(2)}) %collective-permute-start.6) | collective-permute-done | bytes 1179680 | tf_op jit(solution)/shard_map/ppermute | solution.py:377
  39.4 7.2 %collective-permute-start.3 = (f32[3,17,32,128]{3,2,1,0:T(8,128)S(1)}, f32[3,17,32,128]{3,2,1,0:T(8,128)S(1)}, u32[]{:S(2)}, u32[]{:S(2)}) collective-permute-start(f32[3,17,32,128]{3,2,1,0:T(8,128)S(1)} %get-tuple-element.135.own_ref.refs_3_), channel_id=1, source_target_pairs={{0,8},{2,10},{4,12},{6,14},{24,16},{26,18},{28,20},{30,22},{1,9},{... | collective-permute-start | bytes 2506760 | tf_op jit(solution)/shard_map/ppermute | solution.py:377
  51.5 6.5 %collective-permute-done.5.r3_ref = f32[4,6,32,128]{3,2,1,0:T(8,128)S(1)} collective-permute-done((f32[4,6,32,128]{3,2,1,0:T(8,128)S(1)}, f32[4,6,32,128]{3,2,1,0:T(8,128)S(1)}, u32[]{:S(2)}, u32[]{:S(2)}) %collective-permute-start.5) | collective-permute-done | bytes 393248 | tf_op jit(solution)/shard_map/ppermute | solution.py:377
  62.6 2.9 %collective-permute-done.3.in_ref.refs_6_ = f32[3,17,32,128]{3,2,1,0:T(8,128)S(1)} collective-permute-done((f32[3,17,32,128]{3,2,1,0:T(8,128)S(1)}, f32[3,17,32,128]{3,2,1,0:T(8,128)S(1)}, u32[]{:S(2)}, u32[]{:S(2)}) %collective-permute-start.3) | collective-permute-done | bytes 835616 | tf_op jit(solution)/shard_map/ppermute | solution.py:377
  69.0 10.0 %collective-permute-done.16.r3_ref = f32[4,6,40,128]{3,2,1,0:T(8,128)S(1)} collective-permute-done((f32[4,6,40,128]{3,2,1,0:T(8,128)S(1)}, f32[4,6,40,128]{3,2,1,0:T(8,128)S(1)}, u32[]{:S(2)}, u32[]{:S(2)}) %collective-permute-start.16) | collective-permute-done | bytes 491552 | tf_op jit(solution)/shard_map/ppermute | solution.py:377
  85.7 5.7 %collective-permute-done.11.r2_ref = f32[4,6,16,128]{3,2,1,0:T(8,128)S(1)} collective-permute-done((f32[4,6,16,128]{3,2,1,0:T(8,128)S(1)}, f32[4,6,16,128]{3,2,1,0:T(8,128)S(1)}, u32[]{:S(2)}, u32[]{:S(2)}) %collective-permute-start.11) | collective-permute-done | bytes 196640 | tf_op jit(solution)/shard_map/ppermute | solution.py:377
  91.4 3.3 %collective-permute-done.12.r3_ref = f32[4,6,16,128]{3,2,1,0:T(8,128)S(1)} collective-permute-done((f32[4,6,16,128]{3,2,1,0:T(8,128)S(1)}, f32[4,6,16,128]{3,2,1,0:T(8,128)S(1)}, u32[]{:S(2)}, u32[]{:S(2)}) %collective-permute-start.12) | collective-permute-done | bytes 196640 | tf_op jit(solution)/shard_map/ppermute | solution.py:377
  95.2 9.7 %collective-permute-done.20.in_ref.refs_8_ = f32[3,17,40,128]{3,2,1,0:T(8,128)S(1)} collective-permute-done((f32[3,17,40,128]{3,2,1,0:T(8,128)S(1)}, f32[3,17,40,128]{3,2,1,0:T(8,128)S(1)}, u32[]{:S(2)}, u32[]{:S(2)}) %collective-permute-start.20) | collective-permute-done | bytes 1044512 | tf_op jit(solution)/shard_map/ppermute | solution.py:377
  108.2 3.5 %collective-permute-done.19.r3_ref = f32[4,6,32,128]{3,2,1,0:T(8,128)S(1)} collective-permute-done((f32[4,6,32,128]{3,2,1,0:T(8,128)S(1)}, f32[4,6,32,128]{3,2,1,0:T(8,128)S(1)}, u32[]{:S(2)}, u32[]{:S(2)}) %collective-permute-start.19) | collective-permute-done | bytes 393248 | tf_op jit(solution)/shard_map/ppermute | solution.py:377
  113.7 7.3 %collective-permute-done.9.r2_ref = f32[4,6,32,128]{3,2,1,0:T(8,128)S(1)} collective-permute-done((f32[4,6,32,128]{3,2,1,0:T(8,128)S(1)}, f32[4,6,32,128]{3,2,1,0:T(8,128)S(1)}, u32[]{:S(2)}, u32[]{:S(2)}) %collective-permute-start.9) | collective-permute-done | bytes 393248 | tf_op jit(solution)/shard_map/ppermute | solution.py:377
  120.9 4.6 %collective-permute-start.25 = (f32[2,17,32,128]{3,2,1,0:T(8,128)S(1)}, f32[2,17,32,128]{3,2,1,0:T(8,128)S(1)}, u32[]{:S(2)}, u32[]{:S(2)}) collective-permute-start(f32[2,17,32,128]{3,2,1,0:T(8,128)S(1)} %get-tuple-element.183.own_ref), channel_id=1, source_target_pairs={{0,8},{2,10},{4,12},{6,14},{24,16},{26,18},{28,20},{30,22},{1,9},{... | collective-permute-start | bytes 1671176 | tf_op jit(solution)/shard_map/ppermute | solution.py:377
  127.6 4.0 %collective-permute-start.17 = (f32[3,17,16,128]{3,2,1,0:T(8,128)S(1)}, f32[3,17,16,128]{3,2,1,0:T(8,128)S(1)}, u32[]{:S(2)}, u32[]{:S(2)}) collective-permute-start(f32[3,17,16,128]{3,2,1,0:T(8,128)S(1)} %get-tuple-element.167.own_ref.refs_2_), channel_id=1, source_target_pairs={{0,8},{2,10},{4,12},{6,14},{24,16},{26,18},{28,20},{30,22},{1,9},{... | collective-permute-start | bytes 1253384 | tf_op jit(solution)/shard_map/ppermute | solution.py:377
  132.4 11.9 %collective-permute-done.17.in_ref.refs_4_ = f32[3,17,16,128]{3,2,1,0:T(8,128)S(1)} collective-permute-done((f32[3,17,16,128]{3,2,1,0:T(8,128)S(1)}, f32[3,17,16,128]{3,2,1,0:T(8,128)S(1)}, u32[]{:S(2)}, u32[]{:S(2)}) %collective-permute-start.17) | collective-permute-done | bytes 417824 | tf_op jit(solution)/shard_map/ppermute | solution.py:377
  145.7 7.7 %collective-permute-start.22 = (f32[2,17,32,128]{3,2,1,0:T(8,128)S(1)}, f32[2,17,32,128]{3,2,1,0:T(8,128)S(1)}, u32[]{:S(2)}, u32[]{:S(2)}) collective-permute-start(f32[2,17,32,128]{3,2,1,0:T(8,128)S(1)} %get-tuple-element.179.own_ref), channel_id=1, source_target_pairs={{0,8},{2,10},{4,12},{6,14},{24,16},{26,18},{28,20},{30,22},{1,9},{... | collective-permute-start | bytes 1671176 | tf_op jit(solution)/shard_map/ppermute | solution.py:377
  157.7 4.5 %collective-permute-done.7.r2_ref = f32[4,6,16,128]{3,2,1,0:T(8,128)S(1)} collective-permute-done((f32[4,6,16,128]{3,2,1,0:T(8,128)S(1)}, f32[4,6,16,128]{3,2,1,0:T(8,128)S(1)}, u32[]{:S(2)}, u32[]{:S(2)}) %collective-permute-start.7) | collective-permute-done | bytes 196640 | tf_op jit(solution)/shard_map/ppermute | solution.py:377
  162.2 2.9 %collective-permute-start.33 = (f32[2,17,24,128]{3,2,1,0:T(8,128)S(1)}, f32[2,17,24,128]{3,2,1,0:T(8,128)S(1)}, u32[]{:S(2)}, u32[]{:S(2)}) collective-permute-start(f32[2,17,24,128]{3,2,1,0:T(8,128)S(1)} %get-tuple-element.202.own_ref), channel_id=1, source_target_pairs={{0,8},{2,10},{4,12},{6,14},{24,16},{26,18},{28,20},{30,22},{1,9},{... | collective-permute-start | bytes 1253384 | tf_op jit(solution)/shard_map/ppermute | solution.py:377
  169.8 12.5 %collective-permute-start.40 = (f32[17,88,128]{2,1,0:T(8,128)S(1)}, f32[17,88,128]{2,1,0:T(8,128)S(1)}, u32[]{:S(2)}, u32[]{:S(2)}) collective-permute-start(f32[17,88,128]{2,1,0:T(8,128)S(1)} %get-tuple-element.225), channel_id=1, source_target_pairs={{0,8},{2,10},{4,12},{6,14},{24,16},{26,18},{28,20},{30,22},{1,9},{... | collective-permute-start | bytes 2297864 | tf_op jit(solution)/shard_map/ppermute | solution.py:377
  184.8 6.4 %collective-permute-done.32.refs_3_ = f32[11,32,128]{2,1,0:T(8,128)S(1)} collective-permute-done((f32[11,32,128]{2,1,0:T(8,128)S(1)}, f32[11,32,128]{2,1,0:T(8,128)S(1)}, u32[]{:S(2)}, u32[]{:S(2)}) %collective-permute-start.32) | collective-permute-done | bytes 180256 | tf_op jit(solution)/shard_map/ppermute | solution.py:377
  191.9 12.8 %collective-permute-done.37.in_ref = f32[2,17,16,128]{3,2,1,0:T(8,128)S(1)} collective-permute-done((f32[2,17,16,128]{3,2,1,0:T(8,128)S(1)}, f32[2,17,16,128]{3,2,1,0:T(8,128)S(1)}, u32[]{:S(2)}, u32[]{:S(2)}) %collective-permute-start.37) | collective-permute-done | bytes 278560 | tf_op jit(solution)/shard_map/ppermute | solution.py:377
  213.8 5.3 %collective-permute-done.41.refs_8_ = f32[17,48,128]{2,1,0:T(8,128)S(1)} collective-permute-done((f32[17,48,128]{2,1,0:T(8,128)S(1)}, f32[17,48,128]{2,1,0:T(8,128)S(1)}, u32[]{:S(2)}, u32[]{:S(2)}) %collective-permute-start.41) | collective-permute-done | bytes 417824 | tf_op jit(solution)/shard_map/ppermute | solution.py:377
  (110 shorter events, 79.1 us)
Async XLA Ops:
  5.7 24.6 %collective-permute-start = (f32[4,6,224,128]{3,2,1,0:T(8,128)S(1)}, f32[4,6,224,128]{3,2,1,0:T(8,128)S(1)}, u32[]{:S(2)}, u32[]{:S(2)}) collective-permute-start(f32[4,6,224,128]{3,2,1,0:T(8,128)S(1)} %get-tuple-element.128), channel_id=1, source_target_pairs={{0,2},{2,0},{4,6},{6,4},{8,10},{10,8},{12,14},{14,12},{16,18},{18,... | collective-permute-start | bytes 8257544 | tf_op jit(solution)/shard_map/ppermute | solution.py:377
  6.3 30.3 %collective-permute-start.6 = (f32[3,6,32,512]{3,2,1,0:T(8,128)S(1)}, f32[3,6,32,512]{3,2,1,0:T(8,128)S(1)}, u32[]{:S(2)}, u32[]{:S(2)}) collective-permute-start(f32[3,6,32,512]{3,2,1,0:T(8,128)S(1)} %get-tuple-element.140), channel_id=1, source_target_pairs={{0,8},{2,10},{4,12},{6,14},{24,16},{26,18},{28,20},{30,22},{1,9},{... | collective-permute-start | bytes 3538952 | tf_op jit(solution)/shard_map/ppermute | solution.py:377
  14.4 33.8 %collective-permute-start.4 = (f32[4,6,32,128]{3,2,1,0:T(8,128)S(1)}, f32[4,6,32,128]{3,2,1,0:T(8,128)S(1)}, u32[]{:S(2)}, u32[]{:S(2)}) collective-permute-start(f32[4,6,32,128]{3,2,1,0:T(8,128)S(1)} %get-tuple-element.137), channel_id=1, source_target_pairs={{0,4},{2,6},{4,0},{6,2},{8,12},{10,14},{12,8},{14,10},{16,20},{18,... | collective-permute-start | bytes 1179656 | tf_op jit(solution)/shard_map/ppermute | solution.py:377
  38.6 43.6 %collective-permute-start.13 = (f32[2,11,32,512]{3,2,1,0:T(8,128)S(1)}, f32[2,11,32,512]{3,2,1,0:T(8,128)S(1)}, u32[]{:S(2)}, u32[]{:S(2)}) collective-permute-start(f32[2,11,32,512]{3,2,1,0:T(8,128)S(1)} %get-tuple-element.158), channel_id=1, source_target_pairs={{8,16},{10,18},{12,20},{14,22},{16,8},{18,10},{20,12},{22,14},{9,1... | collective-permute-start | bytes 4325384 | tf_op jit(solution)/shard_map/ppermute | solution.py:377
  39.4 26.1 %collective-permute-start.3 = (f32[3,17,32,128]{3,2,1,0:T(8,128)S(1)}, f32[3,17,32,128]{3,2,1,0:T(8,128)S(1)}, u32[]{:S(2)}, u32[]{:S(2)}) collective-permute-start(f32[3,17,32,128]{3,2,1,0:T(8,128)S(1)} %get-tuple-element.135.own_ref.refs_3_), channel_id=1, source_target_pairs={{0,8},{2,10},{4,12},{6,14},{24,16},{26,18},{28,20},{30,22},{1,9},{... | collective-permute-start | bytes 2506760 | tf_op jit(solution)/shard_map/ppermute | solution.py:377
  46.8 22.2 %collective-permute-start.15 = (f32[4,6,40,128]{3,2,1,0:T(8,128)S(1)}, f32[4,6,40,128]{3,2,1,0:T(8,128)S(1)}, u32[]{:S(2)}, u32[]{:S(2)}) collective-permute-start(f32[4,6,40,128]{3,2,1,0:T(8,128)S(1)} %get-tuple-element.161), channel_id=1, source_target_pairs={{0,4},{2,6},{4,0},{6,2},{8,12},{10,14},{12,8},{14,10},{16,20},{18,... | collective-permute-start | bytes 1474568 | tf_op jit(solution)/shard_map/ppermute | solution.py:377
  48.2 30.9 %collective-permute-start.16 = (f32[4,6,40,128]{3,2,1,0:T(8,128)S(1)}, f32[4,6,40,128]{3,2,1,0:T(8,128)S(1)}, u32[]{:S(2)}, u32[]{:S(2)}) collective-permute-start(f32[4,6,40,128]{3,2,1,0:T(8,128)S(1)} %get-tuple-element.162), channel_id=1, source_target_pairs={{0,6},{2,4},{4,2},{6,0},{8,14},{10,12},{12,10},{14,8},{16,22},{18,... | collective-permute-start | bytes 1474568 | tf_op jit(solution)/shard_map/ppermute | solution.py:377
  59.3 22.8 %collective-permute-start.14 = (f32[3,17,32,128]{3,2,1,0:T(8,128)S(1)}, f32[3,17,32,128]{3,2,1,0:T(8,128)S(1)}, u32[]{:S(2)}, u32[]{:S(2)}) collective-permute-start(f32[3,17,32,128]{3,2,1,0:T(8,128)S(1)} %get-tuple-element.159.own_ref.refs_4_), channel_id=1, source_target_pairs={{0,8},{2,10},{4,12},{6,14},{24,16},{26,18},{28,20},{30,22},{1,9},{... | collective-permute-start | bytes 2506760 | tf_op jit(solution)/shard_map/ppermute | solution.py:377
  80.7 24.2 %collective-permute-start.20 = (f32[3,17,40,128]{3,2,1,0:T(8,128)S(1)}, f32[3,17,40,128]{3,2,1,0:T(8,128)S(1)}, u32[]{:S(2)}, u32[]{:S(2)}) collective-permute-start(f32[3,17,40,128]{3,2,1,0:T(8,128)S(1)} %get-tuple-element.171.own_ref.refs_5_), channel_id=1, source_target_pairs={{0,8},{2,10},{4,12},{6,14},{24,16},{26,18},{28,20},{30,22},{1,9},{... | collective-permute-start | bytes 3133448 | tf_op jit(solution)/shard_map/ppermute | solution.py:377
  82.3 22.6 %collective-permute-start.21 = (f32[11,32,512]{2,1,0:T(8,128)S(1)}, f32[11,32,512]{2,1,0:T(8,128)S(1)}, u32[]{:S(2)}, u32[]{:S(2)}) collective-permute-start(f32[11,32,512]{2,1,0:T(8,128)S(1)} %get-tuple-element.173), channel_id=1, source_target_pairs={{8,0},{10,2},{12,4},{14,6},{16,24},{18,26},{20,28},{22,30},{9,1},{... | collective-permute-start | bytes 2162696 | tf_op jit(solution)/shard_map/ppermute | solution.py:377
  85.2 22.2 %collective-permute-start.18 = (f32[4,6,32,128]{3,2,1,0:T(8,128)S(1)}, f32[4,6,32,128]{3,2,1,0:T(8,128)S(1)}, u32[]{:S(2)}, u32[]{:S(2)}) collective-permute-start(f32[4,6,32,128]{3,2,1,0:T(8,128)S(1)} %get-tuple-element.169), channel_id=1, source_target_pairs={{0,4},{2,6},{4,0},{6,2},{8,12},{10,14},{12,8},{14,10},{16,20},{18,... | collective-permute-start | bytes 1179656 | tf_op jit(solution)/shard_map/ppermute | solution.py:377
  94.8 26.2 %collective-permute-start.9 = (f32[4,6,32,128]{3,2,1,0:T(8,128)S(1)}, f32[4,6,32,128]{3,2,1,0:T(8,128)S(1)}, u32[]{:S(2)}, u32[]{:S(2)}) collective-permute-start(f32[4,6,32,128]{3,2,1,0:T(8,128)S(1)} %get-tuple-element.152), channel_id=1, source_target_pairs={{0,4},{2,6},{4,0},{6,2},{8,12},{10,14},{12,8},{14,10},{16,20},{18,... | collective-permute-start | bytes 1179656 | tf_op jit(solution)/shard_map/ppermute | solution.py:377
  104.9 22.7 %collective-permute-start.10 = (f32[4,6,32,128]{3,2,1,0:T(8,128)S(1)}, f32[4,6,32,128]{3,2,1,0:T(8,128)S(1)}, u32[]{:S(2)}, u32[]{:S(2)}) collective-permute-start(f32[4,6,32,128]{3,2,1,0:T(8,128)S(1)} %get-tuple-element.153), channel_id=1, source_target_pairs={{0,6},{2,4},{4,2},{6,0},{8,14},{10,12},{12,10},{14,8},{16,22},{18,... | collective-permute-start | bytes 1179656 | tf_op jit(solution)/shard_map/ppermute | solution.py:377
  104.9 26.8 %collective-permute-start.26 = (f32[2,17,32,128]{3,2,1,0:T(8,128)S(1)}, f32[2,17,32,128]{3,2,1,0:T(8,128)S(1)}, u32[]{:S(2)}, u32[]{:S(2)}) collective-permute-start(f32[2,17,32,128]{3,2,1,0:T(8,128)S(1)} %get-tuple-element.187), channel_id=1, source_target_pairs={{8,16},{10,18},{12,20},{14,22},{16,8},{18,10},{20,12},{22,14},{9,1... | collective-permute-start | bytes 1671176 | tf_op jit(solution)/shard_map/ppermute | solution.py:377
  107.4 46.0 %collective-permute-start.28 = (f32[2,17,40,128]{3,2,1,0:T(8,128)S(1)}, f32[2,17,40,128]{3,2,1,0:T(8,128)S(1)}, u32[]{:S(2)}, u32[]{:S(2)}) collective-permute-start(f32[2,17,40,128]{3,2,1,0:T(8,128)S(1)} %get-tuple-element.189), channel_id=1, source_target_pairs={{8,16},{10,18},{12,20},{14,22},{16,8},{18,10},{20,12},{22,14},{9,1... | collective-permute-start | bytes 2088968 | tf_op jit(solution)/shard_map/ppermute | solution.py:377
  111.6 34.1 %collective-permute-start.27 = (f32[2,17,32,128]{3,2,1,0:T(8,128)S(1)}, f32[2,17,32,128]{3,2,1,0:T(8,128)S(1)}, u32[]{:S(2)}, u32[]{:S(2)}) collective-permute-start(f32[2,17,32,128]{3,2,1,0:T(8,128)S(1)} %get-tuple-element.188), channel_id=1, source_target_pairs={{8,16},{10,18},{12,20},{14,22},{16,8},{18,10},{20,12},{22,14},{9,1... | collective-permute-start | bytes 1671176 | tf_op jit(solution)/shard_map/ppermute | solution.py:377
  120.9 32.6 %collective-permute-start.25 = (f32[2,17,32,128]{3,2,1,0:T(8,128)S(1)}, f32[2,17,32,128]{3,2,1,0:T(8,128)S(1)}, u32[]{:S(2)}, u32[]{:S(2)}) collective-permute-start(f32[2,17,32,128]{3,2,1,0:T(8,128)S(1)} %get-tuple-element.183.own_ref), channel_id=1, source_target_pairs={{0,8},{2,10},{4,12},{6,14},{24,16},{26,18},{28,20},{30,22},{1,9},{... | collective-permute-start | bytes 1671176 | tf_op jit(solution)/shard_map/ppermute | solution.py:377
  131.7 24.0 %collective-permute-start.23 = (f32[4,6,24,128]{3,2,1,0:T(8,128)S(1)}, f32[4,6,24,128]{3,2,1,0:T(8,128)S(1)}, u32[]{:S(2)}, u32[]{:S(2)}) collective-permute-start(f32[4,6,24,128]{3,2,1,0:T(8,128)S(1)} %get-tuple-element.181), channel_id=1, source_target_pairs={{0,4},{2,6},{4,0},{6,2},{8,12},{10,14},{12,8},{14,10},{16,20},{18,... | collective-permute-start | bytes 884744 | tf_op jit(solution)/shard_map/ppermute | solution.py:377
  162.2 22.1 %collective-permute-start.33 = (f32[2,17,24,128]{3,2,1,0:T(8,128)S(1)}, f32[2,17,24,128]{3,2,1,0:T(8,128)S(1)}, u32[]{:S(2)}, u32[]{:S(2)}) collective-permute-start(f32[2,17,24,128]{3,2,1,0:T(8,128)S(1)} %get-tuple-element.202.own_ref), channel_id=1, source_target_pairs={{0,8},{2,10},{4,12},{6,14},{24,16},{26,18},{28,20},{30,22},{1,9},{... | collective-permute-start | bytes 1253384 | tf_op jit(solution)/shard_map/ppermute | solution.py:377
  165.1 43.3 %collective-permute-start.29 = (f32[17,104,128]{2,1,0:T(8,128)S(1)}, f32[17,104,128]{2,1,0:T(8,128)S(1)}, u32[]{:S(2)}, u32[]{:S(2)}) collective-permute-start(f32[17,104,128]{2,1,0:T(8,128)S(1)} %get-tuple-element.197), channel_id=1, source_target_pairs={{8,0},{10,2},{12,4},{14,6},{16,24},{18,26},{20,28},{22,30},{9,1},{... | collective-permute-start | bytes 2715656 | tf_op jit(solution)/shard_map/ppermute | solution.py:377
  168.0 39.7 %collective-permute-start.36 = (f32[2,17,32,128]{3,2,1,0:T(8,128)S(1)}, f32[2,17,32,128]{3,2,1,0:T(8,128)S(1)}, u32[]{:S(2)}, u32[]{:S(2)}) collective-permute-start(f32[2,17,32,128]{3,2,1,0:T(8,128)S(1)} %get-tuple-element.217), channel_id=1, source_target_pairs={{8,16},{10,18},{12,20},{14,22},{16,8},{18,10},{20,12},{22,14},{9,1... | collective-permute-start | bytes 1671176 | tf_op jit(solution)/shard_map/ppermute | solution.py:377
  169.8 51.6 %collective-permute-start.40 = (f32[17,88,128]{2,1,0:T(8,128)S(1)}, f32[17,88,128]{2,1,0:T(8,128)S(1)}, u32[]{:S(2)}, u32[]{:S(2)}) collective-permute-start(f32[17,88,128]{2,1,0:T(8,128)S(1)} %get-tuple-element.225), channel_id=1, source_target_pairs={{0,8},{2,10},{4,12},{6,14},{24,16},{26,18},{28,20},{30,22},{1,9},{... | collective-permute-start | bytes 2297864 | tf_op jit(solution)/shard_map/ppermute | solution.py:377
  182.3 22.4 %collective-permute-start.37 = (f32[2,17,16,128]{3,2,1,0:T(8,128)S(1)}, f32[2,17,16,128]{3,2,1,0:T(8,128)S(1)}, u32[]{:S(2)}, u32[]{:S(2)}) collective-permute-start(f32[2,17,16,128]{3,2,1,0:T(8,128)S(1)} %get-tuple-element.218.own_ref), channel_id=1, source_target_pairs={{0,8},{2,10},{4,12},{6,14},{24,16},{26,18},{28,20},{30,22},{1,9},{... | collective-permute-start | bytes 835592 | tf_op jit(solution)/shard_map/ppermute | solution.py:377
  191.2 21.3 %collective-permute-start.42 = (f32[2,17,24,128]{3,2,1,0:T(8,128)S(1)}, f32[2,17,24,128]{3,2,1,0:T(8,128)S(1)}, u32[]{:S(2)}, u32[]{:S(2)}) collective-permute-start(f32[2,17,24,128]{3,2,1,0:T(8,128)S(1)} %get-tuple-element.230), channel_id=1, source_target_pairs={{8,16},{10,18},{12,20},{14,22},{16,8},{18,10},{20,12},{22,14},{9,1... | collective-permute-start | bytes 1253384 | tf_op jit(solution)/shard_map/ppermute | solution.py:377
  (22 other events, 278.6 us)

commit v5 on v4

--- a/solution.py
+++ b/solution.py
@@ -24,13 +24,13 @@
     "P0 q0 p1 p2",
     "p3 t0 S0 p4",
     "t1 p5 m0 p6",
-    "p7 t2 m1 R0",
-    "t3 T0 m2 t4",
-    "m3 t5 r0 m4",
-    "t6 m5 t7 r1",
-    "n0 m6 F0 m7",
-    "r2 f0 n1 r3",
-    "f1 r4 f2 f3",
+    "p7 t2 m1 t3",
+    "R0 m2 t4 m3",
+    "t5 T0 m4 r0",
+    "t6 m5 t7 n0",
+    "n1 m6 r1 m7",
+    "F0 f0 r2 r3",
+    "r4 f1 f2 f3",
     "f4",
 )).split()
 FINAL_ROWS = 8

time: 233 us -> 232 us (level)
  waiting for transfers between devices: 111 us -> 103 us
  starting transfers between devices: 77.7 us -> 84.1 us
    ppermute x46, waiting for transfers between devices: 111 us -> 103 us  [move(): return lax.ppermute(value, 'io', pairs)]
    ppermute x46, starting transfers between devices: 77.7 us -> 84.1 us  [move(): return lax.ppermute(value, 'io', pairs)]
  transfers between devices with their start and end apart: 46 -> 46, of which waited for: 19 -> 21; matrix products, arithmetic and copies ran while one was open for 0% -> 0% of each run, Pallas kernels for 16% -> 16%
where the time goes in v5:
time: 232 us; the launch traced here: 231 us
  waiting for transfers between devices  103 us (44%)
  starting transfers between devices  84.1 us (36%)
  Pallas kernels  42.6 us (18%)
    ppermute x46, waiting for transfers between devices, move(): return lax.ppermute(value, 'io', pairs)  103 us
    ppermute x46, starting transfers between devices, move(): return lax.ppermute(value, 'io', pairs)  84.1 us
    pallas_call x41, Pallas kernels, call(): pl.pallas_call(kernel, in_specs=ins, out_specs=(out_specs or [vmem] * len...  42.6 us
  transfers between devices with their start and end apart: 46, of which 21 were waited for; matrix products, arithmetic and copies ran while one was open for 0% of the time, Pallas kernels for 16%

profile of v5, /device:TPU:0, one launch (start us, length us, event | category | flops | bytes accessed | tf_op | source)
XLA Modules:
  0.0 230.9 jit_solution(220237163344808824)
XLA Ops:
  2.8 2.9 %shard_map.42 = (f32[4,6,224,128]{3,2,1,0:T(8,128)S(1)}, f32[4,6,32,512]{3,2,1,0:T(8,128)S(1)}, f32[4,6,32,128]{3,2,1,0:T(8,128)S(1)}, f32[8,24]{1,0:T(8,128)S(1)}, f32[8,128]{1,0:T(8,128)}) custom-call(s32[4]{0:T(128)S(1)} %pad_add_fusion.where_ref, f32[6,256,2048]{2,1,0:T(8,128)} %bitcast.6, f32[16,8,24]{2,1,0:T(8,128)} %constant.37.clone.table_ref, ...), custom_call_target="tpu_custom_call" | custom-call | flops 458752 | bytes 22020096 | tf_op jit(solution)/shard_map/pallas_call | solution.py:364
  6.3 4.6 %collective-permute-start.6 = (f32[3,6,32,512]{3,2,1,0:T(8,128)S(1)}, f32[3,6,32,512]{3,2,1,0:T(8,128)S(1)}, u32[]{:S(2)}, u32[]{:S(2)}) collective-permute-start(f32[3,6,32,512]{3,2,1,0:T(8,128)S(1)} %get-tuple-element.140), channel_id=1, source_target_pairs={{0,8},{2,10},{4,12},{6,14},{24,16},{26,18},{28,20},{30,22},{1,9},{... | collective-permute-start | bytes 3538952 | tf_op jit(solution)/shard_map/ppermute | solution.py:377
  18.0 4.8 %collective-permute-done.1.r2_ref = f32[4,6,32,128]{3,2,1,0:T(8,128)S(1)} collective-permute-done((f32[4,6,32,128]{3,2,1,0:T(8,128)S(1)}, f32[4,6,32,128]{3,2,1,0:T(8,128)S(1)}, u32[]{:S(2)}, u32[]{:S(2)}) %collective-permute-start.1) | collective-permute-done | bytes 393248 | tf_op jit(solution)/shard_map/ppermute | solution.py:377
  22.9 6.9 %collective-permute-done.2.r3_ref = f32[4,6,32,128]{3,2,1,0:T(8,128)S(1)} collective-permute-done((f32[4,6,32,128]{3,2,1,0:T(8,128)S(1)}, f32[4,6,32,128]{3,2,1,0:T(8,128)S(1)}, u32[]{:S(2)}, u32[]{:S(2)}) %collective-permute-start.2) | collective-permute-done | bytes 393248 | tf_op jit(solution)/shard_map/ppermute | solution.py:377
  34.7 2.4 %collective-permute-done.6.in_ref = f32[3,6,32,512]{3,2,1,0:T(8,128)S(1)} collective-permute-done((f32[3,6,32,512]{3,2,1,0:T(8,128)S(1)}, f32[3,6,32,512]{3,2,1,0:T(8,128)S(1)}, u32[]{:S(2)}, u32[]{:S(2)}) %collective-permute-start.6) | collective-permute-done | bytes 1179680 | tf_op jit(solution)/shard_map/ppermute | solution.py:377
  41.4 3.6 %collective-permute-done.4.r2_ref = f32[4,6,32,128]{3,2,1,0:T(8,128)S(1)} collective-permute-done((f32[4,6,32,128]{3,2,1,0:T(8,128)S(1)}, f32[4,6,32,128]{3,2,1,0:T(8,128)S(1)}, u32[]{:S(2)}, u32[]{:S(2)}) %collective-permute-start.4) | collective-permute-done | bytes 393248 | tf_op jit(solution)/shard_map/ppermute | solution.py:377
  46.9 5.5 %collective-permute-done.5.r3_ref = f32[4,6,32,128]{3,2,1,0:T(8,128)S(1)} collective-permute-done((f32[4,6,32,128]{3,2,1,0:T(8,128)S(1)}, f32[4,6,32,128]{3,2,1,0:T(8,128)S(1)}, u32[]{:S(2)}, u32[]{:S(2)}) %collective-permute-start.5) | collective-permute-done | bytes 393248 | tf_op jit(solution)/shard_map/ppermute | solution.py:377
  64.0 9.5 %collective-permute-done.15.r3_ref = f32[4,6,40,128]{3,2,1,0:T(8,128)S(1)} collective-permute-done((f32[4,6,40,128]{3,2,1,0:T(8,128)S(1)}, f32[4,6,40,128]{3,2,1,0:T(8,128)S(1)}, u32[]{:S(2)}, u32[]{:S(2)}) %collective-permute-start.15) | collective-permute-done | bytes 491552 | tf_op jit(solution)/shard_map/ppermute | solution.py:377
  79.6 4.3 %collective-permute-done.12.r3_ref = f32[4,6,16,128]{3,2,1,0:T(8,128)S(1)} collective-permute-done((f32[4,6,16,128]{3,2,1,0:T(8,128)S(1)}, f32[4,6,16,128]{3,2,1,0:T(8,128)S(1)}, u32[]{:S(2)}, u32[]{:S(2)}) %collective-permute-start.12) | collective-permute-done | bytes 196640 | tf_op jit(solution)/shard_map/ppermute | solution.py:377
  85.7 7.5 %collective-permute-done.17.r2_ref = f32[4,6,32,128]{3,2,1,0:T(8,128)S(1)} collective-permute-done((f32[4,6,32,128]{3,2,1,0:T(8,128)S(1)}, f32[4,6,32,128]{3,2,1,0:T(8,128)S(1)}, u32[]{:S(2)}, u32[]{:S(2)}) %collective-permute-start.17) | collective-permute-done | bytes 393248 | tf_op jit(solution)/shard_map/ppermute | solution.py:377
  95.7 4.9 %collective-permute-done.18.r3_ref = f32[4,6,32,128]{3,2,1,0:T(8,128)S(1)} collective-permute-done((f32[4,6,32,128]{3,2,1,0:T(8,128)S(1)}, f32[4,6,32,128]{3,2,1,0:T(8,128)S(1)}, u32[]{:S(2)}, u32[]{:S(2)}) %collective-permute-start.18) | collective-permute-done | bytes 393248 | tf_op jit(solution)/shard_map/ppermute | solution.py:377
  103.1 6.0 %collective-permute-done.10.r3_ref = f32[4,6,32,128]{3,2,1,0:T(8,128)S(1)} collective-permute-done((f32[4,6,32,128]{3,2,1,0:T(8,128)S(1)}, f32[4,6,32,128]{3,2,1,0:T(8,128)S(1)}, u32[]{:S(2)}, u32[]{:S(2)}) %collective-permute-start.10) | collective-permute-done | bytes 393248 | tf_op jit(solution)/shard_map/ppermute | solution.py:377
  110.4 8.1 %collective-permute-done.9.r2_ref = f32[4,6,32,128]{3,2,1,0:T(8,128)S(1)} collective-permute-done((f32[4,6,32,128]{3,2,1,0:T(8,128)S(1)}, f32[4,6,32,128]{3,2,1,0:T(8,128)S(1)}, u32[]{:S(2)}, u32[]{:S(2)}) %collective-permute-start.9) | collective-permute-done | bytes 393248 | tf_op jit(solution)/shard_map/ppermute | solution.py:377
  124.0 6.8 %collective-permute-start.27 = (f32[2,17,32,128]{3,2,1,0:T(8,128)S(1)}, f32[2,17,32,128]{3,2,1,0:T(8,128)S(1)}, u32[]{:S(2)}, u32[]{:S(2)}) collective-permute-start(f32[2,17,32,128]{3,2,1,0:T(8,128)S(1)} %get-tuple-element.186.own_ref), channel_id=1, source_target_pairs={{0,8},{2,10},{4,12},{6,14},{24,16},{26,18},{28,20},{30,22},{1,9},{... | collective-permute-start | bytes 1671176 | tf_op jit(solution)/shard_map/ppermute | solution.py:377
  132.3 5.1 %collective-permute-start.21 = (f32[2,17,32,128]{3,2,1,0:T(8,128)S(1)}, f32[2,17,32,128]{3,2,1,0:T(8,128)S(1)}, u32[]{:S(2)}, u32[]{:S(2)}) collective-permute-start(f32[2,17,32,128]{3,2,1,0:T(8,128)S(1)} %get-tuple-element.176.own_ref), channel_id=1, source_target_pairs={{0,8},{2,10},{4,12},{6,14},{24,16},{26,18},{28,20},{30,22},{1,9},{... | collective-permute-start | bytes 1671176 | tf_op jit(solution)/shard_map/ppermute | solution.py:377
  139.0 4.8 %collective-permute-done.27.in_ref = f32[2,17,32,128]{3,2,1,0:T(8,128)S(1)} collective-permute-done((f32[2,17,32,128]{3,2,1,0:T(8,128)S(1)}, f32[2,17,32,128]{3,2,1,0:T(8,128)S(1)}, u32[]{:S(2)}, u32[]{:S(2)}) %collective-permute-start.27) | collective-permute-done | bytes 557088 | tf_op jit(solution)/shard_map/ppermute | solution.py:377
  145.5 3.5 %collective-permute-done.8.r3_ref = f32[4,6,16,128]{3,2,1,0:T(8,128)S(1)} collective-permute-done((f32[4,6,16,128]{3,2,1,0:T(8,128)S(1)}, f32[4,6,16,128]{3,2,1,0:T(8,128)S(1)}, u32[]{:S(2)}, u32[]{:S(2)}) %collective-permute-start.8) | collective-permute-done | bytes 196640 | tf_op jit(solution)/shard_map/ppermute | solution.py:377
  155.7 15.6 %collective-permute-start.33 = (f32[2,17,24,128]{3,2,1,0:T(8,128)S(1)}, f32[2,17,24,128]{3,2,1,0:T(8,128)S(1)}, u32[]{:S(2)}, u32[]{:S(2)}) collective-permute-start(f32[2,17,24,128]{3,2,1,0:T(8,128)S(1)} %get-tuple-element.208.own_ref), channel_id=1, source_target_pairs={{0,8},{2,10},{4,12},{6,14},{24,16},{26,18},{28,20},{30,22},{1,9},{... | collective-permute-start | bytes 1253384 | tf_op jit(solution)/shard_map/ppermute | solution.py:377
  173.8 5.1 %collective-permute-done.39.refs_2_ = f32[11,32,128]{2,1,0:T(8,128)S(1)} collective-permute-done((f32[11,32,128]{2,1,0:T(8,128)S(1)}, f32[11,32,128]{2,1,0:T(8,128)S(1)}, u32[]{:S(2)}, u32[]{:S(2)}) %collective-permute-start.39) | collective-permute-done | bytes 180256 | tf_op jit(solution)/shard_map/ppermute | solution.py:377
  181.3 4.6 %collective-permute-start.30 = (f32[2,17,16,128]{3,2,1,0:T(8,128)S(1)}, f32[2,17,16,128]{3,2,1,0:T(8,128)S(1)}, u32[]{:S(2)}, u32[]{:S(2)}) collective-permute-start(f32[2,17,16,128]{3,2,1,0:T(8,128)S(1)} %get-tuple-element.203.own_ref), channel_id=1, source_target_pairs={{0,8},{2,10},{4,12},{6,14},{24,16},{26,18},{28,20},{30,22},{1,9},{... | collective-permute-start | bytes 835592 | tf_op jit(solution)/shard_map/ppermute | solution.py:377
  186.8 16.2 %collective-permute-done.30.in_ref = f32[2,17,16,128]{3,2,1,0:T(8,128)S(1)} collective-permute-done((f32[2,17,16,128]{3,2,1,0:T(8,128)S(1)}, f32[2,17,16,128]{3,2,1,0:T(8,128)S(1)}, u32[]{:S(2)}, u32[]{:S(2)}) %collective-permute-start.30) | collective-permute-done | bytes 278560 | tf_op jit(solution)/shard_map/ppermute | solution.py:377
  206.6 2.7 %shard_map.74 = (f32[16,256,128]{2,1,0:T(8,128)}, f32[256,128]{1,0:T(8,128)}, f32[8,128]{1,0:T(8,128)}) custom-call(s32[4]{0:T(128)S(1)} %pad_add_fusion.where_ref, f32[17,32,128]{2,1,0:T(8,128)S(1)} %get-tuple-element.180.refs_0_, f32[17,32,128]{2,1,0:T(8,128)S(1)} %get-tuple-element.181.refs_1_, ...), custom_call_target="tpu_custom_call", output_to_operand_aliasing={{0}: (14, {}), {1}: (15, {})} | custom-call | flops 11075584 | bytes 3620864 | tf_op jit(solution)/shard_map/pallas_call | solution.py:364
  212.0 7.5 %collective-permute-start.29 = (f32[17,16,128]{2,1,0:T(8,128)S(1)}, f32[17,16,128]{2,1,0:T(8,128)S(1)}, u32[]{:S(2)}, u32[]{:S(2)}) collective-permute-start(f32[17,16,128]{2,1,0:T(8,128)S(1)} %get-tuple-element.202), channel_id=1, source_target_pairs={{0,8},{2,10},{4,12},{6,14},{24,16},{26,18},{28,20},{30,22},{1,9},{... | collective-permute-start | bytes 417800 | tf_op jit(solution)/shard_map/ppermute | solution.py:377
  225.4 2.5 %collective-permute-done.43.refs_4_ = f32[17,24,128]{2,1,0:T(8,128)S(1)} collective-permute-done((f32[17,24,128]{2,1,0:T(8,128)S(1)}, f32[17,24,128]{2,1,0:T(8,128)S(1)}, u32[]{:S(2)}, u32[]{:S(2)}) %collective-permute-start.43) | collective-permute-done | bytes 208928 | tf_op jit(solution)/shard_map/ppermute | solution.py:377
  (110 shorter events, 84.1 us)
Async XLA Ops:
  5.7 24.1 %collective-permute-start = (f32[4,6,224,128]{3,2,1,0:T(8,128)S(1)}, f32[4,6,224,128]{3,2,1,0:T(8,128)S(1)}, u32[]{:S(2)}, u32[]{:S(2)}) collective-permute-start(f32[4,6,224,128]{3,2,1,0:T(8,128)S(1)} %get-tuple-element.128), channel_id=1, source_target_pairs={{0,2},{2,0},{4,6},{6,4},{8,10},{10,8},{12,14},{14,12},{16,18},{18,... | collective-permute-start | bytes 8257544 | tf_op jit(solution)/shard_map/ppermute | solution.py:377
  6.3 30.8 %collective-permute-start.6 = (f32[3,6,32,512]{3,2,1,0:T(8,128)S(1)}, f32[3,6,32,512]{3,2,1,0:T(8,128)S(1)}, u32[]{:S(2)}, u32[]{:S(2)}) collective-permute-start(f32[3,6,32,512]{3,2,1,0:T(8,128)S(1)} %get-tuple-element.140), channel_id=1, source_target_pairs={{0,8},{2,10},{4,12},{6,14},{24,16},{26,18},{28,20},{30,22},{1,9},{... | collective-permute-start | bytes 3538952 | tf_op jit(solution)/shard_map/ppermute | solution.py:377
  31.1 24.2 %collective-permute-start.3 = (f32[3,17,32,128]{3,2,1,0:T(8,128)S(1)}, f32[3,17,32,128]{3,2,1,0:T(8,128)S(1)}, u32[]{:S(2)}, u32[]{:S(2)}) collective-permute-start(f32[3,17,32,128]{3,2,1,0:T(8,128)S(1)} %get-tuple-element.135.own_ref.refs_3_), channel_id=1, source_target_pairs={{0,8},{2,10},{4,12},{6,14},{24,16},{26,18},{28,20},{30,22},{1,9},{... | collective-permute-start | bytes 2506760 | tf_op jit(solution)/shard_map/ppermute | solution.py:377
  39.1 63.1 %collective-permute-start.20 = (f32[2,11,32,512]{3,2,1,0:T(8,128)S(1)}, f32[2,11,32,512]{3,2,1,0:T(8,128)S(1)}, u32[]{:S(2)}, u32[]{:S(2)}) collective-permute-start(f32[2,11,32,512]{3,2,1,0:T(8,128)S(1)} %get-tuple-element.170), channel_id=1, source_target_pairs={{8,16},{10,18},{12,20},{14,22},{16,8},{18,10},{20,12},{22,14},{9,1... | collective-permute-start | bytes 4325384 | tf_op jit(solution)/shard_map/ppermute | solution.py:377
  39.9 24.1 %collective-permute-start.14 = (f32[4,6,40,128]{3,2,1,0:T(8,128)S(1)}, f32[4,6,40,128]{3,2,1,0:T(8,128)S(1)}, u32[]{:S(2)}, u32[]{:S(2)}) collective-permute-start(f32[4,6,40,128]{3,2,1,0:T(8,128)S(1)} %get-tuple-element.159), channel_id=1, source_target_pairs={{0,4},{2,6},{4,0},{6,2},{8,12},{10,14},{12,8},{14,10},{16,20},{18,... | collective-permute-start | bytes 1474568 | tf_op jit(solution)/shard_map/ppermute | solution.py:377
  45.0 28.5 %collective-permute-start.15 = (f32[4,6,40,128]{3,2,1,0:T(8,128)S(1)}, f32[4,6,40,128]{3,2,1,0:T(8,128)S(1)}, u32[]{:S(2)}, u32[]{:S(2)}) collective-permute-start(f32[4,6,40,128]{3,2,1,0:T(8,128)S(1)} %get-tuple-element.160), channel_id=1, source_target_pairs={{0,6},{2,4},{4,2},{6,0},{8,14},{10,12},{12,10},{14,8},{16,22},{18,... | collective-permute-start | bytes 1474568 | tf_op jit(solution)/shard_map/ppermute | solution.py:377
  53.8 39.5 %collective-permute-start.13 = (f32[3,17,32,128]{3,2,1,0:T(8,128)S(1)}, f32[3,17,32,128]{3,2,1,0:T(8,128)S(1)}, u32[]{:S(2)}, u32[]{:S(2)}) collective-permute-start(f32[3,17,32,128]{3,2,1,0:T(8,128)S(1)} %get-tuple-element.157.own_ref.refs_4_), channel_id=1, source_target_pairs={{0,8},{2,10},{4,12},{6,14},{24,16},{26,18},{28,20},{30,22},{1,9},{... | collective-permute-start | bytes 2506760 | tf_op jit(solution)/shard_map/ppermute | solution.py:377
  55.4 23.2 %collective-permute-start.11 = (f32[4,6,16,128]{3,2,1,0:T(8,128)S(1)}, f32[4,6,16,128]{3,2,1,0:T(8,128)S(1)}, u32[]{:S(2)}, u32[]{:S(2)}) collective-permute-start(f32[4,6,16,128]{3,2,1,0:T(8,128)S(1)} %get-tuple-element.155), channel_id=1, source_target_pairs={{0,4},{2,6},{4,0},{6,2},{8,12},{10,14},{12,8},{14,10},{16,20},{18,... | collective-permute-start | bytes 589832 | tf_op jit(solution)/shard_map/ppermute | solution.py:377
  75.2 44.0 %collective-permute-start.19 = (f32[3,17,40,128]{3,2,1,0:T(8,128)S(1)}, f32[3,17,40,128]{3,2,1,0:T(8,128)S(1)}, u32[]{:S(2)}, u32[]{:S(2)}) collective-permute-start(f32[3,17,40,128]{3,2,1,0:T(8,128)S(1)} %get-tuple-element.168.own_ref.refs_5_), channel_id=1, source_target_pairs={{0,8},{2,10},{4,12},{6,14},{24,16},{26,18},{28,20},{30,22},{1,9},{... | collective-permute-start | bytes 3133448 | tf_op jit(solution)/shard_map/ppermute | solution.py:377
  93.2 25.3 %collective-permute-start.9 = (f32[4,6,32,128]{3,2,1,0:T(8,128)S(1)}, f32[4,6,32,128]{3,2,1,0:T(8,128)S(1)}, u32[]{:S(2)}, u32[]{:S(2)}) collective-permute-start(f32[4,6,32,128]{3,2,1,0:T(8,128)S(1)} %get-tuple-element.152), channel_id=1, source_target_pairs={{0,4},{2,6},{4,0},{6,2},{8,12},{10,14},{12,8},{14,10},{16,20},{18,... | collective-permute-start | bytes 1179656 | tf_op jit(solution)/shard_map/ppermute | solution.py:377
  100.7 23.3 %collective-permute-start.16 = (f32[3,17,16,128]{3,2,1,0:T(8,128)S(1)}, f32[3,17,16,128]{3,2,1,0:T(8,128)S(1)}, u32[]{:S(2)}, u32[]{:S(2)}) collective-permute-start(f32[3,17,16,128]{3,2,1,0:T(8,128)S(1)} %get-tuple-element.164.own_ref.refs_2_), channel_id=1, source_target_pairs={{0,8},{2,10},{4,12},{6,14},{24,16},{26,18},{28,20},{30,22},{1,9},{... | collective-permute-start | bytes 1253384 | tf_op jit(solution)/shard_map/ppermute | solution.py:377
  102.2 19.8 %collective-permute-start.7 = (f32[4,6,16,128]{3,2,1,0:T(8,128)S(1)}, f32[4,6,16,128]{3,2,1,0:T(8,128)S(1)}, u32[]{:S(2)}, u32[]{:S(2)}) collective-permute-start(f32[4,6,16,128]{3,2,1,0:T(8,128)S(1)} %get-tuple-element.149), channel_id=1, source_target_pairs={{0,4},{2,6},{4,0},{6,2},{8,12},{10,14},{12,8},{14,10},{16,20},{18,... | collective-permute-start | bytes 589832 | tf_op jit(solution)/shard_map/ppermute | solution.py:377
  109.1 29.9 %collective-permute-start.28 = (f32[11,32,512]{2,1,0:T(8,128)S(1)}, f32[11,32,512]{2,1,0:T(8,128)S(1)}, u32[]{:S(2)}, u32[]{:S(2)}) collective-permute-start(f32[11,32,512]{2,1,0:T(8,128)S(1)} %get-tuple-element.188), channel_id=1, source_target_pairs={{8,0},{10,2},{12,4},{14,6},{16,24},{18,26},{20,28},{22,30},{9,1},{... | collective-permute-start | bytes 2162696 | tf_op jit(solution)/shard_map/ppermute | solution.py:377
  121.9 21.9 %collective-permute-start.26 = (f32[2,17,40,128]{3,2,1,0:T(8,128)S(1)}, f32[2,17,40,128]{3,2,1,0:T(8,128)S(1)}, u32[]{:S(2)}, u32[]{:S(2)}) collective-permute-start(f32[2,17,40,128]{3,2,1,0:T(8,128)S(1)} %get-tuple-element.185), channel_id=1, source_target_pairs={{8,16},{10,18},{12,20},{14,22},{16,8},{18,10},{20,12},{22,14},{9,1... | collective-permute-start | bytes 2088968 | tf_op jit(solution)/shard_map/ppermute | solution.py:377
  124.0 19.8 %collective-permute-start.27 = (f32[2,17,32,128]{3,2,1,0:T(8,128)S(1)}, f32[2,17,32,128]{3,2,1,0:T(8,128)S(1)}, u32[]{:S(2)}, u32[]{:S(2)}) collective-permute-start(f32[2,17,32,128]{3,2,1,0:T(8,128)S(1)} %get-tuple-element.186.own_ref), channel_id=1, source_target_pairs={{0,8},{2,10},{4,12},{6,14},{24,16},{26,18},{28,20},{30,22},{1,9},{... | collective-permute-start | bytes 1671176 | tf_op jit(solution)/shard_map/ppermute | solution.py:377
  132.3 40.2 %collective-permute-start.21 = (f32[2,17,32,128]{3,2,1,0:T(8,128)S(1)}, f32[2,17,32,128]{3,2,1,0:T(8,128)S(1)}, u32[]{:S(2)}, u32[]{:S(2)}) collective-permute-start(f32[2,17,32,128]{3,2,1,0:T(8,128)S(1)} %get-tuple-element.176.own_ref), channel_id=1, source_target_pairs={{0,8},{2,10},{4,12},{6,14},{24,16},{26,18},{28,20},{30,22},{1,9},{... | collective-permute-start | bytes 1671176 | tf_op jit(solution)/shard_map/ppermute | solution.py:377
  149.0 55.3 %collective-permute-start.37 = (f32[17,104,128]{2,1,0:T(8,128)S(1)}, f32[17,104,128]{2,1,0:T(8,128)S(1)}, u32[]{:S(2)}, u32[]{:S(2)}) collective-permute-start(f32[17,104,128]{2,1,0:T(8,128)S(1)} %get-tuple-element.217), channel_id=1, source_target_pairs={{8,0},{10,2},{12,4},{14,6},{16,24},{18,26},{20,28},{22,30},{9,1},{... | collective-permute-start | bytes 2715656 | tf_op jit(solution)/shard_map/ppermute | solution.py:377
  150.3 21.1 %collective-permute-start.38 = (f32[11,32,128]{2,1,0:T(8,128)S(1)}, f32[11,32,128]{2,1,0:T(8,128)S(1)}, u32[]{:S(2)}, u32[]{:S(2)}) collective-permute-start(f32[11,32,128]{2,1,0:T(8,128)S(1)} %get-tuple-element.219), channel_id=1, source_target_pairs={{0,2},{2,0},{4,6},{6,4},{8,10},{10,8},{12,14},{14,12},{16,18},{18,... | collective-permute-start | bytes 540680 | tf_op jit(solution)/shard_map/ppermute | solution.py:377
  153.7 32.3 %collective-permute-start.32 = (f32[2,17,32,128]{3,2,1,0:T(8,128)S(1)}, f32[2,17,32,128]{3,2,1,0:T(8,128)S(1)}, u32[]{:S(2)}, u32[]{:S(2)}) collective-permute-start(f32[2,17,32,128]{3,2,1,0:T(8,128)S(1)} %get-tuple-element.207), channel_id=1, source_target_pairs={{8,16},{10,18},{12,20},{14,22},{16,8},{18,10},{20,12},{22,14},{9,1... | collective-permute-start | bytes 1671176 | tf_op jit(solution)/shard_map/ppermute | solution.py:377
  155.7 25.6 %collective-permute-start.33 = (f32[2,17,24,128]{3,2,1,0:T(8,128)S(1)}, f32[2,17,24,128]{3,2,1,0:T(8,128)S(1)}, u32[]{:S(2)}, u32[]{:S(2)}) collective-permute-start(f32[2,17,24,128]{3,2,1,0:T(8,128)S(1)} %get-tuple-element.208.own_ref), channel_id=1, source_target_pairs={{0,8},{2,10},{4,12},{6,14},{24,16},{26,18},{28,20},{30,22},{1,9},{... | collective-permute-start | bytes 1253384 | tf_op jit(solution)/shard_map/ppermute | solution.py:377
  178.8 40.8 %collective-permute-start.42 = (f32[17,88,128]{2,1,0:T(8,128)S(1)}, f32[17,88,128]{2,1,0:T(8,128)S(1)}, u32[]{:S(2)}, u32[]{:S(2)}) collective-permute-start(f32[17,88,128]{2,1,0:T(8,128)S(1)} %get-tuple-element.230), channel_id=1, source_target_pairs={{0,8},{2,10},{4,12},{6,14},{24,16},{26,18},{28,20},{30,22},{1,9},{... | collective-permute-start | bytes 2297864 | tf_op jit(solution)/shard_map/ppermute | solution.py:377
  180.6 28.8 %collective-permute-start.36 = (f32[2,17,32,128]{3,2,1,0:T(8,128)S(1)}, f32[2,17,32,128]{3,2,1,0:T(8,128)S(1)}, u32[]{:S(2)}, u32[]{:S(2)}) collective-permute-start(f32[2,17,32,128]{3,2,1,0:T(8,128)S(1)} %get-tuple-element.216), channel_id=1, source_target_pairs={{8,16},{10,18},{12,20},{14,22},{16,8},{18,10},{20,12},{22,14},{9,1... | collective-permute-start | bytes 1671176 | tf_op jit(solution)/shard_map/ppermute | solution.py:377
  181.3 21.6 %collective-permute-start.30 = (f32[2,17,16,128]{3,2,1,0:T(8,128)S(1)}, f32[2,17,16,128]{3,2,1,0:T(8,128)S(1)}, u32[]{:S(2)}, u32[]{:S(2)}) collective-permute-start(f32[2,17,16,128]{3,2,1,0:T(8,128)S(1)} %get-tuple-element.203.own_ref), channel_id=1, source_target_pairs={{0,8},{2,10},{4,12},{6,14},{24,16},{26,18},{28,20},{30,22},{1,9},{... | collective-permute-start | bytes 835592 | tf_op jit(solution)/shard_map/ppermute | solution.py:377
  186.0 24.7 %collective-permute-start.35 = (f32[2,17,24,128]{3,2,1,0:T(8,128)S(1)}, f32[2,17,24,128]{3,2,1,0:T(8,128)S(1)}, u32[]{:S(2)}, u32[]{:S(2)}) collective-permute-start(f32[2,17,24,128]{3,2,1,0:T(8,128)S(1)} %get-tuple-element.214), channel_id=1, source_target_pairs={{8,16},{10,18},{12,20},{14,22},{16,8},{18,10},{20,12},{22,14},{9,1... | collective-permute-start | bytes 1253384 | tf_op jit(solution)/shard_map/ppermute | solution.py:377
  (22 other events, 290.6 us)
